TPU v7x, 256 devices: a whole 4x4x8 slice. The times are simulated.
256 devices in a mesh: seq: 16 (over z, core), head: 4 (over x), batch: 4 (over y).
Axes of the slice: x: 4, y: 4, z: 8, core: 2. Of those that a mesh axis runs over, the one named last changes fastest.
Arguments:
- queries: bfloat16 [4, 8192, 8, 8, 128], P('batch', 'seq', 'head'), may hold values from -160 to 160
- key_rows: bfloat16 [4, 8192, 8, 128], P('batch', 'seq'), may hold values from -6 to 6
- value_rows: bfloat16 [4, 8192, 8, 128], P('batch', 'seq'), may hold values from -6 to 6
- compressed: bfloat16 [4, 128, 8, 128], P('batch', 'seq'), may hold values from -6 to 6
- chosen: int32 [4, 128, 8, 16], P('batch', 'seq'), may hold values from 0 to 127, as said below
Outputs:
- block_scores: float32 [4, 128, 8, 128], P('batch', 'seq', 'head')
- attended: bfloat16 [4, 8192, 8, 8, 128], P('batch', 'seq', 'head')
Inputs may be any that keep to these rules, and one draw needn't show every extreme that they name: `chosen`: every entry is at most its own tile number, and entry 0 of every row is the tile's own block. Over the tiles of one device of seq and one group, at most 2 different blocks of any other device are named, and every device after the first names exactly 2 blocks of the first device for each group.
All inputs are finite; a program needn't handle non-finite values.
Results may differ from a plain program's by a relative error of at most 0.008.
Values may be sent and summed in bfloat16 or wider, within the bound.
No kernel may reach another device: no remote copies, remote signals or barrier semaphores. Data moves between devices by JAX's collectives and lax.ppermute only.
A program may use at most 128 MiB of HBM per device.

v0:
```python
import functools
import math

import jax
import jax.numpy as jnp
from jax import lax
from jax.experimental import pallas as pl
from jax.experimental.pallas import tpu as pltpu
from jax.sharding import PartitionSpec as P


HPG = 8
GROUPS = 8
DH = 128
BLOCK = 64
TOPN = 16
NBLK = 128
SHARDS = 16
CHIPS = 8
COLS = 4
TOK = 512
TILES = 8
COMP_PAD = 16
PIECE = 2 * TOK + COMP_PAD
PARTS = 8
CHUNKS = 2
TOK_CHUNK = TOK // CHUNKS
TILES_CHUNK = TILES // CHUNKS
KEYS = TOPN * BLOCK
ROWS = HPG * BLOCK
COMP_ROWS = SHARDS * COMP_PAD
STEPS = 4
STEP_BLOCKS = TOPN // STEPS
STEP_KEYS = KEYS // STEPS
STEP_COMP = NBLK // STEPS
ONES = 16
FAR = -1.0e9
EXP2_SCALE = DH**-0.5 * math.log2(math.e)


def iota(shape, dim):
    return lax.broadcasted_iota(jnp.int32, shape, dim)


def dot(lhs, rhs, dims=(((1,), (0,)), ((), ()))):
    return lax.dot_general(lhs, rhs, dims, preferred_element_type=jnp.float32)


def one_hot(cond):
    return jnp.where(cond, 1.0, 0.0).astype(jnp.bfloat16)


def split_pools(place, keys, values, comp, own, other):
    mine = place[0] * 2 + place[1]
    theirs = place[0] * 2 + 1 - place[1]
    step = 32
    row = iota((2 * step, step * GROUPS), 0)
    col = iota((2 * step, step * GROUPS), 1)
    group = jnp.where(row < step, mine, theirs)
    pick = one_hot(col == (row % step) * GROUPS + group)
    for i in range(TOK // step):
        rows = pl.ds(i * step * GROUPS, step * GROUPS)
        both = jnp.concatenate([keys[rows, :], values[rows, :]], axis=1)
        got = dot(pick, both).astype(jnp.bfloat16)
        own[pl.ds(i * step, step), :] = got[:step, :DH]
        own[pl.ds(TOK + i * step, step), :] = got[:step, DH:]
        other[pl.ds(i * step, step), :] = got[step:, :DH]
        other[pl.ds(TOK + i * step, step), :] = got[step:, DH:]
    row = iota((2 * COMP_PAD, TILES * GROUPS), 0)
    col = iota((2 * COMP_PAD, TILES * GROUPS), 1)
    group = jnp.where(row < COMP_PAD, mine, theirs)
    block = row % COMP_PAD
    got = dot(one_hot((col == block * GROUPS + group) & (block < TILES)), comp[...]).astype(jnp.bfloat16)
    own[pl.ds(2 * TOK, COMP_PAD), :] = got[:COMP_PAD]
    other[pl.ds(2 * TOK, COMP_PAD), :] = got[COMP_PAD:]


def row_of(r, place):
    part = r // 32
    head = (r // 16) % 2
    token = r % 16
    group = 2 * ((place[0] + part // 2) % COLS) + (place[1] + part % 2) % 2
    return token * 16 + head * GROUPS + group


def split_queries(tokens, place, queries, *parts):
    shape = (256, 256)
    pick = one_hot(iota(shape, 1) == row_of(iota(shape, 0), place))
    for i in range(tokens // 32):
        pair = jnp.concatenate([queries[pl.ds(i * 512, 256), :], queries[pl.ds(i * 512 + 256, 256), :]], axis=1)
        got = dot(pick, pair).astype(jnp.bfloat16)
        for k in range(PARTS):
            for j in range(2):
                rows = got[k * 32 + j * 16 : k * 32 + j * 16 + 16]
                parts[k][j, pl.ds(i * 32, 16), :] = rows[:, :DH]
                parts[k][j, pl.ds(i * 32 + 16, 16), :] = rows[:, DH:]


def join_outputs(tokens, place, *refs):
    parts, out = refs[:PARTS], refs[-1]
    shape = (256, 256)
    pick = one_hot(iota(shape, 0) == row_of(iota(shape, 1), place))
    for i in range(tokens // 32):
        halves = []
        for h in range(2):
            at = pl.ds(i * 32 + h * 16, 16)
            halves.append(jnp.concatenate([parts[k][j, at, :] for k in range(PARTS) for j in range(2)], axis=0))
        got = dot(pick, jnp.concatenate(halves, axis=1)).astype(jnp.bfloat16)
        out[pl.ds(i * 512, 256), :] = got[:, :DH]
        out[pl.ds(i * 512 + 256, 256), :] = got[:, DH:]


def attend(chunk, place, picks, *refs):
    pieces = refs[: 2 * CHIPS]
    queries = refs[2 * CHIPS : 2 * CHIPS + PARTS]
    outs = refs[2 * CHIPS + PARTS : 2 * CHIPS + 2 * PARTS]
    pooled = refs[2 * CHIPS + 2 * PARTS : 2 * CHIPS + 2 * PARTS + 2]
    pool, comp, mask, *rest, sems = refs[2 * CHIPS + 2 * PARTS + 2 :]
    turned, scores, logits, tops = rest[0:2], rest[2:4], rest[4:6], rest[6:8]
    core, chip = place[1], place[2]
    copies = []
    for k in range(CHIPS):
        for h in range(2):
            slot = 2 * ((chip + k) % CHIPS) + (core + h) % 2
            copies.append(pltpu.make_async_copy(pieces[2 * k + h], pool.at[slot], sems.at[2 * k + h]))
    for copy in copies:
        copy.start()
    shape = (2 * BLOCK, DH)
    row = iota(shape, 0)
    hidden = (row >= BLOCK) & (row - BLOCK > iota(shape, 1))
    mask[...] = jnp.where(hidden, FAR, 0.0).astype(jnp.bfloat16)
    shape = (DH, ROWS)
    for half in range(2):
        turned[half][pl.ds(DH, DH), :] = one_hot(iota(shape, 0) == iota(shape, 1) % BLOCK)
    shape = (NBLK, COMP_ROWS)
    take = one_hot(iota(shape, 1) == iota(shape, 0) // TILES * COMP_PAD + iota(shape, 0) % TILES)
    for copy in copies:
        copy.wait()
    padded = jnp.concatenate([pool[s, pl.ds(2 * TOK, COMP_PAD), :] for s in range(SHARDS)], axis=0)
    comp[...] = dot(take, padded).astype(jnp.bfloat16)
    block_row = iota((NBLK, ROWS), 0)
    ones = jnp.full((ONES, STEP_KEYS), 1.0, jnp.bfloat16)

    def spot(local):
        return pl.ds(pl.multiple_of(local * BLOCK, BLOCK), BLOCK)

    def number_of(local, half):
        return (2 * chip + (core + half) % 2) * TILES + chunk * TILES_CHUNK + local

    def pick_of(local, half, b):
        return picks[(half * TILES + chunk * TILES_CHUNK + local) * TOPN + b]

    def block_of(n, offset):
        return pool[n // TILES, pl.ds(pl.multiple_of(offset + n % TILES * BLOCK, BLOCK), BLOCK), :]

    def turn(local, half):
        at = spot(local)
        query = jnp.concatenate([queries[2 * dx + half][j, at, :] for dx in range(COLS) for j in range(2)], axis=0)
        turned[half][pl.ds(0, DH), :] = query.T

    def score(local, half, i):
        number = number_of(local, half)
        keys = []
        for b in range(STEP_BLOCKS):
            n = pick_of(local, half, i * STEP_BLOCKS + b)
            own = jnp.where(n == number, BLOCK, 0)
            keys.append(jnp.concatenate([block_of(n, 0), mask[pl.ds(pl.multiple_of(own, BLOCK), BLOCK), :]], axis=1))
        some = comp[pl.ds(i * STEP_COMP, STEP_COMP), :]
        keys.append(jnp.concatenate([some, jnp.zeros_like(some)], axis=1))
        got = dot(jnp.concatenate(keys, axis=0), turned[half][...])
        near = got[:STEP_KEYS]
        scores[half][pl.ds(i * STEP_KEYS, STEP_KEYS), :] = near
        logits[half][pl.ds(i * STEP_COMP, STEP_COMP), :] = got[STEP_KEYS:]
        top = jnp.max(near.reshape(STEP_KEYS // 8, 8, ROWS), axis=0)
        tops[half][...] = top if i == 0 else jnp.maximum(tops[half][...], top)

    def weigh(local, half, i, top):
        weight = jnp.exp2((scores[half][pl.ds(i * STEP_KEYS, STEP_KEYS), :] - top) * EXP2_SCALE).astype(jnp.bfloat16)
        blocks = [block_of(pick_of(local, half, i * STEP_BLOCKS + b), TOK) for b in range(STEP_BLOCKS)]
        values = jnp.concatenate([jnp.concatenate(blocks, axis=0).T, ones], axis=0)
        return dot(values, weight)

    def finish(local, half, mixed):
        result = (mixed[:DH] * (1.0 / mixed[DH : DH + 1])).astype(jnp.bfloat16).T
        at = spot(local)
        for dx in range(COLS):
            for j in range(2):
                r = (dx * 2 + j) * BLOCK
                outs[2 * dx + half][j, at, :] = result[r : r + BLOCK]
        number = number_of(local, half)
        known = jnp.where(block_row <= number, logits[half][...], -jnp.inf)
        raised = jnp.exp2((known - jnp.max(known, axis=0, keepdims=True)) * EXP2_SCALE)
        prob = raised * (1.0 / jnp.sum(raised, axis=0, keepdims=True))
        folded = prob[:, :128] + prob[:, 128:256] + prob[:, 256:384] + prob[:, 384:]
        factor = (number + 1).astype(jnp.float32) * (1.0 / (BLOCK * HPG))
        pooled[half][pl.ds(local, 1), :] = jnp.sum(folded.T, axis=0, keepdims=True) * factor

    def pair(this, half, that, other):
        top = jnp.max(tops[half][...], axis=0, keepdims=True)
        mixed = None
        for i in range(STEPS):
            score(that, other, i)
            got = weigh(this, half, i, top)
            mixed = got if mixed is None else mixed + got
        finish(this, half, mixed)

    def step(local, carry):
        following = jnp.minimum(local + 1, TILES_CHUNK - 1)
        pair(local, 0, local, 1)
        turn(following, 0)
        pair(local, 1, following, 0)
        turn(following, 1)
        return carry

    turn(0, 0)
    turn(0, 1)
    for i in range(STEPS):
        score(0, 0, i)
    lax.fori_loop(0, TILES_CHUNK, step, 0)


SMEM = pl.BlockSpec(memory_space=pltpu.SMEM)
VMEM = pl.BlockSpec(memory_space=pltpu.VMEM)
ANY = pl.BlockSpec(memory_space=pl.ANY)


def bf16(*shape):
    return jax.ShapeDtypeStruct(shape, jnp.bfloat16)


def call_split_pools(place, keys, values, comp):
    return pl.pallas_call(
        split_pools,
        in_specs=[SMEM, VMEM, VMEM, VMEM],
        out_specs=[VMEM, VMEM],
        out_shape=[bf16(PIECE, DH)] * 2,
        name="split_pools",
    )(place, keys, values, comp)


def call_split_queries(place, queries):
    steps = 4
    tokens = TOK // steps
    return pl.pallas_call(
        functools.partial(split_queries, tokens),
        grid=(steps,),
        in_specs=[SMEM, pl.BlockSpec((tokens * 16, DH), lambda i: (i, 0))],
        out_specs=[pl.BlockSpec((2, tokens, DH), lambda i: (0, i, 0))] * PARTS,
        out_shape=[bf16(2, TOK, DH)] * PARTS,
        name="split_queries",
    )(place, queries)


def call_attend(chunk, place, picks, pieces, queries):
    return pl.pallas_call(
        functools.partial(attend, chunk),
        grid=(1,),
        in_specs=[SMEM, SMEM]
        + [ANY] * (2 * CHIPS)
        + [pl.BlockSpec((2, TOK_CHUNK, DH), lambda i: (0, chunk, 0))] * PARTS,
        out_specs=[pl.BlockSpec((2, TOK_CHUNK, DH), lambda i: (0, 0, 0))] * PARTS
        + [pl.BlockSpec((TILES_CHUNK, NBLK), lambda i: (0, 0))] * 2,
        out_shape=[bf16(2, TOK_CHUNK, DH)] * PARTS + [jax.ShapeDtypeStruct((TILES_CHUNK, NBLK), jnp.float32)] * 2,
        scratch_shapes=[
            pltpu.VMEM((SHARDS, PIECE, DH), jnp.bfloat16),
            pltpu.VMEM((NBLK, DH), jnp.bfloat16),
            pltpu.VMEM((2 * BLOCK, DH), jnp.bfloat16),
        ]
        + [pltpu.VMEM((2 * DH, ROWS), jnp.bfloat16)] * 2
        + [pltpu.VMEM((KEYS, ROWS), jnp.float32)] * 2
        + [pltpu.VMEM((NBLK, ROWS), jnp.float32)] * 2
        + [pltpu.VMEM((8, ROWS), jnp.float32)] * 2
        + [pltpu.SemaphoreType.DMA((2 * CHIPS,))],
        name="attend",
    )(place, picks, *pieces, *queries)


def call_join_outputs(chunk, place, parts, before):
    extra = [] if before is None else [before]
    return pl.pallas_call(
        functools.partial(join_outputs, TOK_CHUNK),
        grid=(1,),
        in_specs=[SMEM] + [pl.BlockSpec((2, TOK_CHUNK, DH), lambda i: (0, 0, 0))] * PARTS + [ANY] * len(extra),
        out_specs=pl.BlockSpec((TOK_CHUNK * 16, DH), lambda i: (chunk, 0)),
        out_shape=bf16(TOK * 16, DH),
        input_output_aliases={PARTS + 1: 0} if extra else {},
        name="join_outputs",
    )(place, *parts, *extra)


def by_seq(value, move):
    return lax.ppermute(value, "seq", [(s, move(s // 2, s % 2)) for s in range(SHARDS)])


def to_seq(chip, core):
    return chip % CHIPS * 2 + core % 2


def by_part(value, dx, dc, back):
    if dx == 0 and dc == 0:
        return value
    pairs = []
    for s in range(SHARDS):
        for x in range(COLS):
            there = (s ^ dc) * COLS + (x + dx) % COLS
            here = s * COLS + x
            pairs.append((there, here) if back else (here, there))
    return lax.ppermute(value, ("seq", "head"), pairs)


def whole(queries, key_rows, value_rows, compressed, chosen):
    seq = lax.axis_index("seq")
    col = lax.axis_index("head")
    chip, core = seq // 2, seq % 2
    place = jnp.stack([col, core, chip]).astype(jnp.int32)
    own, other = call_split_pools(
        place, key_rows.reshape(TOK * GROUPS, DH), value_rows.reshape(TOK * GROUPS, DH), compressed.reshape(TILES * GROUPS, DH)
    )
    pieces = [None] * (2 * CHIPS)
    pieces[0] = own
    pieces[1] = by_seq(other, lambda z, c: to_seq(z, c + 1))
    up, down = [own, other], [own, other]
    for k in range(1, 4):
        for h in range(2):
            turn = h if k == 1 else 0
            up[h] = by_seq(up[h], lambda z, c: to_seq(z + 1, c + turn))
            down[h] = by_seq(down[h], lambda z, c: to_seq(z - 1, c + turn))
            pieces[2 * (CHIPS - k) + h] = up[h]
            pieces[2 * k + h] = down[h]
    for h in range(2):
        onward = jnp.where(core == 0, up[h], down[h])
        pieces[2 * 4 + h] = by_seq(onward, lambda z, c: to_seq(z + (1 if c == 0 else -1), c))
    parts = call_split_queries(place, queries.reshape(TOK * 16, DH))
    moved = []
    for k in range(PARTS):
        moved.append(by_part(parts[k], k // 2, k % 2, False))
    groups = chosen[0].transpose(1, 0, 2)
    mine = lax.dynamic_index_in_dim(groups, 2 * col + core, 0, False)
    theirs = lax.dynamic_index_in_dim(groups, 2 * col + 1 - core, 0, False)
    theirs = by_seq(theirs, lambda z, c: to_seq(z, c + 1))
    picks = jnp.concatenate([mine, theirs]).reshape(-1)
    attended, kept, came, joined = None, [], [], []
    for chunk in range(CHUNKS):
        *outs, keep, send = call_attend(chunk, place, picks, pieces, moved)
        back = []
        for k in range(PARTS):
            back.append(by_part(outs[k], k // 2, k % 2, True))
        came.append(by_seq(send, lambda z, c: to_seq(z, c + 1)))
        kept.append(keep)
        joined.append(back)
    for chunk in range(CHUNKS):
        attended = call_join_outputs(chunk, place, joined[chunk], attended)
    kept, came = jnp.concatenate(kept), jnp.concatenate(came)
    both = jnp.where(core == 0, jnp.stack([kept, came], axis=1), jnp.stack([came, kept], axis=1))
    return both[None], attended.reshape(1, TOK, 2, GROUPS, DH)


def solution(mesh):
    placed = (
        P("batch", "seq", "head", None, None),
        P("batch", "seq", None, None),
        P("batch", "seq", None, None),
        P("batch", "seq", None, None),
        P("batch", "seq", None, None),
    )
    return jax.shard_map(
        whole,
        mesh=mesh,
        in_specs=placed,
        out_specs=(P("batch", "seq", "head", None), P("batch", "seq", "head", None, None)),
        check_vma=False,
    )
```

profile of v0, /device:TPU:1, one launch (start us, length us, event | category | flops | bytes accessed | tf_op | source)
XLA Modules:
  0.0 138.0 jit_solution(18038408175370839107)
XLA Ops:
  0.6 0.6 pad_add_fusion.1.place
  1.3 2.8 %split_pools.1 = (bf16[1040,128]{1,0:T(8,128)(2,1)}, bf16[1040,128]{1,0:T(8,128)(2,1)}) custom-call(s32[3]{0:T(128)} %pad_add_fusion.1.place, bf16[4096,128]{1,0:T(8,128)(2,1)} %bitcast.20, bf16[4096,128]{1,0:T(8,128)(2,1)} %bitcast.21, bf16[64,128]{1,0:T(8,128)(2,1)} %bitcast.22), custom_call_target="tpu_custom_call" | custom-call | tf_op jit(solution)/shard_map/split_pools/pallas_call | solution.py:232
  4.1 3.0 %collective-permute-start.12 = (bf16[1040,128]{1,0:T(8,128)(2,1)}, bf16[1040,128]{1,0:T(8,128)(2,1)S(1)}, u32[]{:S(2)}, u32[]{:S(2)}) collective-permute-start(bf16[1040,128]{1,0:T(8,128)(2,1)} %get-tuple-element.33), channel_id=1, source_target_pairs={{0,48},{16,32},{32,80},{48,64},{64,112},{80,96},{96,144},{112,128}... | collective-permute-start | bytes 798728 | tf_op jit(solution)/shard_map/ppermute | solution.py:292
  7.1 3.9 %collective-permute-start.3 = (bf16[1040,128]{1,0:T(8,128)(2,1)}, bf16[1040,128]{1,0:T(8,128)(2,1)S(1)}, u32[]{:S(2)}, u32[]{:S(2)}) collective-permute-start(bf16[1040,128]{1,0:T(8,128)(2,1)} %get-tuple-element.33), channel_id=1, source_target_pairs={{0,240},{16,224},{32,16},{48,0},{64,48},{80,32},{96,80},{112,64},{... | collective-permute-start | bytes 798728 | tf_op jit(solution)/shard_map/ppermute | solution.py:292
  11.1 0.0 collective-permute-start.8
  11.1 2.7 %collective-permute-start.2 = (bf16[1040,128]{1,0:T(8,128)(2,1)}, bf16[1040,128]{1,0:T(8,128)(2,1)S(1)}, u32[]{:S(2)}, u32[]{:S(2)}) collective-permute-start(bf16[1040,128]{1,0:T(8,128)(2,1)} %get-tuple-element.32.refs_0_), channel_id=1, source_target_pairs={{0,224},{16,240},{32,0},{48,16},{64,32},{80,48},{96,64},{112,80},{... | collective-permute-start | bytes 798728 | tf_op jit(solution)/shard_map/ppermute | solution.py:292
  13.8 4.5 %collective-permute-done.12.refs_15_ = bf16[1040,128]{1,0:T(8,128)(2,1)S(1)} collective-permute-done((bf16[1040,128]{1,0:T(8,128)(2,1)}, bf16[1040,128]{1,0:T(8,128)(2,1)S(1)}, u32[]{:S(2)}, u32[]{:S(2)}) %collective-permute-start.12) | collective-permute-done | bytes 266272 | tf_op jit(solution)/shard_map/ppermute | solution.py:292
  18.3 2.7 %collective-permute-start.5 = (bf16[1040,128]{1,0:T(8,128)(2,1)S(1)}, bf16[1040,128]{1,0:T(8,128)(2,1)S(1)}, u32[]{:S(2)}, u32[]{:S(2)}) collective-permute-start(bf16[1040,128]{1,0:T(8,128)(2,1)S(1)} %collective-permute-done.3.refs_3_), channel_id=1, source_target_pairs={{0,224},{16,240},{32,0},{48,16},{64,32},{80,48},{96,64},{112,80},{... | collective-permute-start | bytes 798728 | tf_op jit(solution)/shard_map/ppermute | solution.py:292
  20.9 1.6 %collective-permute-done.8.refs_14_ = bf16[1040,128]{1,0:T(8,128)(2,1)S(1)} collective-permute-done((bf16[1040,128]{1,0:T(8,128)(2,1)}, bf16[1040,128]{1,0:T(8,128)(2,1)S(1)}, u32[]{:S(2)}, u32[]{:S(2)}) %collective-permute-start.8) | collective-permute-done | bytes 266272 | tf_op jit(solution)/shard_map/ppermute | solution.py:292
  22.5 0.8 collective-permute-done.2.refs_2_
  23.3 3.3 %collective-permute-start.4 = (bf16[1040,128]{1,0:T(8,128)(2,1)S(1)}, bf16[1040,128]{1,0:T(8,128)(2,1)S(1)}, u32[]{:S(2)}, u32[]{:S(2)}) collective-permute-start(bf16[1040,128]{1,0:T(8,128)(2,1)S(1)} %collective-permute-done.2.refs_2_), channel_id=1, source_target_pairs={{0,224},{16,240},{32,0},{48,16},{64,32},{80,48},{96,64},{112,80},{... | collective-permute-start | bytes 798728 | tf_op jit(solution)/shard_map/ppermute | solution.py:292
  26.6 1.6 %collective-permute-done.13.refs_13_ = bf16[1040,128]{1,0:T(8,128)(2,1)S(1)} collective-permute-done((bf16[1040,128]{1,0:T(8,128)(2,1)S(1)}, bf16[1040,128]{1,0:T(8,128)(2,1)S(1)}, u32[]{:S(2)}, u32[]{:S(2)}) %collective-permute-start.13) | collective-permute-done | bytes 266272 | tf_op jit(solution)/shard_map/ppermute | solution.py:292
  28.2 0.7 collective-permute-done.5.refs_5_
  28.9 3.4 %collective-permute-start.7 = (bf16[1040,128]{1,0:T(8,128)(2,1)S(1)}, bf16[1040,128]{1,0:T(8,128)(2,1)S(1)}, u32[]{:S(2)}, u32[]{:S(2)}) collective-permute-start(bf16[1040,128]{1,0:T(8,128)(2,1)S(1)} %collective-permute-done.5.refs_5_), channel_id=1, source_target_pairs={{0,224},{16,240},{32,0},{48,16},{64,32},{80,48},{96,64},{112,80},{... | collective-permute-start | bytes 798728 | tf_op jit(solution)/shard_map/ppermute | solution.py:292
  32.3 0.8 constant_dynamic-slice_fusion.1
  33.2 1.4 collective-permute-start
  34.5 4.6 %split_queries.1 = (bf16[2,512,128]{2,1,0:T(8,128)(2,1)}, bf16[2,512,128]{2,1,0:T(8,128)(2,1)}, bf16[2,512,128]{2,1,0:T(8,128)(2,1)}, bf16[2,512,128]{2,1,0:T(8,...) custom-call(s32[3]{0:T(128)} %pad_add_fusion.1.place, ...), custom_call_target="tpu_custom_call" | custom-call | tf_op jit(solution)/shard_map/split_queries/pallas_call | solution.py:244
  39.1 0.0 collective-permute-done.9.refs_12_
  39.2 0.1 collective-permute-start.16
  39.3 1.3 collective-permute-start.17
  40.6 3.1 %collective-permute-start.6 = (bf16[1040,128]{1,0:T(8,128)(2,1)S(1)}, bf16[1040,128]{1,0:T(8,128)(2,1)S(1)}, u32[]{:S(2)}, u32[]{:S(2)}) collective-permute-start(bf16[1040,128]{1,0:T(8,128)(2,1)S(1)} %collective-permute-done.4.refs_4_), channel_id=1, source_target_pairs={{0,224},{16,240},{32,0},{48,16},{64,32},{80,48},{96,64},{112,80},{... | collective-permute-start | bytes 798728 | tf_op jit(solution)/shard_map/ppermute | solution.py:292
  43.7 0.8 broadcast_select_fusion
  44.5 1.9 %collective-permute-start.18 = (bf16[2,512,128]{2,1,0:T(8,128)(2,1)}, bf16[2,512,128]{2,1,0:T(8,128)(2,1)}, u32[]{:S(2)}, u32[]{:S(2)}) collective-permute-start(bf16[2,512,128]{2,1,0:T(8,128)(2,1)} %get-tuple-element.37), channel_id=1, source_target_pairs={{0,20},{4,24},{8,28},{12,16},{16,4},{20,8},{24,12},{28,0},{32,52},... | collective-permute-start | bytes 786440 | tf_op jit(solution)/shard_map/ppermute | solution.py:308
  46.3 2.8 %collective-permute-done.10.refs_10_ = bf16[1040,128]{1,0:T(8,128)(2,1)S(1)} collective-permute-done((bf16[1040,128]{1,0:T(8,128)(2,1)S(1)}, bf16[1040,128]{1,0:T(8,128)(2,1)S(1)}, u32[]{:S(2)}, u32[]{:S(2)}) %collective-permute-start.10) | collective-permute-done | bytes 266272 | tf_op jit(solution)/shard_map/ppermute | solution.py:292
  49.1 2.3 %collective-permute-start.19 = (bf16[2,512,128]{2,1,0:T(8,128)(2,1)}, bf16[2,512,128]{2,1,0:T(8,128)(2,1)}, u32[]{:S(2)}, u32[]{:S(2)}) collective-permute-start(bf16[2,512,128]{2,1,0:T(8,128)(2,1)} %get-tuple-element.38), channel_id=1, source_target_pairs={{0,8},{4,12},{8,0},{12,4},{16,24},{20,28},{24,16},{28,20},{32,40},... | collective-permute-start | bytes 786440 | tf_op jit(solution)/shard_map/ppermute | solution.py:308
  51.5 2.2 %collective-permute-start.20 = (bf16[2,512,128]{2,1,0:T(8,128)(2,1)}, bf16[2,512,128]{2,1,0:T(8,128)(2,1)}, u32[]{:S(2)}, u32[]{:S(2)}) collective-permute-start(bf16[2,512,128]{2,1,0:T(8,128)(2,1)} %get-tuple-element.39), channel_id=1, source_target_pairs={{0,24},{4,28},{8,16},{12,20},{16,8},{20,12},{24,0},{28,4},{32,56},... | collective-permute-start | bytes 786440 | tf_op jit(solution)/shard_map/ppermute | solution.py:308
  53.7 0.8 broadcast_select_fusion.1
  54.5 2.7 %collective-permute-start.15 = (bf16[1040,128]{1,0:T(8,128)(2,1)}, bf16[1040,128]{1,0:T(8,128)(2,1)}, u32[]{:S(2)}, u32[]{:S(2)}) collective-permute-start(bf16[1040,128]{1,0:T(8,128)(2,1)} %broadcast_select_fusion), channel_id=1, source_target_pairs={{0,32},{16,240},{32,64},{48,16},{64,96},{80,48},{96,128},{112,80},... | collective-permute-start | bytes 798728 | tf_op jit(solution)/shard_map/ppermute | solution.py:292
  57.2 0.1 collective-permute-start.11
  57.3 4.2 %collective-permute-done.19.refs_20_ = bf16[2,512,128]{2,1,0:T(8,128)(2,1)} collective-permute-done((bf16[2,512,128]{2,1,0:T(8,128)(2,1)}, bf16[2,512,128]{2,1,0:T(8,128)(2,1)}, u32[]{:S(2)}, u32[]{:S(2)}) %collective-permute-start.19) | collective-permute-done | bytes 262176 | tf_op jit(solution)/shard_map/ppermute | solution.py:308
  61.5 5.6 %collective-permute-done.20.refs_21_ = bf16[2,512,128]{2,1,0:T(8,128)(2,1)} collective-permute-done((bf16[2,512,128]{2,1,0:T(8,128)(2,1)}, bf16[2,512,128]{2,1,0:T(8,128)(2,1)}, u32[]{:S(2)}, u32[]{:S(2)}) %collective-permute-start.20) | collective-permute-done | bytes 262176 | tf_op jit(solution)/shard_map/ppermute | solution.py:308
  67.1 0.7 reshape.89.picks
  67.8 1.5 %collective-permute-done.21.refs_22_ = bf16[2,512,128]{2,1,0:T(8,128)(2,1)} collective-permute-done((bf16[2,512,128]{2,1,0:T(8,128)(2,1)}, bf16[2,512,128]{2,1,0:T(8,128)(2,1)}, u32[]{:S(2)}, u32[]{:S(2)}) %collective-permute-start.21) | collective-permute-done | bytes 262176 | tf_op jit(solution)/shard_map/ppermute | solution.py:308
  69.3 6.5 %collective-permute-done.22.refs_23_ = bf16[2,512,128]{2,1,0:T(8,128)(2,1)} collective-permute-done((bf16[2,512,128]{2,1,0:T(8,128)(2,1)}, bf16[2,512,128]{2,1,0:T(8,128)(2,1)}, u32[]{:S(2)}, u32[]{:S(2)}) %collective-permute-start.22) | collective-permute-done | bytes 262176 | tf_op jit(solution)/shard_map/ppermute | solution.py:308
  75.9 0.6 copy-done.12
  76.5 12.0 %attend.3 = (bf16[2,256,128]{2,1,0:T(8,128)(2,1)}, bf16[2,256,128]{2,1,0:T(8,128)(2,1)}, bf16[2,256,128]{2,1,0:T(8,128)(2,1)}, bf16[2,256,128]{2,1,0:T(8,128)(2,...) custom-call(s32[3]{0:T(128)} %pad_add_fusion.1.place, ...), custom_call_target="tpu_custom_call" | custom-call | tf_op jit(solution)/shard_map/attend/pallas_call | solution.py:255
  88.5 0.5 collective-permute-start.25
  89.0 1.3 collective-permute-start.26
  90.2 11.9 %attend.2 = (bf16[2,256,128]{2,1,0:T(8,128)(2,1)}, bf16[2,256,128]{2,1,0:T(8,128)(2,1)}, bf16[2,256,128]{2,1,0:T(8,128)(2,1)}, bf16[2,256,128]{2,1,0:T(8,128)(2,...) custom-call(s32[3]{0:T(128)} %pad_add_fusion.1.place, ...), custom_call_target="tpu_custom_call" | custom-call | tf_op jit(solution)/shard_map/attend/pallas_call | solution.py:255
  102.2 0.6 collective-permute-start.32
  102.8 0.7 collective-permute-start.33
  103.6 0.6 collective-permute-start.24
  104.2 0.8 collective-permute-done.24
  105.0 0.3 collective-permute-start.23
  105.3 1.0 collective-permute-done.23
  106.4 1.4 %collective-permute-start.34 = (bf16[2,256,128]{2,1,0:T(8,128)(2,1)}, bf16[2,256,128]{2,1,0:T(8,128)(2,1)S(1)}, u32[]{:S(2)}, u32[]{:S(2)}) collective-permute-start(bf16[2,256,128]{2,1,0:T(8,128)(2,1)} %get-tuple-element.57), channel_id=1, source_target_pairs={{20,0},{24,4},{28,8},{16,12},{4,16},{8,20},{12,24},{0,28},{52,32},... | collective-permute-start | bytes 393224 | tf_op jit(solution)/shard_map/ppermute | solution.py:308
  107.8 1.3 collective-permute-start.35
  109.1 2.0 %collective-permute-start.36 = (bf16[2,256,128]{2,1,0:T(8,128)(2,1)}, bf16[2,256,128]{2,1,0:T(8,128)(2,1)S(1)}, u32[]{:S(2)}, u32[]{:S(2)}) collective-permute-start(bf16[2,256,128]{2,1,0:T(8,128)(2,1)} %get-tuple-element.59), channel_id=1, source_target_pairs={{24,0},{28,4},{16,8},{20,12},{8,16},{12,20},{0,24},{4,28},{56,32},... | collective-permute-start | bytes 393224 | tf_op jit(solution)/shard_map/ppermute | solution.py:308
  111.1 0.3 collective-permute-start.37
  111.4 1.0 collective-permute-start.38
  112.3 0.6 maximum_bitcast_fusion
  113.0 2.1 %collective-permute-start.27 = (bf16[2,256,128]{2,1,0:T(8,128)(2,1)S(1)}, bf16[2,256,128]{2,1,0:T(8,128)(2,1)S(1)}, u32[]{:S(2)}, u32[]{:S(2)}) collective-permute-start(bf16[2,256,128]{2,1,0:T(8,128)(2,1)S(1)} %copy-done.32), channel_id=1, source_target_pairs={{20,0},{24,4},{28,8},{16,12},{4,16},{8,20},{12,24},{0,28},{52,32},... | collective-permute-start | bytes 393224 | tf_op jit(solution)/shard_map/ppermute | solution.py:308
  115.1 1.0 collective-permute-start.28
  116.1 2.1 %collective-permute-done.36.refs_5_ = bf16[2,256,128]{2,1,0:T(8,128)(2,1)S(1)} collective-permute-done((bf16[2,256,128]{2,1,0:T(8,128)(2,1)}, bf16[2,256,128]{2,1,0:T(8,128)(2,1)S(1)}, u32[]{:S(2)}, u32[]{:S(2)}) %collective-permute-start.36) | collective-permute-done | bytes 131104 | tf_op jit(solution)/shard_map/ppermute | solution.py:308
  118.2 2.6 %collective-permute-start.29 = (bf16[2,256,128]{2,1,0:T(8,128)(2,1)S(1)}, bf16[2,256,128]{2,1,0:T(8,128)(2,1)S(1)}, u32[]{:S(2)}, u32[]{:S(2)}) collective-permute-start(bf16[2,256,128]{2,1,0:T(8,128)(2,1)S(1)} %copy-done.30), channel_id=1, source_target_pairs={{24,0},{28,4},{16,8},{20,12},{8,16},{12,20},{0,24},{4,28},{56,32},... | collective-permute-start | bytes 393224 | tf_op jit(solution)/shard_map/ppermute | solution.py:308
  120.9 0.2 collective-permute-start.30
  121.0 2.9 %collective-permute-done.38.refs_7_ = bf16[2,256,128]{2,1,0:T(8,128)(2,1)S(1)} collective-permute-done((bf16[2,256,128]{2,1,0:T(8,128)(2,1)}, bf16[2,256,128]{2,1,0:T(8,128)(2,1)S(1)}, u32[]{:S(2)}, u32[]{:S(2)}) %collective-permute-start.38) | collective-permute-done | bytes 131104 | tf_op jit(solution)/shard_map/ppermute | solution.py:308
  124.0 0.6 copy.10
  124.6 2.7 %join_outputs.2.refs_8_ = bf16[8192,128]{1,0:T(8,128)(2,1)} custom-call(s32[3]{0:T(128)} %pad_add_fusion.1.place, bf16[2,256,128]{2,1,0:T(8,128)(2,1)} %get-tuple-element.54.refs_0_, bf16[2,256,128]{2,1,0:T(8,128)(2,1)} %copy-done.20, bf16[2,256,128]{2,1,0:T(8,128)(2,1)} %copy-done.21, bf16[2,256,128]{2,1,0:T(8,128)(2,1)} %copy-done.22, ...), custom_call_target="tpu_custom_call" | custom-call | tf_op jit(solution)/shard_map/join_outputs/pallas_call | solution.py:280
  127.4 2.1 %collective-permute-done.29.refs_5_ = bf16[2,256,128]{2,1,0:T(8,128)(2,1)S(1)} collective-permute-done((bf16[2,256,128]{2,1,0:T(8,128)(2,1)S(1)}, bf16[2,256,128]{2,1,0:T(8,128)(2,1)S(1)}, u32[]{:S(2)}, u32[]{:S(2)}) %collective-permute-start.29) | collective-permute-done | bytes 131104 | tf_op jit(solution)/shard_map/ppermute | solution.py:308
  129.5 2.3 %collective-permute-done.30.refs_6_ = bf16[2,256,128]{2,1,0:T(8,128)(2,1)S(1)} collective-permute-done((bf16[2,256,128]{2,1,0:T(8,128)(2,1)S(1)}, bf16[2,256,128]{2,1,0:T(8,128)(2,1)S(1)}, u32[]{:S(2)}, u32[]{:S(2)}) %collective-permute-start.30) | collective-permute-done | bytes 131104 | tf_op jit(solution)/shard_map/ppermute | solution.py:308
  131.8 2.8 %collective-permute-done.31.refs_7_ = bf16[2,256,128]{2,1,0:T(8,128)(2,1)S(1)} collective-permute-done((bf16[2,256,128]{2,1,0:T(8,128)(2,1)S(1)}, bf16[2,256,128]{2,1,0:T(8,128)(2,1)S(1)}, u32[]{:S(2)}, u32[]{:S(2)}) %collective-permute-start.31) | collective-permute-done | bytes 131104 | tf_op jit(solution)/shard_map/ppermute | solution.py:308
  134.7 0.6 copy-done.19
  135.3 2.7 %join_outputs.3 = bf16[8192,128]{1,0:T(8,128)(2,1)} custom-call(s32[3]{0:T(128)} %pad_add_fusion.1.place, bf16[2,256,128]{2,1,0:T(8,128)(2,1)} %get-tuple-element.46.refs_0_, bf16[2,256,128]{2,1,0:T(8,128)(2,1)} %copy-done.13, bf16[2,256,128]{2,1,0:T(8,128)(2,1)} %copy-done.14, bf16[2,256,128]{2,1,0:T(8,128)(2,1)} %copy-done.15, ...), custom_call_target="tpu_custom_call", output_to_operand_aliasing={{}: (9, {})} | custom-call | tf_op jit(solution)/shard_map/join_outputs/pallas_call | solution.py:280
  (98 shorter events, 0.2 us)
Async XLA Ops:
  4.1 14.1 %collective-permute-start.12 = (bf16[1040,128]{1,0:T(8,128)(2,1)}, bf16[1040,128]{1,0:T(8,128)(2,1)S(1)}, u32[]{:S(2)}, u32[]{:S(2)}) collective-permute-start(bf16[1040,128]{1,0:T(8,128)(2,1)} %get-tuple-element.33), channel_id=1, source_target_pairs={{0,48},{16,32},{32,80},{48,64},{64,112},{80,96},{96,144},{112,128}... | collective-permute-start | bytes 798728 | tf_op jit(solution)/shard_map/ppermute | solution.py:292
  7.1 11.1 %collective-permute-start.3 = (bf16[1040,128]{1,0:T(8,128)(2,1)}, bf16[1040,128]{1,0:T(8,128)(2,1)S(1)}, u32[]{:S(2)}, u32[]{:S(2)}) collective-permute-start(bf16[1040,128]{1,0:T(8,128)(2,1)} %get-tuple-element.33), channel_id=1, source_target_pairs={{0,240},{16,224},{32,16},{48,0},{64,48},{80,32},{96,80},{112,64},{... | collective-permute-start | bytes 798728 | tf_op jit(solution)/shard_map/ppermute | solution.py:292
  11.1 11.4 %collective-permute-start.8 = (bf16[1040,128]{1,0:T(8,128)(2,1)}, bf16[1040,128]{1,0:T(8,128)(2,1)S(1)}, u32[]{:S(2)}, u32[]{:S(2)}) collective-permute-start(bf16[1040,128]{1,0:T(8,128)(2,1)} %get-tuple-element.32.refs_0_), channel_id=1, source_target_pairs={{0,32},{16,48},{32,64},{48,80},{64,96},{80,112},{96,128},{112,144}... | collective-permute-start | bytes 798728 | tf_op jit(solution)/shard_map/ppermute | solution.py:292
  11.1 12.2 %collective-permute-start.2 = (bf16[1040,128]{1,0:T(8,128)(2,1)}, bf16[1040,128]{1,0:T(8,128)(2,1)S(1)}, u32[]{:S(2)}, u32[]{:S(2)}) collective-permute-start(bf16[1040,128]{1,0:T(8,128)(2,1)} %get-tuple-element.32.refs_0_), channel_id=1, source_target_pairs={{0,224},{16,240},{32,0},{48,16},{64,32},{80,48},{96,64},{112,80},{... | collective-permute-start | bytes 798728 | tf_op jit(solution)/shard_map/ppermute | solution.py:292
  18.2 57.5 %copy-start.4 = (bf16[1040,128]{1,0:T(8,128)(2,1)}, bf16[1040,128]{1,0:T(8,128)(2,1)S(1)}, u32[]{:S(2)}) copy-start(bf16[1040,128]{1,0:T(8,128)(2,1)S(1)} %collective-permute-done.12.refs_15_) | copy-start | bytes 798724
  18.2 10.0 %collective-permute-start.13 = (bf16[1040,128]{1,0:T(8,128)(2,1)S(1)}, bf16[1040,128]{1,0:T(8,128)(2,1)S(1)}, u32[]{:S(2)}, u32[]{:S(2)}) collective-permute-start(bf16[1040,128]{1,0:T(8,128)(2,1)S(1)} %collective-permute-done.12.refs_15_), channel_id=1, source_target_pairs={{0,32},{16,48},{32,64},{48,80},{64,96},{80,112},{96,128},{112,144}... | collective-permute-start | bytes 798728 | tf_op jit(solution)/shard_map/ppermute | solution.py:292
  18.3 57.5 %copy-start.5 = (bf16[1040,128]{1,0:T(8,128)(2,1)}, bf16[1040,128]{1,0:T(8,128)(2,1)S(1)}, u32[]{:S(2)}) copy-start(bf16[1040,128]{1,0:T(8,128)(2,1)S(1)} %collective-permute-done.3.refs_3_) | copy-start | bytes 798724
  18.3 10.6 %collective-permute-start.5 = (bf16[1040,128]{1,0:T(8,128)(2,1)S(1)}, bf16[1040,128]{1,0:T(8,128)(2,1)S(1)}, u32[]{:S(2)}, u32[]{:S(2)}) collective-permute-start(bf16[1040,128]{1,0:T(8,128)(2,1)S(1)} %collective-permute-done.3.refs_3_), channel_id=1, source_target_pairs={{0,224},{16,240},{32,0},{48,16},{64,32},{80,48},{96,64},{112,80},{... | collective-permute-start | bytes 798728 | tf_op jit(solution)/shard_map/ppermute | solution.py:292
  22.5 53.3 %copy-start.6 = (bf16[1040,128]{1,0:T(8,128)(2,1)}, bf16[1040,128]{1,0:T(8,128)(2,1)S(1)}, u32[]{:S(2)}) copy-start(bf16[1040,128]{1,0:T(8,128)(2,1)S(1)} %collective-permute-done.8.refs_14_) | copy-start | bytes 798724
  22.5 16.6 %collective-permute-start.9 = (bf16[1040,128]{1,0:T(8,128)(2,1)S(1)}, bf16[1040,128]{1,0:T(8,128)(2,1)S(1)}, u32[]{:S(2)}, u32[]{:S(2)}) collective-permute-start(bf16[1040,128]{1,0:T(8,128)(2,1)S(1)} %collective-permute-done.8.refs_14_), channel_id=1, source_target_pairs={{0,32},{16,48},{32,64},{48,80},{64,96},{80,112},{96,128},{112,144}... | collective-permute-start | bytes 798728 | tf_op jit(solution)/shard_map/ppermute | solution.py:292
  23.3 52.5 %copy-start.7 = (bf16[1040,128]{1,0:T(8,128)(2,1)}, bf16[1040,128]{1,0:T(8,128)(2,1)S(1)}, u32[]{:S(2)}) copy-start(bf16[1040,128]{1,0:T(8,128)(2,1)S(1)} %collective-permute-done.2.refs_2_) | copy-start | bytes 798724
  23.3 16.0 %collective-permute-start.4 = (bf16[1040,128]{1,0:T(8,128)(2,1)S(1)}, bf16[1040,128]{1,0:T(8,128)(2,1)S(1)}, u32[]{:S(2)}, u32[]{:S(2)}) collective-permute-start(bf16[1040,128]{1,0:T(8,128)(2,1)S(1)} %collective-permute-done.2.refs_2_), channel_id=1, source_target_pairs={{0,224},{16,240},{32,0},{48,16},{64,32},{80,48},{96,64},{112,80},{... | collective-permute-start | bytes 798728 | tf_op jit(solution)/shard_map/ppermute | solution.py:292
  28.2 47.6 %copy-start.8 = (bf16[1040,128]{1,0:T(8,128)(2,1)}, bf16[1040,128]{1,0:T(8,128)(2,1)S(1)}, u32[]{:S(2)}) copy-start(bf16[1040,128]{1,0:T(8,128)(2,1)S(1)} %collective-permute-done.13.refs_13_) | copy-start | bytes 798724
  28.2 12.3 %collective-permute-start.14 = (bf16[1040,128]{1,0:T(8,128)(2,1)S(1)}, bf16[1040,128]{1,0:T(8,128)(2,1)S(1)}, u32[]{:S(2)}, u32[]{:S(2)}) collective-permute-start(bf16[1040,128]{1,0:T(8,128)(2,1)S(1)} %collective-permute-done.13.refs_13_), channel_id=1, source_target_pairs={{0,32},{16,48},{32,64},{48,80},{64,96},{80,112},{96,128},{112,144}... | collective-permute-start | bytes 798728 | tf_op jit(solution)/shard_map/ppermute | solution.py:292
  28.9 46.9 %copy-start.9 = (bf16[1040,128]{1,0:T(8,128)(2,1)}, bf16[1040,128]{1,0:T(8,128)(2,1)S(1)}, u32[]{:S(2)}) copy-start(bf16[1040,128]{1,0:T(8,128)(2,1)S(1)} %collective-permute-done.5.refs_5_) | copy-start | bytes 798724
  28.9 11.7 %collective-permute-start.7 = (bf16[1040,128]{1,0:T(8,128)(2,1)S(1)}, bf16[1040,128]{1,0:T(8,128)(2,1)S(1)}, u32[]{:S(2)}, u32[]{:S(2)}) collective-permute-start(bf16[1040,128]{1,0:T(8,128)(2,1)S(1)} %collective-permute-done.5.refs_5_), channel_id=1, source_target_pairs={{0,224},{16,240},{32,0},{48,16},{64,32},{80,48},{96,64},{112,80},{... | collective-permute-start | bytes 798728 | tf_op jit(solution)/shard_map/ppermute | solution.py:292
  33.2 11.3 %collective-permute-start = (s32[8,16]{1,0:T(8,128)S(1)}, s32[8,16]{1,0:T(8,128)S(1)}, u32[]{:S(2)}, u32[]{:S(2)}) collective-permute-start(s32[8,16]{1,0:T(8,128)S(1)} %bitcast.24), channel_id=1, source_target_pairs={{0,16},{16,0},{32,48},{48,32},{64,80},{80,64},{96,112},{112,96},{1... | collective-permute-start | bytes 1544 | tf_op jit(solution)/shard_map/ppermute | solution.py:292
  39.1 36.7 %copy-start.10 = (bf16[1040,128]{1,0:T(8,128)(2,1)}, bf16[1040,128]{1,0:T(8,128)(2,1)S(1)}, u32[]{:S(2)}) copy-start(bf16[1040,128]{1,0:T(8,128)(2,1)S(1)} %collective-permute-done.9.refs_12_) | copy-start | bytes 798724
  39.2 15.3 %collective-permute-start.16 = (bf16[2,512,128]{2,1,0:T(8,128)(2,1)}, bf16[2,512,128]{2,1,0:T(8,128)(2,1)}, u32[]{:S(2)}, u32[]{:S(2)}) collective-permute-start(bf16[2,512,128]{2,1,0:T(8,128)(2,1)} %get-tuple-element.35), channel_id=1, source_target_pairs={{0,16},{4,20},{8,24},{12,28},{16,0},{20,4},{24,8},{28,12},{32,48},... | collective-permute-start | bytes 786440 | tf_op jit(solution)/shard_map/ppermute | solution.py:308
  39.3 36.6 %copy-start.11 = (bf16[1040,128]{1,0:T(8,128)(2,1)}, bf16[1040,128]{1,0:T(8,128)(2,1)S(1)}, u32[]{:S(2)}) copy-start(bf16[1040,128]{1,0:T(8,128)(2,1)S(1)} %collective-permute-done.4.refs_4_) | copy-start | bytes 798724
  39.3 15.2 %collective-permute-start.17 = (bf16[2,512,128]{2,1,0:T(8,128)(2,1)}, bf16[2,512,128]{2,1,0:T(8,128)(2,1)}, u32[]{:S(2)}, u32[]{:S(2)}) collective-permute-start(bf16[2,512,128]{2,1,0:T(8,128)(2,1)} %get-tuple-element.36), channel_id=1, source_target_pairs={{0,4},{4,8},{8,12},{12,0},{16,20},{20,24},{24,28},{28,16},{32,36},... | collective-permute-start | bytes 786440 | tf_op jit(solution)/shard_map/ppermute | solution.py:308
  40.6 35.3 %copy-start = (bf16[1040,128]{1,0:T(8,128)(2,1)}, bf16[1040,128]{1,0:T(8,128)(2,1)S(1)}, u32[]{:S(2)}) copy-start(bf16[1040,128]{1,0:T(8,128)(2,1)S(1)} %collective-permute-done.14.refs_11_) | copy-start | bytes 798724
  40.6 8.6 %collective-permute-start.10 = (bf16[1040,128]{1,0:T(8,128)(2,1)S(1)}, bf16[1040,128]{1,0:T(8,128)(2,1)S(1)}, u32[]{:S(2)}, u32[]{:S(2)}) collective-permute-start(bf16[1040,128]{1,0:T(8,128)(2,1)S(1)} %collective-permute-done.9.refs_12_), channel_id=1, source_target_pairs={{0,32},{16,48},{32,64},{48,80},{64,96},{80,112},{96,128},{112,144}... | collective-permute-start | bytes 798728 | tf_op jit(solution)/shard_map/ppermute | solution.py:292
  40.6 35.3 %copy-start.1 = (bf16[1040,128]{1,0:T(8,128)(2,1)}, bf16[1040,128]{1,0:T(8,128)(2,1)S(1)}, u32[]{:S(2)}) copy-start(bf16[1040,128]{1,0:T(8,128)(2,1)S(1)} %collective-permute-done.7.refs_7_) | copy-start | bytes 798724
  40.6 10.9 %collective-permute-start.6 = (bf16[1040,128]{1,0:T(8,128)(2,1)S(1)}, bf16[1040,128]{1,0:T(8,128)(2,1)S(1)}, u32[]{:S(2)}, u32[]{:S(2)}) collective-permute-start(bf16[1040,128]{1,0:T(8,128)(2,1)S(1)} %collective-permute-done.4.refs_4_), channel_id=1, source_target_pairs={{0,224},{16,240},{32,0},{48,16},{64,32},{80,48},{96,64},{112,80},{... | collective-permute-start | bytes 798728 | tf_op jit(solution)/shard_map/ppermute | solution.py:292
  44.5 12.7 %collective-permute-start.18 = (bf16[2,512,128]{2,1,0:T(8,128)(2,1)}, bf16[2,512,128]{2,1,0:T(8,128)(2,1)}, u32[]{:S(2)}, u32[]{:S(2)}) collective-permute-start(bf16[2,512,128]{2,1,0:T(8,128)(2,1)} %get-tuple-element.37), channel_id=1, source_target_pairs={{0,20},{4,24},{8,28},{12,16},{16,4},{20,8},{24,12},{28,0},{32,52},... | collective-permute-start | bytes 786440 | tf_op jit(solution)/shard_map/ppermute | solution.py:308
  49.1 26.7 %copy-start.2 = (bf16[1040,128]{1,0:T(8,128)(2,1)}, bf16[1040,128]{1,0:T(8,128)(2,1)S(1)}, u32[]{:S(2)}) copy-start(bf16[1040,128]{1,0:T(8,128)(2,1)S(1)} %collective-permute-done.10.refs_10_) | copy-start | bytes 798724
  49.1 12.4 %collective-permute-start.19 = (bf16[2,512,128]{2,1,0:T(8,128)(2,1)}, bf16[2,512,128]{2,1,0:T(8,128)(2,1)}, u32[]{:S(2)}, u32[]{:S(2)}) collective-permute-start(bf16[2,512,128]{2,1,0:T(8,128)(2,1)} %get-tuple-element.38), channel_id=1, source_target_pairs={{0,8},{4,12},{8,0},{12,4},{16,24},{20,28},{24,16},{28,20},{32,40},... | collective-permute-start | bytes 786440 | tf_op jit(solution)/shard_map/ppermute | solution.py:308
  51.5 24.4 %copy-start.3 = (bf16[1040,128]{1,0:T(8,128)(2,1)}, bf16[1040,128]{1,0:T(8,128)(2,1)S(1)}, u32[]{:S(2)}) copy-start(bf16[1040,128]{1,0:T(8,128)(2,1)S(1)} %collective-permute-done.6.refs_6_) | copy-start | bytes 798724
  51.5 15.6 %collective-permute-start.20 = (bf16[2,512,128]{2,1,0:T(8,128)(2,1)}, bf16[2,512,128]{2,1,0:T(8,128)(2,1)}, u32[]{:S(2)}, u32[]{:S(2)}) collective-permute-start(bf16[2,512,128]{2,1,0:T(8,128)(2,1)} %get-tuple-element.39), channel_id=1, source_target_pairs={{0,24},{4,28},{8,16},{12,20},{16,8},{20,12},{24,0},{28,4},{32,56},... | collective-permute-start | bytes 786440 | tf_op jit(solution)/shard_map/ppermute | solution.py:308
  54.5 21.3 %collective-permute-start.1 = (bf16[1040,128]{1,0:T(8,128)(2,1)}, bf16[1040,128]{1,0:T(8,128)(2,1)S(1)}, u32[]{:S(2)}, u32[]{:S(2)}) collective-permute-start(bf16[1040,128]{1,0:T(8,128)(2,1)} %get-tuple-element.33), channel_id=1, source_target_pairs={{0,16},{16,0},{32,48},{48,32},{64,80},{80,64},{96,112},{112,96},{1... | collective-permute-start | bytes 798728 | tf_op jit(solution)/shard_map/ppermute | solution.py:292
  54.5 21.3 %collective-permute-start.15 = (bf16[1040,128]{1,0:T(8,128)(2,1)}, bf16[1040,128]{1,0:T(8,128)(2,1)}, u32[]{:S(2)}, u32[]{:S(2)}) collective-permute-start(bf16[1040,128]{1,0:T(8,128)(2,1)} %broadcast_select_fusion), channel_id=1, source_target_pairs={{0,32},{16,240},{32,64},{48,16},{64,96},{80,48},{96,128},{112,80},... | collective-permute-start | bytes 798728 | tf_op jit(solution)/shard_map/ppermute | solution.py:292
  57.2 18.6 %collective-permute-start.11 = (bf16[1040,128]{1,0:T(8,128)(2,1)}, bf16[1040,128]{1,0:T(8,128)(2,1)}, u32[]{:S(2)}, u32[]{:S(2)}) collective-permute-start(bf16[1040,128]{1,0:T(8,128)(2,1)} %broadcast_select_fusion.1), channel_id=1, source_target_pairs={{0,32},{16,240},{32,64},{48,16},{64,96},{80,48},{96,128},{112,80},... | collective-permute-start | bytes 798728 | tf_op jit(solution)/shard_map/ppermute | solution.py:292
  61.5 7.8 %collective-permute-start.21 = (bf16[2,512,128]{2,1,0:T(8,128)(2,1)}, bf16[2,512,128]{2,1,0:T(8,128)(2,1)}, u32[]{:S(2)}, u32[]{:S(2)}) collective-permute-start(bf16[2,512,128]{2,1,0:T(8,128)(2,1)} %get-tuple-element.40), channel_id=1, source_target_pairs={{0,12},{4,0},{8,4},{12,8},{16,28},{20,16},{24,20},{28,24},{32,44},... | collective-permute-start | bytes 786440 | tf_op jit(solution)/shard_map/ppermute | solution.py:308
  67.1 8.6 %collective-permute-start.22 = (bf16[2,512,128]{2,1,0:T(8,128)(2,1)}, bf16[2,512,128]{2,1,0:T(8,128)(2,1)}, u32[]{:S(2)}, u32[]{:S(2)}) collective-permute-start(bf16[2,512,128]{2,1,0:T(8,128)(2,1)} %get-tuple-element.41), channel_id=1, source_target_pairs={{0,28},{4,16},{8,20},{12,24},{16,12},{20,0},{24,4},{28,8},{32,60},... | collective-permute-start | bytes 786440 | tf_op jit(solution)/shard_map/ppermute | solution.py:308
  88.5 19.3 %collective-permute-start.25 = (bf16[2,256,128]{2,1,0:T(8,128)(2,1)}, bf16[2,256,128]{2,1,0:T(8,128)(2,1)S(1)}, u32[]{:S(2)}, u32[]{:S(2)}) collective-permute-start(bf16[2,256,128]{2,1,0:T(8,128)(2,1)} %get-tuple-element.47), channel_id=1, source_target_pairs={{16,0},{20,4},{24,8},{28,12},{0,16},{4,20},{8,24},{12,28},{48,32},... | collective-permute-start | bytes 393224 | tf_op jit(solution)/shard_map/ppermute | solution.py:308
  88.9 14.6 %copy-start.33 = (f32[4,128]{1,0:T(4,128)S(1)}, f32[4,128]{1,0:T(4,128)}, u32[]{:S(2)}) copy-start(f32[4,128]{1,0:T(4,128)} %get-tuple-element.45) | copy-start | bytes 6148
  88.9 23.4 %copy-start.27 = (f32[4,128]{1,0:T(4,128)S(1)}, f32[4,128]{1,0:T(4,128)}, u32[]{:S(2)}) copy-start(f32[4,128]{1,0:T(4,128)} %get-tuple-element.43) | copy-start | bytes 6148
  88.9 24.1 %copy-start.32 = (bf16[2,256,128]{2,1,0:T(8,128)(2,1)S(1)}, bf16[2,256,128]{2,1,0:T(8,128)(2,1)}, u32[]{:S(2)}) copy-start(bf16[2,256,128]{2,1,0:T(8,128)(2,1)} %get-tuple-element.49) | copy-start | bytes 393220
  88.9 26.1 %copy-start.31 = (bf16[2,256,128]{2,1,0:T(8,128)(2,1)S(1)}, bf16[2,256,128]{2,1,0:T(8,128)(2,1)}, u32[]{:S(2)}) copy-start(bf16[2,256,128]{2,1,0:T(8,128)(2,1)} %get-tuple-element.50) | copy-start | bytes 393220
  88.9 29.3 %copy-start.30 = (bf16[2,256,128]{2,1,0:T(8,128)(2,1)S(1)}, bf16[2,256,128]{2,1,0:T(8,128)(2,1)}, u32[]{:S(2)}) copy-start(bf16[2,256,128]{2,1,0:T(8,128)(2,1)} %get-tuple-element.51) | copy-start | bytes 393220
  89.0 31.9 %copy-start.29 = (bf16[2,256,128]{2,1,0:T(8,128)(2,1)S(1)}, bf16[2,256,128]{2,1,0:T(8,128)(2,1)}, u32[]{:S(2)}) copy-start(bf16[2,256,128]{2,1,0:T(8,128)(2,1)} %get-tuple-element.52) | copy-start | bytes 393220
  89.0 35.0 %copy-start.28 = (bf16[2,256,128]{2,1,0:T(8,128)(2,1)S(1)}, bf16[2,256,128]{2,1,0:T(8,128)(2,1)}, u32[]{:S(2)}) copy-start(bf16[2,256,128]{2,1,0:T(8,128)(2,1)} %get-tuple-element.53) | copy-start | bytes 393220
  89.0 20.1 %collective-permute-start.26 = (bf16[2,256,128]{2,1,0:T(8,128)(2,1)}, bf16[2,256,128]{2,1,0:T(8,128)(2,1)S(1)}, u32[]{:S(2)}, u32[]{:S(2)}) collective-permute-start(bf16[2,256,128]{2,1,0:T(8,128)(2,1)} %get-tuple-element.48), channel_id=1, source_target_pairs={{4,0},{8,4},{12,8},{0,12},{20,16},{24,20},{28,24},{16,28},{36,32},... | collective-permute-start | bytes 393224 | tf_op jit(solution)/shard_map/ppermute | solution.py:308
  102.2 8.9 %collective-permute-start.32 = (bf16[2,256,128]{2,1,0:T(8,128)(2,1)}, bf16[2,256,128]{2,1,0:T(8,128)(2,1)S(1)}, u32[]{:S(2)}, u32[]{:S(2)}) collective-permute-start(bf16[2,256,128]{2,1,0:T(8,128)(2,1)} %get-tuple-element.55), channel_id=1, source_target_pairs={{16,0},{20,4},{24,8},{28,12},{0,16},{4,20},{8,24},{12,28},{48,32},... | collective-permute-start | bytes 393224 | tf_op jit(solution)/shard_map/ppermute | solution.py:308
  102.8 8.5 %collective-permute-start.33 = (bf16[2,256,128]{2,1,0:T(8,128)(2,1)}, bf16[2,256,128]{2,1,0:T(8,128)(2,1)S(1)}, u32[]{:S(2)}, u32[]{:S(2)}) collective-permute-start(bf16[2,256,128]{2,1,0:T(8,128)(2,1)} %get-tuple-element.56), channel_id=1, source_target_pairs={{4,0},{8,4},{12,8},{0,12},{20,16},{24,20},{28,24},{16,28},{36,32},... | collective-permute-start | bytes 393224 | tf_op jit(solution)/shard_map/ppermute | solution.py:308
  103.6 1.4 %collective-permute-start.24 = (f32[4,128]{1,0:T(4,128)S(1)}, f32[4,128]{1,0:T(4,128)S(1)}, u32[]{:S(2)}, u32[]{:S(2)}) collective-permute-start(f32[4,128]{1,0:T(4,128)S(1)} %copy-done.33), channel_id=1, source_target_pairs={{0,16},{16,0},{32,48},{48,32},{64,80},{80,64},{96,112},{112,96},{1... | collective-permute-start | bytes 6152 | tf_op jit(solution)/shard_map/ppermute | solution.py:292
  105.0 1.4 collective-permute-start.23
  106.4 6.6 %collective-permute-start.34 = (bf16[2,256,128]{2,1,0:T(8,128)(2,1)}, bf16[2,256,128]{2,1,0:T(8,128)(2,1)S(1)}, u32[]{:S(2)}, u32[]{:S(2)}) collective-permute-start(bf16[2,256,128]{2,1,0:T(8,128)(2,1)} %get-tuple-element.57), channel_id=1, source_target_pairs={{20,0},{24,4},{28,8},{16,12},{4,16},{8,20},{12,24},{0,28},{52,32},... | collective-permute-start | bytes 393224 | tf_op jit(solution)/shard_map/ppermute | solution.py:308
  107.8 26.9 %copy-start.13 = (bf16[2,256,128]{2,1,0:T(8,128)(2,1)}, bf16[2,256,128]{2,1,0:T(8,128)(2,1)S(1)}, u32[]{:S(2)}) copy-start(bf16[2,256,128]{2,1,0:T(8,128)(2,1)S(1)} %collective-permute-done.25.refs_1_) | copy-start | bytes 393220
  107.8 7.3 %collective-permute-start.35 = (bf16[2,256,128]{2,1,0:T(8,128)(2,1)}, bf16[2,256,128]{2,1,0:T(8,128)(2,1)S(1)}, u32[]{:S(2)}, u32[]{:S(2)}) collective-permute-start(bf16[2,256,128]{2,1,0:T(8,128)(2,1)} %get-tuple-element.58), channel_id=1, source_target_pairs={{8,0},{12,4},{0,8},{4,12},{24,16},{28,20},{16,24},{20,28},{40,32},... | collective-permute-start | bytes 393224 | tf_op jit(solution)/shard_map/ppermute | solution.py:308
  109.1 25.5 %copy-start.14 = (bf16[2,256,128]{2,1,0:T(8,128)(2,1)}, bf16[2,256,128]{2,1,0:T(8,128)(2,1)S(1)}, u32[]{:S(2)}) copy-start(bf16[2,256,128]{2,1,0:T(8,128)(2,1)S(1)} %collective-permute-done.26.refs_2_) | copy-start | bytes 393220
  109.1 9.1 %collective-permute-start.36 = (bf16[2,256,128]{2,1,0:T(8,128)(2,1)}, bf16[2,256,128]{2,1,0:T(8,128)(2,1)S(1)}, u32[]{:S(2)}, u32[]{:S(2)}) collective-permute-start(bf16[2,256,128]{2,1,0:T(8,128)(2,1)} %get-tuple-element.59), channel_id=1, source_target_pairs={{24,0},{28,4},{16,8},{20,12},{8,16},{12,20},{0,24},{4,28},{56,32},... | collective-permute-start | bytes 393224 | tf_op jit(solution)/shard_map/ppermute | solution.py:308
  111.1 13.5 %copy-start.20 = (bf16[2,256,128]{2,1,0:T(8,128)(2,1)}, bf16[2,256,128]{2,1,0:T(8,128)(2,1)S(1)}, u32[]{:S(2)}) copy-start(bf16[2,256,128]{2,1,0:T(8,128)(2,1)S(1)} %collective-permute-done.32.refs_1_) | copy-start | bytes 393220
  111.1 9.8 %collective-permute-start.37 = (bf16[2,256,128]{2,1,0:T(8,128)(2,1)}, bf16[2,256,128]{2,1,0:T(8,128)(2,1)S(1)}, u32[]{:S(2)}, u32[]{:S(2)}) collective-permute-start(bf16[2,256,128]{2,1,0:T(8,128)(2,1)} %get-tuple-element.60), channel_id=1, source_target_pairs={{12,0},{0,4},{4,8},{8,12},{28,16},{16,20},{20,24},{24,28},{44,32},... | collective-permute-start | bytes 393224 | tf_op jit(solution)/shard_map/ppermute | solution.py:308
  111.4 13.2 %copy-start.21 = (bf16[2,256,128]{2,1,0:T(8,128)(2,1)}, bf16[2,256,128]{2,1,0:T(8,128)(2,1)S(1)}, u32[]{:S(2)}) copy-start(bf16[2,256,128]{2,1,0:T(8,128)(2,1)S(1)} %collective-permute-done.33.refs_2_) | copy-start | bytes 393220
  111.4 12.5 %collective-permute-start.38 = (bf16[2,256,128]{2,1,0:T(8,128)(2,1)}, bf16[2,256,128]{2,1,0:T(8,128)(2,1)S(1)}, u32[]{:S(2)}, u32[]{:S(2)}) collective-permute-start(bf16[2,256,128]{2,1,0:T(8,128)(2,1)} %get-tuple-element.61), channel_id=1, source_target_pairs={{28,0},{16,4},{20,8},{24,12},{12,16},{0,20},{4,24},{8,28},{60,32},... | collective-permute-start | bytes 393224 | tf_op jit(solution)/shard_map/ppermute | solution.py:308
  113.0 11.6 %copy-start.22 = (bf16[2,256,128]{2,1,0:T(8,128)(2,1)}, bf16[2,256,128]{2,1,0:T(8,128)(2,1)S(1)}, u32[]{:S(2)}) copy-start(bf16[2,256,128]{2,1,0:T(8,128)(2,1)S(1)} %collective-permute-done.34.refs_3_) | copy-start | bytes 393220
  113.0 14.3 %collective-permute-start.27 = (bf16[2,256,128]{2,1,0:T(8,128)(2,1)S(1)}, bf16[2,256,128]{2,1,0:T(8,128)(2,1)S(1)}, u32[]{:S(2)}, u32[]{:S(2)}) collective-permute-start(bf16[2,256,128]{2,1,0:T(8,128)(2,1)S(1)} %copy-done.32), channel_id=1, source_target_pairs={{20,0},{24,4},{28,8},{16,12},{4,16},{8,20},{12,24},{0,28},{52,32},... | collective-permute-start | bytes 393224 | tf_op jit(solution)/shard_map/ppermute | solution.py:308
  115.1 9.5 %copy-start.23 = (bf16[2,256,128]{2,1,0:T(8,128)(2,1)}, bf16[2,256,128]{2,1,0:T(8,128)(2,1)S(1)}, u32[]{:S(2)}) copy-start(bf16[2,256,128]{2,1,0:T(8,128)(2,1)S(1)} %collective-permute-done.35.refs_4_) | copy-start | bytes 393220
  115.1 12.3 %collective-permute-start.28 = (bf16[2,256,128]{2,1,0:T(8,128)(2,1)S(1)}, bf16[2,256,128]{2,1,0:T(8,128)(2,1)S(1)}, u32[]{:S(2)}, u32[]{:S(2)}) collective-permute-start(bf16[2,256,128]{2,1,0:T(8,128)(2,1)S(1)} %copy-done.31), channel_id=1, source_target_pairs={{8,0},{12,4},{0,8},{4,12},{24,16},{28,20},{16,24},{20,28},{40,32},... | collective-permute-start | bytes 393224 | tf_op jit(solution)/shard_map/ppermute | solution.py:308
  118.2 11.3 %collective-permute-start.29 = (bf16[2,256,128]{2,1,0:T(8,128)(2,1)S(1)}, bf16[2,256,128]{2,1,0:T(8,128)(2,1)S(1)}, u32[]{:S(2)}, u32[]{:S(2)}) collective-permute-start(bf16[2,256,128]{2,1,0:T(8,128)(2,1)S(1)} %copy-done.30), channel_id=1, source_target_pairs={{24,0},{28,4},{16,8},{20,12},{8,16},{12,20},{0,24},{4,28},{56,32},... | collective-permute-start | bytes 393224 | tf_op jit(solution)/shard_map/ppermute | solution.py:308
  120.9 11.0 %collective-permute-start.30 = (bf16[2,256,128]{2,1,0:T(8,128)(2,1)S(1)}, bf16[2,256,128]{2,1,0:T(8,128)(2,1)S(1)}, u32[]{:S(2)}, u32[]{:S(2)}) collective-permute-start(bf16[2,256,128]{2,1,0:T(8,128)(2,1)S(1)} %copy-done.29), channel_id=1, source_target_pairs={{12,0},{0,4},{4,8},{8,12},{28,16},{16,20},{20,24},{24,28},{44,32},... | collective-permute-start | bytes 393224 | tf_op jit(solution)/shard_map/ppermute | solution.py:308
  123.9 10.7 %collective-permute-start.31 = (bf16[2,256,128]{2,1,0:T(8,128)(2,1)S(1)}, bf16[2,256,128]{2,1,0:T(8,128)(2,1)S(1)}, u32[]{:S(2)}, u32[]{:S(2)}) collective-permute-start(bf16[2,256,128]{2,1,0:T(8,128)(2,1)S(1)} %copy-done.28), channel_id=1, source_target_pairs={{28,0},{16,4},{20,8},{24,12},{12,16},{0,20},{4,24},{8,28},{60,32},... | collective-permute-start | bytes 393224 | tf_op jit(solution)/shard_map/ppermute | solution.py:308
  (9 other events, 34.8 us)
where the time goes:
time: 138 us
  starting transfers between devices  50.1 us (36%)
  waiting for transfers between devices  43.9 us (32%)
  Pallas kernels  36.8 us (27%)
  local copies, waits for them, and re-layouts  3.43 us (2%)
  other arithmetic  2.8 us (2%)
    ppermute x21, waiting for transfers between devices, by_part(): return lax.ppermute(value, ('seq', 'head'), pairs)  30.1 us
    ppermute x18, starting transfers between devices, by_seq(): lax.ppermute(value, 'seq', [(s, move(s // 2, s % 2)) for s in range(SHARD...  27.3 us
    pallas_call x2, Pallas kernels, call_attend(): pl.pallas_call(functools.partial(attend, chunk), grid=(1,), in_specs=[SME...  23.9 us
    ppermute x21, starting transfers between devices, by_part(): return lax.ppermute(value, ('seq', 'head'), pairs)  22.8 us
    ppermute x18, waiting for transfers between devices, by_seq(): lax.ppermute(value, 'seq', [(s, move(s // 2, s % 2)) for s in range(SHARD...  13.8 us
    pallas_call x2, Pallas kernels, call_join_outputs(): pl.pallas_call(functools.partial(join_outputs, TOK_CHUNK), grid=(1,), in_...  5.41 us
    pallas_call x1, Pallas kernels, call_split_queries(): pl.pallas_call(functools.partial(split_queries, tokens), grid=(steps,), i...  4.61 us
    pallas_call x1, Pallas kernels, call_split_pools(): pl.pallas_call(split_pools, in_specs=[SMEM, VMEM, VMEM, VMEM], out_specs=...  2.84 us
  transfers between devices with their start and end apart: 39, of which 17 were waited for; matrix products, arithmetic and copies ran while one was open for 3% of the time, Pallas kernels for 14%

commit v1 on v0

--- a/solution.py
+++ b/solution.py
@@ -23,11 +23,12 @@
 COMP_PAD = 16
 PIECE = 2 * TOK + COMP_PAD
 PARTS = 8
-CHUNKS = 2
-TOK_CHUNK = TOK // CHUNKS
-TILES_CHUNK = TILES // CHUNKS
+POOL_TOK = 128
+JOIN_TOK = 64
+CHUNKS = ((1, 2), (3, 0))
+WIDE = 2
 KEYS = TOPN * BLOCK
-ROWS = HPG * BLOCK
+ROWS = WIDE * 2 * BLOCK
 COMP_ROWS = SHARDS * COMP_PAD
 STEPS = 4
 STEP_BLOCKS = TOPN // STEPS
@@ -58,21 +59,26 @@
     col = iota((2 * step, step * GROUPS), 1)
     group = jnp.where(row < step, mine, theirs)
     pick = one_hot(col == (row % step) * GROUPS + group)
-    for i in range(TOK // step):
+    base = pl.program_id(0) * POOL_TOK
+    for i in range(POOL_TOK // step):
         rows = pl.ds(i * step * GROUPS, step * GROUPS)
-        both = jnp.concatenate([keys[rows, :], values[rows, :]], axis=1)
-        got = dot(pick, both).astype(jnp.bfloat16)
-        own[pl.ds(i * step, step), :] = got[:step, :DH]
-        own[pl.ds(TOK + i * step, step), :] = got[:step, DH:]
-        other[pl.ds(i * step, step), :] = got[step:, :DH]
-        other[pl.ds(TOK + i * step, step), :] = got[step:, DH:]
-    row = iota((2 * COMP_PAD, TILES * GROUPS), 0)
-    col = iota((2 * COMP_PAD, TILES * GROUPS), 1)
-    group = jnp.where(row < COMP_PAD, mine, theirs)
-    block = row % COMP_PAD
-    got = dot(one_hot((col == block * GROUPS + group) & (block < TILES)), comp[...]).astype(jnp.bfloat16)
-    own[pl.ds(2 * TOK, COMP_PAD), :] = got[:COMP_PAD]
-    other[pl.ds(2 * TOK, COMP_PAD), :] = got[COMP_PAD:]
+        got = dot(pick, jnp.concatenate([keys[rows, :], values[rows, :]], axis=1)).astype(jnp.bfloat16)
+        low = pl.ds(pl.multiple_of(base + i * step, step), step)
+        high = pl.ds(pl.multiple_of(base + TOK + i * step, step), step)
+        own[low, :] = got[:step, :DH]
+        own[high, :] = got[:step, DH:]
+        other[low, :] = got[step:, :DH]
+        other[high, :] = got[step:, DH:]
+
+    @pl.when(pl.program_id(0) == 0)
+    def _():
+        row = iota((2 * COMP_PAD, TILES * GROUPS), 0)
+        col = iota((2 * COMP_PAD, TILES * GROUPS), 1)
+        group = jnp.where(row < COMP_PAD, mine, theirs)
+        block = row % COMP_PAD
+        got = dot(one_hot((col == block * GROUPS + group) & (block < TILES)), comp[...]).astype(jnp.bfloat16)
+        own[pl.ds(2 * TOK, COMP_PAD), :] = got[:COMP_PAD]
+        other[pl.ds(2 * TOK, COMP_PAD), :] = got[COMP_PAD:]
 
 
 def row_of(r, place):
@@ -110,12 +116,15 @@
         out[pl.ds(i * 512 + 256, 256), :] = got[:, DH:]
 
 
-def attend(chunk, place, picks, *refs):
+def attend(follows, place, picks, *refs):
     pieces = refs[: 2 * CHIPS]
-    queries = refs[2 * CHIPS : 2 * CHIPS + PARTS]
-    outs = refs[2 * CHIPS + PARTS : 2 * CHIPS + 2 * PARTS]
-    pooled = refs[2 * CHIPS + 2 * PARTS : 2 * CHIPS + 2 * PARTS + 2]
-    pool, comp, mask, *rest, sems = refs[2 * CHIPS + 2 * PARTS + 2 :]
+    refs = refs[2 * CHIPS :]
+    count = 2 * WIDE
+    queries, refs = refs[:count], refs[count:]
+    sofar, refs = (refs[:2], refs[2:]) if follows else (None, refs)
+    outs, refs = refs[:count], refs[count:]
+    pooled, refs = refs[:2], refs[2:]
+    pool, comp, mask, *rest, sems = refs
     turned, scores, logits, tops = rest[0:2], rest[2:4], rest[4:6], rest[6:8]
     core, chip = place[1], place[2]
     copies = []
@@ -145,17 +154,17 @@
         return pl.ds(pl.multiple_of(local * BLOCK, BLOCK), BLOCK)
 
     def number_of(local, half):
-        return (2 * chip + (core + half) % 2) * TILES + chunk * TILES_CHUNK + local
+        return (2 * chip + (core + half) % 2) * TILES + local
 
     def pick_of(local, half, b):
-        return picks[(half * TILES + chunk * TILES_CHUNK + local) * TOPN + b]
+        return picks[(half * TILES + local) * TOPN + b]
 
     def block_of(n, offset):
         return pool[n // TILES, pl.ds(pl.multiple_of(offset + n % TILES * BLOCK, BLOCK), BLOCK), :]
 
     def turn(local, half):
         at = spot(local)
-        query = jnp.concatenate([queries[2 * dx + half][j, at, :] for dx in range(COLS) for j in range(2)], axis=0)
+        query = jnp.concatenate([queries[2 * w + half][j, at, :] for w in range(WIDE) for j in range(2)], axis=0)
         turned[half][pl.ds(0, DH), :] = query.T
 
     def score(local, half, i):
@@ -183,17 +192,19 @@
     def finish(local, half, mixed):
         result = (mixed[:DH] * (1.0 / mixed[DH : DH + 1])).astype(jnp.bfloat16).T
         at = spot(local)
-        for dx in range(COLS):
+        for w in range(WIDE):
             for j in range(2):
-                r = (dx * 2 + j) * BLOCK
-                outs[2 * dx + half][j, at, :] = result[r : r + BLOCK]
+                r = (w * 2 + j) * BLOCK
+                outs[2 * w + half][j, at, :] = result[r : r + BLOCK]
         number = number_of(local, half)
         known = jnp.where(block_row <= number, logits[half][...], -jnp.inf)
         raised = jnp.exp2((known - jnp.max(known, axis=0, keepdims=True)) * EXP2_SCALE)
         prob = raised * (1.0 / jnp.sum(raised, axis=0, keepdims=True))
-        folded = prob[:, :128] + prob[:, 128:256] + prob[:, 256:384] + prob[:, 384:]
+        folded = prob[:, :128] + prob[:, 128:]
         factor = (number + 1).astype(jnp.float32) * (1.0 / (BLOCK * HPG))
-        pooled[half][pl.ds(local, 1), :] = jnp.sum(folded.T, axis=0, keepdims=True) * factor
+        sums = jnp.sum(folded.T, axis=0, keepdims=True) * factor
+        at = pl.ds(local, 1)
+        pooled[half][at, :] = sums + sofar[half][at, :] if follows else sums
 
     def pair(this, half, that, other):
         top = jnp.max(tops[half][...], axis=0, keepdims=True)
@@ -205,7 +216,7 @@
         finish(this, half, mixed)
 
     def step(local, carry):
-        following = jnp.minimum(local + 1, TILES_CHUNK - 1)
+        following = jnp.minimum(local + 1, TILES - 1)
         pair(local, 0, local, 1)
         turn(following, 0)
         pair(local, 1, following, 0)
@@ -216,7 +227,7 @@
     turn(0, 1)
     for i in range(STEPS):
         score(0, 0, i)
-    lax.fori_loop(0, TILES_CHUNK, step, 0)
+    lax.fori_loop(0, TILES, step, 0)
 
 
 SMEM = pl.BlockSpec(memory_space=pltpu.SMEM)
@@ -229,10 +240,13 @@
 
 
 def call_split_pools(place, keys, values, comp):
+    rows = pl.BlockSpec((POOL_TOK * GROUPS, DH), lambda i: (i, 0))
+    piece = pl.BlockSpec((PIECE, DH), lambda i: (0, 0))
     return pl.pallas_call(
         split_pools,
-        in_specs=[SMEM, VMEM, VMEM, VMEM],
-        out_specs=[VMEM, VMEM],
+        grid=(TOK // POOL_TOK,),
+        in_specs=[SMEM, rows, rows, pl.BlockSpec((TILES * GROUPS, DH), lambda i: (0, 0))],
+        out_specs=[piece, piece],
         out_shape=[bf16(PIECE, DH)] * 2,
         name="split_pools",
     )(place, keys, values, comp)
@@ -251,16 +265,15 @@
     )(place, queries)
 
 
-def call_attend(chunk, place, picks, pieces, queries):
+def call_attend(chunk, place, picks, pieces, queries, sofar):
+    parts = pl.BlockSpec((2, TOK, DH), lambda i: (0, 0, 0))
+    sums = pl.BlockSpec((TILES, NBLK), lambda i: (0, 0))
     return pl.pallas_call(
-        functools.partial(attend, chunk),
+        functools.partial(attend, bool(sofar)),
         grid=(1,),
-        in_specs=[SMEM, SMEM]
-        + [ANY] * (2 * CHIPS)
-        + [pl.BlockSpec((2, TOK_CHUNK, DH), lambda i: (0, chunk, 0))] * PARTS,
-        out_specs=[pl.BlockSpec((2, TOK_CHUNK, DH), lambda i: (0, 0, 0))] * PARTS
-        + [pl.BlockSpec((TILES_CHUNK, NBLK), lambda i: (0, 0))] * 2,
-        out_shape=[bf16(2, TOK_CHUNK, DH)] * PARTS + [jax.ShapeDtypeStruct((TILES_CHUNK, NBLK), jnp.float32)] * 2,
+        in_specs=[SMEM, SMEM] + [ANY] * (2 * CHIPS) + [parts] * (2 * WIDE) + [sums] * len(sofar),
+        out_specs=[parts] * (2 * WIDE) + [sums] * 2,
+        out_shape=[bf16(2, TOK, DH)] * (2 * WIDE) + [jax.ShapeDtypeStruct((TILES, NBLK), jnp.float32)] * 2,
         scratch_shapes=[
             pltpu.VMEM((SHARDS, PIECE, DH), jnp.bfloat16),
             pltpu.VMEM((NBLK, DH), jnp.bfloat16),
@@ -272,20 +285,18 @@
         + [pltpu.VMEM((8, ROWS), jnp.float32)] * 2
         + [pltpu.SemaphoreType.DMA((2 * CHIPS,))],
         name="attend",
-    )(place, picks, *pieces, *queries)
-
-
-def call_join_outputs(chunk, place, parts, before):
-    extra = [] if before is None else [before]
+    )(place, picks, *pieces, *[queries[2 * dx + half] for dx in chunk for half in range(2)], *sofar)
+
+
+def call_join_outputs(place, parts):
     return pl.pallas_call(
-        functools.partial(join_outputs, TOK_CHUNK),
-        grid=(1,),
-        in_specs=[SMEM] + [pl.BlockSpec((2, TOK_CHUNK, DH), lambda i: (0, 0, 0))] * PARTS + [ANY] * len(extra),
-        out_specs=pl.BlockSpec((TOK_CHUNK * 16, DH), lambda i: (chunk, 0)),
+        functools.partial(join_outputs, JOIN_TOK),
+        grid=(TOK // JOIN_TOK,),
+        in_specs=[SMEM] + [pl.BlockSpec((2, JOIN_TOK, DH), lambda i: (0, i, 0))] * PARTS,
+        out_specs=pl.BlockSpec((JOIN_TOK * 16, DH), lambda i: (i, 0)),
         out_shape=bf16(TOK * 16, DH),
-        input_output_aliases={PARTS + 1: 0} if extra else {},
         name="join_outputs",
-    )(place, *parts, *extra)
+    )(place, *parts)
 
 
 def by_seq(value, move):
@@ -327,9 +338,8 @@
             down[h] = by_seq(down[h], lambda z, c: to_seq(z - 1, c + turn))
             pieces[2 * (CHIPS - k) + h] = up[h]
             pieces[2 * k + h] = down[h]
-    for h in range(2):
-        onward = jnp.where(core == 0, up[h], down[h])
-        pieces[2 * 4 + h] = by_seq(onward, lambda z, c: to_seq(z + (1 if c == 0 else -1), c))
+    pieces[2 * 4] = by_seq(up[0], lambda z, c: to_seq(z + 1, c))
+    pieces[2 * 4 + 1] = by_seq(down[1], lambda z, c: to_seq(z - 1, c))
     parts = call_split_queries(place, queries.reshape(TOK * 16, DH))
     moved = []
     for k in range(PARTS):
@@ -339,19 +349,16 @@
     theirs = lax.dynamic_index_in_dim(groups, 2 * col + 1 - core, 0, False)
     theirs = by_seq(theirs, lambda z, c: to_seq(z, c + 1))
     picks = jnp.concatenate([mine, theirs]).reshape(-1)
-    attended, kept, came, joined = None, [], [], []
-    for chunk in range(CHUNKS):
-        *outs, keep, send = call_attend(chunk, place, picks, pieces, moved)
-        back = []
-        for k in range(PARTS):
-            back.append(by_part(outs[k], k // 2, k % 2, True))
-        came.append(by_seq(send, lambda z, c: to_seq(z, c + 1)))
-        kept.append(keep)
-        joined.append(back)
-    for chunk in range(CHUNKS):
-        attended = call_join_outputs(chunk, place, joined[chunk], attended)
-    kept, came = jnp.concatenate(kept), jnp.concatenate(came)
-    both = jnp.where(core == 0, jnp.stack([kept, came], axis=1), jnp.stack([came, kept], axis=1))
+    joined, sums = [None] * PARTS, []
+    for chunk in CHUNKS:
+        *outs, keep, send = call_attend(chunk, place, picks, pieces, moved, sums)
+        sums = [keep, send]
+        for w, dx in enumerate(chunk):
+            for half in range(2):
+                joined[2 * dx + half] = by_part(outs[2 * w + half], dx, half, True)
+    came = by_seq(send, lambda z, c: to_seq(z, c + 1))
+    attended = call_join_outputs(place, joined)
+    both = jnp.where(core == 0, jnp.stack([keep, came], axis=1), jnp.stack([came, keep], axis=1))
     return both[None], attended.reshape(1, TOK, 2, GROUPS, DH)
 
 

time: 138 us -> 126 us (0.913); the launches traced: 138 us -> 124 us
  waiting for transfers between devices: 43.9 us -> 34.2 us
  starting transfers between devices: 50.1 us -> 42.8 us
  Pallas kernels: 36.8 us -> 41.8 us
    ppermute x21 -> x14, waiting for transfers between devices: 30.1 us -> 23.2 us  [by_part(): return lax.ppermute(value, ('seq', 'head'), pairs)]
    pallas_call x5 -> x4, Pallas kernels: 32.2 us -> 37.2 us  [the longest x2 27.4 us: call_attend(): pl.pallas_call(functools.partial(attend, bool(sofar)), grid=(1,), in_spec...]
    ppermute x18 -> x17, starting transfers between devices: 27.3 us -> 22.4 us  [by_seq(): lax.ppermute(value, 'seq', [(s, move(s // 2, s % 2)) for s in range(SHARD...]
    ppermute x18 -> x17, waiting for transfers between devices: 13.8 us -> 11 us  [by_seq(): lax.ppermute(value, 'seq', [(s, move(s // 2, s % 2)) for s in range(SHARD...]
    ppermute x21 -> x14, starting transfers between devices: 22.8 us -> 20.4 us  [by_part(): return lax.ppermute(value, ('seq', 'head'), pairs)]
  transfers between devices with their start and end apart: 39 -> 31, of which waited for: 17 -> 10; matrix products, arithmetic and copies ran while one was open for 3% -> 2% of each run, Pallas kernels for 14% -> 14%
where the time goes in v1:
time: 126 us; the launch traced here: 124 us
  starting transfers between devices  42.8 us (34%)
  Pallas kernels  41.8 us (33%)
  waiting for transfers between devices  34.2 us (27%)
  local copies, waits for them, and re-layouts  2.84 us (2%)
  other arithmetic  1.43 us (1%)
    pallas_call x2, Pallas kernels, call_attend(): pl.pallas_call(functools.partial(attend, bool(sofar)), grid=(1,), in_spec...  27.4 us
    ppermute x14, waiting for transfers between devices, by_part(): return lax.ppermute(value, ('seq', 'head'), pairs)  23.2 us
    ppermute x17, starting transfers between devices, by_seq(): lax.ppermute(value, 'seq', [(s, move(s // 2, s % 2)) for s in range(SHARD...  22.4 us
    ppermute x14, starting transfers between devices, by_part(): return lax.ppermute(value, ('seq', 'head'), pairs)  20.4 us
    ppermute x17, waiting for transfers between devices, by_seq(): lax.ppermute(value, 'seq', [(s, move(s // 2, s % 2)) for s in range(SHARD...  11 us
    pallas_call x1, Pallas kernels, call_join_outputs(): pl.pallas_call(functools.partial(join_outputs, JOIN_TOK), grid=(TOK // JO...  6.18 us
    pallas_call x1, Pallas kernels, call_split_queries(): pl.pallas_call(functools.partial(split_queries, tokens), grid=(steps,), i...  4.54 us
    pallas_call x1, Pallas kernels, call_split_pools(): pl.pallas_call(split_pools, grid=(TOK // POOL_TOK,), in_specs=[SMEM, rows...  3.66 us
  transfers between devices with their start and end apart: 31, of which 10 were waited for; matrix products, arithmetic and copies ran while one was open for 2% of the time, Pallas kernels for 14%

profile of v1, /device:TPU:1, one launch (start us, length us, event | category | flops | bytes accessed | tf_op | source)
XLA Modules:
  0.0 124.0 jit_solution(11635146581909241609)
XLA Ops:
  0.6 0.7 pad_add_fusion.1.place
  1.3 4.5 %split_queries.1 = (bf16[2,512,128]{2,1,0:T(8,128)(2,1)}, bf16[2,512,128]{2,1,0:T(8,128)(2,1)}, bf16[2,512,128]{2,1,0:T(8,128)(2,1)}, bf16[2,512,128]{2,1,0:T(8,...) custom-call(s32[3]{0:T(128)} %pad_add_fusion.1.place, ...), custom_call_target="tpu_custom_call" | custom-call | tf_op jit(solution)/shard_map/split_queries/pallas_call | solution.py:258
  5.9 2.1 %collective-permute-start.19 = (bf16[2,512,128]{2,1,0:T(8,128)(2,1)}, bf16[2,512,128]{2,1,0:T(8,128)(2,1)}, u32[]{:S(2)}, u32[]{:S(2)}) collective-permute-start(bf16[2,512,128]{2,1,0:T(8,128)(2,1)} %get-tuple-element.30), channel_id=1, source_target_pairs={{0,4},{4,8},{8,12},{12,0},{16,20},{20,24},{24,28},{28,16},{32,36},... | collective-permute-start | bytes 786440 | tf_op jit(solution)/shard_map/ppermute | solution.py:319
  8.0 2.1 %collective-permute-start.20 = (bf16[2,512,128]{2,1,0:T(8,128)(2,1)}, bf16[2,512,128]{2,1,0:T(8,128)(2,1)S(1)}, u32[]{:S(2)}, u32[]{:S(2)}) collective-permute-start(bf16[2,512,128]{2,1,0:T(8,128)(2,1)} %get-tuple-element.31), channel_id=1, source_target_pairs={{0,20},{4,24},{8,28},{12,16},{16,4},{20,8},{24,12},{28,0},{32,52},... | collective-permute-start | bytes 786440 | tf_op jit(solution)/shard_map/ppermute | solution.py:319
  10.0 3.7 %split_pools.1 = (bf16[1040,128]{1,0:T(8,128)(2,1)}, bf16[1040,128]{1,0:T(8,128)(2,1)}) custom-call(s32[3]{0:T(128)} %pad_add_fusion.1.place, bf16[4096,128]{1,0:T(8,128)(2,1)} %bitcast.18, bf16[4096,128]{1,0:T(8,128)(2,1)} %bitcast.19, bf16[64,128]{1,0:T(8,128)(2,1)} %bitcast.20), custom_call_target="tpu_custom_call" | custom-call | tf_op jit(solution)/shard_map/split_pools/pallas_call | solution.py:245
  13.7 5.0 %collective-permute-start.3 = (bf16[1040,128]{1,0:T(8,128)(2,1)}, bf16[1040,128]{1,0:T(8,128)(2,1)S(1)}, u32[]{:S(2)}, u32[]{:S(2)}) collective-permute-start(bf16[1040,128]{1,0:T(8,128)(2,1)} %get-tuple-element.25), channel_id=1, source_target_pairs={{0,240},{16,224},{32,16},{48,0},{64,48},{80,32},{96,80},{112,64},{... | collective-permute-start | bytes 798728 | tf_op jit(solution)/shard_map/ppermute | solution.py:303
  18.7 0.8 constant_dynamic-slice_fusion.1
  19.6 1.0 collective-permute-start
  20.6 0.8 collective-permute-done
  21.4 0.0 collective-permute-start.13
  21.4 0.0 collective-permute-done.19.refs_16_
  21.4 3.0 %collective-permute-start.2 = (bf16[1040,128]{1,0:T(8,128)(2,1)}, bf16[1040,128]{1,0:T(8,128)(2,1)S(1)}, u32[]{:S(2)}, u32[]{:S(2)}) collective-permute-start(bf16[1040,128]{1,0:T(8,128)(2,1)} %get-tuple-element.24.refs_0_), channel_id=1, source_target_pairs={{0,224},{16,240},{32,0},{48,16},{64,32},{80,48},{96,64},{112,80},{... | collective-permute-start | bytes 798728 | tf_op jit(solution)/shard_map/ppermute | solution.py:303
  24.4 1.5 %collective-permute-start.21 = (bf16[2,512,128]{2,1,0:T(8,128)(2,1)S(1)}, bf16[2,512,128]{2,1,0:T(8,128)(2,1)S(1)}, u32[]{:S(2)}, u32[]{:S(2)}) collective-permute-start(bf16[2,512,128]{2,1,0:T(8,128)(2,1)S(1)} %copy-done.27), channel_id=1, source_target_pairs={{0,8},{4,12},{8,0},{12,4},{16,24},{20,28},{24,16},{28,20},{32,40},... | collective-permute-start | bytes 786440 | tf_op jit(solution)/shard_map/ppermute | solution.py:319
  25.9 0.0 collective-permute-done.3.refs_3_
  25.9 3.4 %collective-permute-start.5 = (bf16[1040,128]{1,0:T(8,128)(2,1)S(1)}, bf16[1040,128]{1,0:T(8,128)(2,1)S(1)}, u32[]{:S(2)}, u32[]{:S(2)}) collective-permute-start(bf16[1040,128]{1,0:T(8,128)(2,1)S(1)} %collective-permute-done.3.refs_3_), channel_id=1, source_target_pairs={{0,224},{16,240},{32,0},{48,16},{64,32},{80,48},{96,64},{112,80},{... | collective-permute-start | bytes 798728 | tf_op jit(solution)/shard_map/ppermute | solution.py:303
  29.3 0.0 collective-permute-done.8.refs_14_
  29.3 0.0 collective-permute-start.9
  29.3 5.6 %collective-permute-done.13.refs_15_ = bf16[1040,128]{1,0:T(8,128)(2,1)S(1)} collective-permute-done((bf16[1040,128]{1,0:T(8,128)(2,1)}, bf16[1040,128]{1,0:T(8,128)(2,1)S(1)}, u32[]{:S(2)}, u32[]{:S(2)}) %collective-permute-start.13) | collective-permute-done | bytes 266272 | tf_op jit(solution)/shard_map/ppermute | solution.py:303
  34.9 0.0 collective-permute-start.14
  34.9 0.0 collective-permute-done.2.refs_2_
  35.0 2.7 %collective-permute-start.4 = (bf16[1040,128]{1,0:T(8,128)(2,1)S(1)}, bf16[1040,128]{1,0:T(8,128)(2,1)S(1)}, u32[]{:S(2)}, u32[]{:S(2)}) collective-permute-start(bf16[1040,128]{1,0:T(8,128)(2,1)S(1)} %collective-permute-done.2.refs_2_), channel_id=1, source_target_pairs={{0,224},{16,240},{32,0},{48,16},{64,32},{80,48},{96,64},{112,80},{... | collective-permute-start | bytes 798728 | tf_op jit(solution)/shard_map/ppermute | solution.py:303
  37.6 0.0 collective-permute-done.21.refs_18_
  37.6 1.0 collective-permute-start.22
  38.6 0.0 collective-permute-done.5.refs_5_
  38.6 0.6 collective-permute-start.7
  39.2 0.9 collective-permute-start.10
  40.1 6.1 %collective-permute-done.22.refs_19_ = bf16[2,512,128]{2,1,0:T(8,128)(2,1)S(1)} collective-permute-done((bf16[2,512,128]{2,1,0:T(8,128)(2,1)S(1)}, bf16[2,512,128]{2,1,0:T(8,128)(2,1)S(1)}, u32[]{:S(2)}, u32[]{:S(2)}) %collective-permute-start.22) | collective-permute-done | bytes 262176 | tf_op jit(solution)/shard_map/ppermute | solution.py:319
  46.1 0.0 collective-permute-start.1
  46.2 0.0 collective-permute-done.14.refs_13_
  46.2 0.3 collective-permute-start.15
  46.4 0.0 collective-permute-done.4.refs_4_
  46.5 2.6 %collective-permute-start.6 = (bf16[1040,128]{1,0:T(8,128)(2,1)S(1)}, bf16[1040,128]{1,0:T(8,128)(2,1)S(1)}, u32[]{:S(2)}, u32[]{:S(2)}) collective-permute-start(bf16[1040,128]{1,0:T(8,128)(2,1)S(1)} %collective-permute-done.4.refs_4_), channel_id=1, source_target_pairs={{0,224},{16,240},{32,0},{48,16},{64,32},{80,48},{96,64},{112,80},{... | collective-permute-start | bytes 798728 | tf_op jit(solution)/shard_map/ppermute | solution.py:303
  49.1 2.6 %collective-permute-start.12 = (bf16[1040,128]{1,0:T(8,128)(2,1)S(1)}, bf16[1040,128]{1,0:T(8,128)(2,1)}, u32[]{:S(2)}, u32[]{:S(2)}) collective-permute-start(bf16[1040,128]{1,0:T(8,128)(2,1)S(1)} %collective-permute-done.7.refs_7_), channel_id=1, source_target_pairs={{0,224},{16,240},{32,0},{48,16},{64,32},{80,48},{96,64},{112,80},{... | collective-permute-start | bytes 798728 | tf_op jit(solution)/shard_map/ppermute | solution.py:303
  51.7 0.0 collective-permute-done.1.refs_1_
  51.7 1.5 %collective-permute-start.16 = (bf16[2,512,128]{2,1,0:T(8,128)(2,1)}, bf16[2,512,128]{2,1,0:T(8,128)(2,1)}, u32[]{:S(2)}, u32[]{:S(2)}) collective-permute-start(bf16[2,512,128]{2,1,0:T(8,128)(2,1)} %get-tuple-element.26), channel_id=1, source_target_pairs={{0,12},{4,0},{8,4},{12,8},{16,28},{20,16},{24,20},{28,24},{32,44},... | collective-permute-start | bytes 786440 | tf_op jit(solution)/shard_map/ppermute | solution.py:319
  53.3 2.8 %collective-permute-done.15.refs_11_ = bf16[1040,128]{1,0:T(8,128)(2,1)S(1)} collective-permute-done((bf16[1040,128]{1,0:T(8,128)(2,1)S(1)}, bf16[1040,128]{1,0:T(8,128)(2,1)S(1)}, u32[]{:S(2)}, u32[]{:S(2)}) %collective-permute-start.15) | collective-permute-done | bytes 266272 | tf_op jit(solution)/shard_map/ppermute | solution.py:303
  56.1 3.3 %collective-permute-start.17 = (bf16[2,512,128]{2,1,0:T(8,128)(2,1)}, bf16[2,512,128]{2,1,0:T(8,128)(2,1)}, u32[]{:S(2)}, u32[]{:S(2)}) collective-permute-start(bf16[2,512,128]{2,1,0:T(8,128)(2,1)} %get-tuple-element.27), channel_id=1, source_target_pairs={{0,28},{4,16},{8,20},{12,24},{16,12},{20,0},{24,4},{28,8},{32,60},... | collective-permute-start | bytes 786440 | tf_op jit(solution)/shard_map/ppermute | solution.py:319
  59.4 0.0 collective-permute-done.6.refs_6_
  59.4 0.1 collective-permute-start.18
  59.5 0.6 reshape.89.picks
  60.2 1.7 %collective-permute-done.11.refs_8_ = bf16[1040,128]{1,0:T(8,128)(2,1)} collective-permute-done((bf16[1040,128]{1,0:T(8,128)(2,1)S(1)}, bf16[1040,128]{1,0:T(8,128)(2,1)}, u32[]{:S(2)}, u32[]{:S(2)}) %collective-permute-start.11) | collective-permute-done | bytes 266272 | tf_op jit(solution)/shard_map/ppermute | solution.py:303
  62.0 13.6 %attend.2 = (bf16[2,512,128]{2,1,0:T(8,128)(2,1)}, bf16[2,512,128]{2,1,0:T(8,128)(2,1)}, bf16[2,512,128]{2,1,0:T(8,128)(2,1)}, bf16[2,512,128]{2,1,0:T(8,128)(2,1)}, f32[8,128]{1,0:T(8,128)}, /*index=5*/f32[8,128]{1,0:T(8,128)}) custom-call(s32[3]{0:T(128)} %pad_add_fusion.1.place, s32[256]{0:T(256)} %reshape.89.picks, ...), custom_call_target="tpu_custom_call" | custom-call | tf_op jit(solution)/shard_map/attend/pallas_call | solution.py:271
  75.6 0.0 collective-permute-done.17.refs_17_
  75.6 0.0 collective-permute-done.18.refs_19_
  75.7 13.8 %attend.3 = (bf16[2,512,128]{2,1,0:T(8,128)(2,1)}, bf16[2,512,128]{2,1,0:T(8,128)(2,1)}, bf16[2,512,128]{2,1,0:T(8,128)(2,1)}, bf16[2,512,128]{2,1,0:T(8,128)(2,1)}, f32[8,128]{1,0:T(8,128)}, /*index=5*/f32[8,128]{1,0:T(8,128)}) custom-call(s32[3]{0:T(128)} %pad_add_fusion.1.place, s32[256]{0:T(256)} %reshape.89.picks, ...), custom_call_target="tpu_custom_call" | custom-call | tf_op jit(solution)/shard_map/attend/pallas_call | solution.py:271
  89.5 1.4 %collective-permute-start.24 = (bf16[2,512,128]{2,1,0:T(8,128)(2,1)}, bf16[2,512,128]{2,1,0:T(8,128)(2,1)S(1)}, u32[]{:S(2)}, u32[]{:S(2)}) collective-permute-start(bf16[2,512,128]{2,1,0:T(8,128)(2,1)} %get-tuple-element.39), channel_id=1, source_target_pairs={{16,0},{20,4},{24,8},{28,12},{0,16},{4,20},{8,24},{12,28},{48,32},... | collective-permute-start | bytes 786440 | tf_op jit(solution)/shard_map/ppermute | solution.py:319
  90.8 0.9 collective-permute-start.29
  91.8 0.4 collective-permute-start.23
  92.2 0.6 collective-permute-start.30
  92.7 2.1 %collective-permute-start.25 = (bf16[2,512,128]{2,1,0:T(8,128)(2,1)S(1)}, bf16[2,512,128]{2,1,0:T(8,128)(2,1)S(1)}, u32[]{:S(2)}, u32[]{:S(2)}) collective-permute-start(bf16[2,512,128]{2,1,0:T(8,128)(2,1)S(1)} %copy-done.28), channel_id=1, source_target_pairs={{4,0},{8,4},{12,8},{0,12},{20,16},{24,20},{28,24},{16,28},{36,32},... | collective-permute-start | bytes 786440 | tf_op jit(solution)/shard_map/ppermute | solution.py:319
  94.9 0.0 collective-permute-done.23
  94.9 1.1 collective-permute-start.26
  95.9 0.0 collective-permute-done.24.refs_1_
  95.9 0.7 collective-permute-start.27
  96.6 3.4 %collective-permute-done.29.refs_6_ = bf16[2,512,128]{2,1,0:T(8,128)(2,1)S(1)} collective-permute-done((bf16[2,512,128]{2,1,0:T(8,128)(2,1)}, bf16[2,512,128]{2,1,0:T(8,128)(2,1)S(1)}, u32[]{:S(2)}, u32[]{:S(2)}) %collective-permute-start.29) | collective-permute-done | bytes 262176 | tf_op jit(solution)/shard_map/ppermute | solution.py:319
  100.0 2.0 %collective-permute-start.28 = (bf16[2,512,128]{2,1,0:T(8,128)(2,1)S(1)}, bf16[2,512,128]{2,1,0:T(8,128)(2,1)S(1)}, u32[]{:S(2)}, u32[]{:S(2)}) collective-permute-start(bf16[2,512,128]{2,1,0:T(8,128)(2,1)S(1)} %copy-done.24), channel_id=1, source_target_pairs={{24,0},{28,4},{16,8},{20,12},{8,16},{12,20},{0,24},{4,28},{56,32},... | collective-permute-start | bytes 786440 | tf_op jit(solution)/shard_map/ppermute | solution.py:319
  102.0 0.8 maximum_select_fusion
  102.8 0.6 copy.9
  103.4 3.4 %collective-permute-done.30.refs_7_ = bf16[2,512,128]{2,1,0:T(8,128)(2,1)S(1)} collective-permute-done((bf16[2,512,128]{2,1,0:T(8,128)(2,1)}, bf16[2,512,128]{2,1,0:T(8,128)(2,1)S(1)}, u32[]{:S(2)}, u32[]{:S(2)}) %collective-permute-start.30) | collective-permute-done | bytes 262176 | tf_op jit(solution)/shard_map/ppermute | solution.py:319
  106.8 0.7 collective-permute-done.26.refs_3_
  107.5 3.7 %collective-permute-done.27.refs_4_ = bf16[2,512,128]{2,1,0:T(8,128)(2,1)S(1)} collective-permute-done((bf16[2,512,128]{2,1,0:T(8,128)(2,1)S(1)}, bf16[2,512,128]{2,1,0:T(8,128)(2,1)S(1)}, u32[]{:S(2)}, u32[]{:S(2)}) %collective-permute-start.27) | collective-permute-done | bytes 262176 | tf_op jit(solution)/shard_map/ppermute | solution.py:319
  111.2 5.9 %collective-permute-done.28.refs_5_ = bf16[2,512,128]{2,1,0:T(8,128)(2,1)S(1)} collective-permute-done((bf16[2,512,128]{2,1,0:T(8,128)(2,1)S(1)}, bf16[2,512,128]{2,1,0:T(8,128)(2,1)S(1)}, u32[]{:S(2)}, u32[]{:S(2)}) %collective-permute-start.28) | collective-permute-done | bytes 262176 | tf_op jit(solution)/shard_map/ppermute | solution.py:319
  117.2 0.7 copy-done.22
  117.9 6.2 %join_outputs.1 = bf16[8192,128]{1,0:T(8,128)(2,1)} custom-call(s32[3]{0:T(128)} %pad_add_fusion.1.place, bf16[2,512,128]{2,1,0:T(8,128)(2,1)} %get-tuple-element.38.refs_0_, bf16[2,512,128]{2,1,0:T(8,128)(2,1)} %copy-done.16, bf16[2,512,128]{2,1,0:T(8,128)(2,1)} %copy-done.19, bf16[2,512,128]{2,1,0:T(8,128)(2,1)} %copy-done.20, ...), custom_call_target="tpu_custom_call" | custom-call | tf_op jit(solution)/shard_map/join_outputs/pallas_call | solution.py:292
  (67 shorter events, 0.1 us)
Async XLA Ops:
  5.9 18.5 %copy-start.27 = (bf16[2,512,128]{2,1,0:T(8,128)(2,1)S(1)}, bf16[2,512,128]{2,1,0:T(8,128)(2,1)}, u32[]{:S(2)}) copy-start(bf16[2,512,128]{2,1,0:T(8,128)(2,1)} %get-tuple-element.32) | copy-start | bytes 786436
  5.9 31.8 %copy-start.23 = (bf16[2,512,128]{2,1,0:T(8,128)(2,1)S(1)}, bf16[2,512,128]{2,1,0:T(8,128)(2,1)}, u32[]{:S(2)}) copy-start(bf16[2,512,128]{2,1,0:T(8,128)(2,1)} %get-tuple-element.33) | copy-start | bytes 786436
  5.9 15.6 %collective-permute-start.19 = (bf16[2,512,128]{2,1,0:T(8,128)(2,1)}, bf16[2,512,128]{2,1,0:T(8,128)(2,1)}, u32[]{:S(2)}, u32[]{:S(2)}) collective-permute-start(bf16[2,512,128]{2,1,0:T(8,128)(2,1)} %get-tuple-element.30), channel_id=1, source_target_pairs={{0,4},{4,8},{8,12},{12,0},{16,20},{20,24},{24,28},{28,16},{32,36},... | collective-permute-start | bytes 786440 | tf_op jit(solution)/shard_map/ppermute | solution.py:319
  8.0 16.4 %collective-permute-start.20 = (bf16[2,512,128]{2,1,0:T(8,128)(2,1)}, bf16[2,512,128]{2,1,0:T(8,128)(2,1)S(1)}, u32[]{:S(2)}, u32[]{:S(2)}) collective-permute-start(bf16[2,512,128]{2,1,0:T(8,128)(2,1)} %get-tuple-element.31), channel_id=1, source_target_pairs={{0,20},{4,24},{8,28},{12,16},{16,4},{20,8},{24,12},{28,0},{32,52},... | collective-permute-start | bytes 786440 | tf_op jit(solution)/shard_map/ppermute | solution.py:319
  13.7 12.2 %collective-permute-start.3 = (bf16[1040,128]{1,0:T(8,128)(2,1)}, bf16[1040,128]{1,0:T(8,128)(2,1)S(1)}, u32[]{:S(2)}, u32[]{:S(2)}) collective-permute-start(bf16[1040,128]{1,0:T(8,128)(2,1)} %get-tuple-element.25), channel_id=1, source_target_pairs={{0,240},{16,224},{32,16},{48,0},{64,48},{80,32},{96,80},{112,64},{... | collective-permute-start | bytes 798728 | tf_op jit(solution)/shard_map/ppermute | solution.py:303
  18.7 10.6 %collective-permute-start.8 = (bf16[1040,128]{1,0:T(8,128)(2,1)}, bf16[1040,128]{1,0:T(8,128)(2,1)S(1)}, u32[]{:S(2)}, u32[]{:S(2)}) collective-permute-start(bf16[1040,128]{1,0:T(8,128)(2,1)} %get-tuple-element.24.refs_0_), channel_id=1, source_target_pairs={{0,32},{16,48},{32,64},{48,80},{64,96},{80,112},{96,128},{112,144}... | collective-permute-start | bytes 798728 | tf_op jit(solution)/shard_map/ppermute | solution.py:303
  19.6 1.9 %collective-permute-start = (s32[8,16]{1,0:T(8,128)S(1)}, s32[8,16]{1,0:T(8,128)S(1)}, u32[]{:S(2)}, u32[]{:S(2)}) collective-permute-start(s32[8,16]{1,0:T(8,128)S(1)} %bitcast.22), channel_id=1, source_target_pairs={{0,16},{16,0},{32,48},{48,32},{64,80},{80,64},{96,112},{112,96},{1... | collective-permute-start | bytes 1544 | tf_op jit(solution)/shard_map/ppermute | solution.py:303
  21.4 13.5 %collective-permute-start.13 = (bf16[1040,128]{1,0:T(8,128)(2,1)}, bf16[1040,128]{1,0:T(8,128)(2,1)S(1)}, u32[]{:S(2)}, u32[]{:S(2)}) collective-permute-start(bf16[1040,128]{1,0:T(8,128)(2,1)} %get-tuple-element.25), channel_id=1, source_target_pairs={{0,48},{16,32},{32,80},{48,64},{64,112},{80,96},{96,144},{112,128}... | collective-permute-start | bytes 798728 | tf_op jit(solution)/shard_map/ppermute | solution.py:303
  21.4 13.5 %collective-permute-start.2 = (bf16[1040,128]{1,0:T(8,128)(2,1)}, bf16[1040,128]{1,0:T(8,128)(2,1)S(1)}, u32[]{:S(2)}, u32[]{:S(2)}) collective-permute-start(bf16[1040,128]{1,0:T(8,128)(2,1)} %get-tuple-element.24.refs_0_), channel_id=1, source_target_pairs={{0,224},{16,240},{32,0},{48,16},{64,32},{80,48},{96,64},{112,80},{... | collective-permute-start | bytes 798728 | tf_op jit(solution)/shard_map/ppermute | solution.py:303
  24.4 1.5 %copy-start.13 = (bf16[2,512,128]{2,1,0:T(8,128)(2,1)}, bf16[2,512,128]{2,1,0:T(8,128)(2,1)S(1)}, u32[]{:S(2)}) copy-start(bf16[2,512,128]{2,1,0:T(8,128)(2,1)S(1)} %collective-permute-done.20.refs_17_) | copy-start | bytes 786436
  24.4 13.2 %collective-permute-start.21 = (bf16[2,512,128]{2,1,0:T(8,128)(2,1)S(1)}, bf16[2,512,128]{2,1,0:T(8,128)(2,1)S(1)}, u32[]{:S(2)}, u32[]{:S(2)}) collective-permute-start(bf16[2,512,128]{2,1,0:T(8,128)(2,1)S(1)} %copy-done.27), channel_id=1, source_target_pairs={{0,8},{4,12},{8,0},{12,4},{16,24},{20,28},{24,16},{28,20},{32,40},... | collective-permute-start | bytes 786440 | tf_op jit(solution)/shard_map/ppermute | solution.py:319
  25.9 36.0 %copy-start = (bf16[1040,128]{1,0:T(8,128)(2,1)}, bf16[1040,128]{1,0:T(8,128)(2,1)S(1)}, u32[]{:S(2)}) copy-start(bf16[1040,128]{1,0:T(8,128)(2,1)S(1)} %collective-permute-done.3.refs_3_) | copy-start | bytes 798724
  25.9 12.7 %collective-permute-start.5 = (bf16[1040,128]{1,0:T(8,128)(2,1)S(1)}, bf16[1040,128]{1,0:T(8,128)(2,1)S(1)}, u32[]{:S(2)}, u32[]{:S(2)}) collective-permute-start(bf16[1040,128]{1,0:T(8,128)(2,1)S(1)} %collective-permute-done.3.refs_3_), channel_id=1, source_target_pairs={{0,224},{16,240},{32,0},{48,16},{64,32},{80,48},{96,64},{112,80},{... | collective-permute-start | bytes 798728 | tf_op jit(solution)/shard_map/ppermute | solution.py:303
  29.3 32.6 %copy-start.1 = (bf16[1040,128]{1,0:T(8,128)(2,1)}, bf16[1040,128]{1,0:T(8,128)(2,1)S(1)}, u32[]{:S(2)}) copy-start(bf16[1040,128]{1,0:T(8,128)(2,1)S(1)} %collective-permute-done.8.refs_14_) | copy-start | bytes 798724
  29.3 9.9 %collective-permute-start.9 = (bf16[1040,128]{1,0:T(8,128)(2,1)S(1)}, bf16[1040,128]{1,0:T(8,128)(2,1)S(1)}, u32[]{:S(2)}, u32[]{:S(2)}) collective-permute-start(bf16[1040,128]{1,0:T(8,128)(2,1)S(1)} %collective-permute-done.8.refs_14_), channel_id=1, source_target_pairs={{0,32},{16,48},{32,64},{48,80},{64,96},{80,112},{96,128},{112,144}... | collective-permute-start | bytes 798728 | tf_op jit(solution)/shard_map/ppermute | solution.py:303
  34.9 26.9 %copy-start.2 = (bf16[1040,128]{1,0:T(8,128)(2,1)}, bf16[1040,128]{1,0:T(8,128)(2,1)S(1)}, u32[]{:S(2)}) copy-start(bf16[1040,128]{1,0:T(8,128)(2,1)S(1)} %collective-permute-done.13.refs_15_) | copy-start | bytes 798724
  34.9 11.2 %collective-permute-start.14 = (bf16[1040,128]{1,0:T(8,128)(2,1)S(1)}, bf16[1040,128]{1,0:T(8,128)(2,1)S(1)}, u32[]{:S(2)}, u32[]{:S(2)}) collective-permute-start(bf16[1040,128]{1,0:T(8,128)(2,1)S(1)} %collective-permute-done.13.refs_15_), channel_id=1, source_target_pairs={{0,32},{16,48},{32,64},{48,80},{64,96},{80,112},{96,128},{112,144}... | collective-permute-start | bytes 798728 | tf_op jit(solution)/shard_map/ppermute | solution.py:303
  35.0 26.9 %copy-start.3 = (bf16[1040,128]{1,0:T(8,128)(2,1)}, bf16[1040,128]{1,0:T(8,128)(2,1)S(1)}, u32[]{:S(2)}) copy-start(bf16[1040,128]{1,0:T(8,128)(2,1)S(1)} %collective-permute-done.2.refs_2_) | copy-start | bytes 798724
  35.0 11.5 %collective-permute-start.4 = (bf16[1040,128]{1,0:T(8,128)(2,1)S(1)}, bf16[1040,128]{1,0:T(8,128)(2,1)S(1)}, u32[]{:S(2)}, u32[]{:S(2)}) collective-permute-start(bf16[1040,128]{1,0:T(8,128)(2,1)S(1)} %collective-permute-done.2.refs_2_), channel_id=1, source_target_pairs={{0,224},{16,240},{32,0},{48,16},{64,32},{80,48},{96,64},{112,80},{... | collective-permute-start | bytes 798728 | tf_op jit(solution)/shard_map/ppermute | solution.py:303
  37.6 21.8 %copy-start.14 = (bf16[2,512,128]{2,1,0:T(8,128)(2,1)}, bf16[2,512,128]{2,1,0:T(8,128)(2,1)S(1)}, u32[]{:S(2)}) copy-start(bf16[2,512,128]{2,1,0:T(8,128)(2,1)S(1)} %collective-permute-done.21.refs_18_) | copy-start | bytes 786436
  37.6 8.5 %collective-permute-start.22 = (bf16[2,512,128]{2,1,0:T(8,128)(2,1)S(1)}, bf16[2,512,128]{2,1,0:T(8,128)(2,1)S(1)}, u32[]{:S(2)}, u32[]{:S(2)}) collective-permute-start(bf16[2,512,128]{2,1,0:T(8,128)(2,1)S(1)} %copy-done.23), channel_id=1, source_target_pairs={{0,24},{4,28},{8,16},{12,20},{16,8},{20,12},{24,0},{28,4},{32,56},... | collective-permute-start | bytes 786440 | tf_op jit(solution)/shard_map/ppermute | solution.py:319
  38.6 23.3 %copy-start.4 = (bf16[1040,128]{1,0:T(8,128)(2,1)}, bf16[1040,128]{1,0:T(8,128)(2,1)S(1)}, u32[]{:S(2)}) copy-start(bf16[1040,128]{1,0:T(8,128)(2,1)S(1)} %collective-permute-done.5.refs_5_) | copy-start | bytes 798724
  38.6 10.5 %collective-permute-start.7 = (bf16[1040,128]{1,0:T(8,128)(2,1)S(1)}, bf16[1040,128]{1,0:T(8,128)(2,1)S(1)}, u32[]{:S(2)}, u32[]{:S(2)}) collective-permute-start(bf16[1040,128]{1,0:T(8,128)(2,1)S(1)} %collective-permute-done.5.refs_5_), channel_id=1, source_target_pairs={{0,224},{16,240},{32,0},{48,16},{64,32},{80,48},{96,64},{112,80},{... | collective-permute-start | bytes 798728 | tf_op jit(solution)/shard_map/ppermute | solution.py:303
  39.2 22.7 %copy-start.5 = (bf16[1040,128]{1,0:T(8,128)(2,1)}, bf16[1040,128]{1,0:T(8,128)(2,1)S(1)}, u32[]{:S(2)}) copy-start(bf16[1040,128]{1,0:T(8,128)(2,1)S(1)} %collective-permute-done.9.refs_12_) | copy-start | bytes 798724
  39.2 12.5 %collective-permute-start.10 = (bf16[1040,128]{1,0:T(8,128)(2,1)S(1)}, bf16[1040,128]{1,0:T(8,128)(2,1)S(1)}, u32[]{:S(2)}, u32[]{:S(2)}) collective-permute-start(bf16[1040,128]{1,0:T(8,128)(2,1)S(1)} %collective-permute-done.9.refs_12_), channel_id=1, source_target_pairs={{0,32},{16,48},{32,64},{48,80},{64,96},{80,112},{96,128},{112,144}... | collective-permute-start | bytes 798728 | tf_op jit(solution)/shard_map/ppermute | solution.py:303
  46.1 13.3 %copy-start.15 = (bf16[2,512,128]{2,1,0:T(8,128)(2,1)}, bf16[2,512,128]{2,1,0:T(8,128)(2,1)S(1)}, u32[]{:S(2)}) copy-start(bf16[2,512,128]{2,1,0:T(8,128)(2,1)S(1)} %collective-permute-done.22.refs_19_) | copy-start | bytes 786436
  46.1 5.5 %collective-permute-start.1 = (bf16[1040,128]{1,0:T(8,128)(2,1)}, bf16[1040,128]{1,0:T(8,128)(2,1)S(1)}, u32[]{:S(2)}, u32[]{:S(2)}) collective-permute-start(bf16[1040,128]{1,0:T(8,128)(2,1)} %get-tuple-element.25), channel_id=1, source_target_pairs={{0,16},{16,0},{32,48},{48,32},{64,80},{80,64},{96,112},{112,96},{1... | collective-permute-start | bytes 798728 | tf_op jit(solution)/shard_map/ppermute | solution.py:303
  46.2 15.8 %copy-start.6 = (bf16[1040,128]{1,0:T(8,128)(2,1)}, bf16[1040,128]{1,0:T(8,128)(2,1)S(1)}, u32[]{:S(2)}) copy-start(bf16[1040,128]{1,0:T(8,128)(2,1)S(1)} %collective-permute-done.14.refs_13_) | copy-start | bytes 798724
  46.2 9.9 %collective-permute-start.15 = (bf16[1040,128]{1,0:T(8,128)(2,1)S(1)}, bf16[1040,128]{1,0:T(8,128)(2,1)S(1)}, u32[]{:S(2)}, u32[]{:S(2)}) collective-permute-start(bf16[1040,128]{1,0:T(8,128)(2,1)S(1)} %collective-permute-done.14.refs_13_), channel_id=1, source_target_pairs={{0,32},{16,48},{32,64},{48,80},{64,96},{80,112},{96,128},{112,144}... | collective-permute-start | bytes 798728 | tf_op jit(solution)/shard_map/ppermute | solution.py:303
  46.5 15.5 %copy-start.7 = (bf16[1040,128]{1,0:T(8,128)(2,1)}, bf16[1040,128]{1,0:T(8,128)(2,1)S(1)}, u32[]{:S(2)}) copy-start(bf16[1040,128]{1,0:T(8,128)(2,1)S(1)} %collective-permute-done.4.refs_4_) | copy-start | bytes 798724
  46.5 13.0 %collective-permute-start.6 = (bf16[1040,128]{1,0:T(8,128)(2,1)S(1)}, bf16[1040,128]{1,0:T(8,128)(2,1)S(1)}, u32[]{:S(2)}, u32[]{:S(2)}) collective-permute-start(bf16[1040,128]{1,0:T(8,128)(2,1)S(1)} %collective-permute-done.4.refs_4_), channel_id=1, source_target_pairs={{0,224},{16,240},{32,0},{48,16},{64,32},{80,48},{96,64},{112,80},{... | collective-permute-start | bytes 798728 | tf_op jit(solution)/shard_map/ppermute | solution.py:303
  49.1 12.8 %copy-start.8 = (bf16[1040,128]{1,0:T(8,128)(2,1)}, bf16[1040,128]{1,0:T(8,128)(2,1)S(1)}, u32[]{:S(2)}) copy-start(bf16[1040,128]{1,0:T(8,128)(2,1)S(1)} %collective-permute-done.7.refs_7_) | copy-start | bytes 798724
  49.1 11.1 %collective-permute-start.12 = (bf16[1040,128]{1,0:T(8,128)(2,1)S(1)}, bf16[1040,128]{1,0:T(8,128)(2,1)}, u32[]{:S(2)}, u32[]{:S(2)}) collective-permute-start(bf16[1040,128]{1,0:T(8,128)(2,1)S(1)} %collective-permute-done.7.refs_7_), channel_id=1, source_target_pairs={{0,224},{16,240},{32,0},{48,16},{64,32},{80,48},{96,64},{112,80},{... | collective-permute-start | bytes 798728 | tf_op jit(solution)/shard_map/ppermute | solution.py:303
  51.7 10.3 %copy-start.9 = (bf16[1040,128]{1,0:T(8,128)(2,1)}, bf16[1040,128]{1,0:T(8,128)(2,1)S(1)}, u32[]{:S(2)}) copy-start(bf16[1040,128]{1,0:T(8,128)(2,1)S(1)} %collective-permute-done.10.refs_10_) | copy-start | bytes 798724
  51.7 10.2 %collective-permute-start.11 = (bf16[1040,128]{1,0:T(8,128)(2,1)S(1)}, bf16[1040,128]{1,0:T(8,128)(2,1)}, u32[]{:S(2)}, u32[]{:S(2)}) collective-permute-start(bf16[1040,128]{1,0:T(8,128)(2,1)S(1)} %collective-permute-done.10.refs_10_), channel_id=1, source_target_pairs={{0,32},{16,48},{32,64},{48,80},{64,96},{80,112},{96,128},{112,144}... | collective-permute-start | bytes 798728 | tf_op jit(solution)/shard_map/ppermute | solution.py:303
  51.7 10.3 %copy-start.10 = (bf16[1040,128]{1,0:T(8,128)(2,1)}, bf16[1040,128]{1,0:T(8,128)(2,1)S(1)}, u32[]{:S(2)}) copy-start(bf16[1040,128]{1,0:T(8,128)(2,1)S(1)} %collective-permute-done.1.refs_1_) | copy-start | bytes 798724
  51.7 23.9 %collective-permute-start.16 = (bf16[2,512,128]{2,1,0:T(8,128)(2,1)}, bf16[2,512,128]{2,1,0:T(8,128)(2,1)}, u32[]{:S(2)}, u32[]{:S(2)}) collective-permute-start(bf16[2,512,128]{2,1,0:T(8,128)(2,1)} %get-tuple-element.26), channel_id=1, source_target_pairs={{0,12},{4,0},{8,4},{12,8},{16,28},{20,16},{24,20},{28,24},{32,44},... | collective-permute-start | bytes 786440 | tf_op jit(solution)/shard_map/ppermute | solution.py:319
  56.1 5.9 %copy-start.11 = (bf16[1040,128]{1,0:T(8,128)(2,1)}, bf16[1040,128]{1,0:T(8,128)(2,1)S(1)}, u32[]{:S(2)}) copy-start(bf16[1040,128]{1,0:T(8,128)(2,1)S(1)} %collective-permute-done.15.refs_11_) | copy-start | bytes 798724
  56.1 19.5 %collective-permute-start.17 = (bf16[2,512,128]{2,1,0:T(8,128)(2,1)}, bf16[2,512,128]{2,1,0:T(8,128)(2,1)}, u32[]{:S(2)}, u32[]{:S(2)}) collective-permute-start(bf16[2,512,128]{2,1,0:T(8,128)(2,1)} %get-tuple-element.27), channel_id=1, source_target_pairs={{0,28},{4,16},{8,20},{12,24},{16,12},{20,0},{24,4},{28,8},{32,60},... | collective-permute-start | bytes 786440 | tf_op jit(solution)/shard_map/ppermute | solution.py:319
  59.4 2.6 %copy-start.12 = (bf16[1040,128]{1,0:T(8,128)(2,1)}, bf16[1040,128]{1,0:T(8,128)(2,1)S(1)}, u32[]{:S(2)}) copy-start(bf16[1040,128]{1,0:T(8,128)(2,1)S(1)} %collective-permute-done.6.refs_6_) | copy-start | bytes 798724
  59.4 16.2 %collective-permute-start.18 = (bf16[2,512,128]{2,1,0:T(8,128)(2,1)}, bf16[2,512,128]{2,1,0:T(8,128)(2,1)}, u32[]{:S(2)}, u32[]{:S(2)}) collective-permute-start(bf16[2,512,128]{2,1,0:T(8,128)(2,1)} %get-tuple-element.29), channel_id=1, source_target_pairs={{0,16},{4,20},{8,24},{12,28},{16,0},{20,4},{24,8},{28,12},{32,48},... | collective-permute-start | bytes 786440 | tf_op jit(solution)/shard_map/ppermute | solution.py:319
  75.6 17.1 %copy-start.28 = (bf16[2,512,128]{2,1,0:T(8,128)(2,1)S(1)}, bf16[2,512,128]{2,1,0:T(8,128)(2,1)}, u32[]{:S(2)}) copy-start(bf16[2,512,128]{2,1,0:T(8,128)(2,1)} %get-tuple-element.40) | copy-start | bytes 786436
  75.6 19.2 %copy-start.26 = (bf16[2,512,128]{2,1,0:T(8,128)(2,1)S(1)}, bf16[2,512,128]{2,1,0:T(8,128)(2,1)}, u32[]{:S(2)}) copy-start(bf16[2,512,128]{2,1,0:T(8,128)(2,1)} %get-tuple-element.41) | copy-start | bytes 786436
  75.6 20.3 %copy-start.25 = (bf16[2,512,128]{2,1,0:T(8,128)(2,1)S(1)}, bf16[2,512,128]{2,1,0:T(8,128)(2,1)}, u32[]{:S(2)}) copy-start(bf16[2,512,128]{2,1,0:T(8,128)(2,1)} %get-tuple-element.42) | copy-start | bytes 786436
  75.7 24.4 %copy-start.24 = (bf16[2,512,128]{2,1,0:T(8,128)(2,1)S(1)}, bf16[2,512,128]{2,1,0:T(8,128)(2,1)}, u32[]{:S(2)}) copy-start(bf16[2,512,128]{2,1,0:T(8,128)(2,1)} %get-tuple-element.43) | copy-start | bytes 786436
  89.5 6.5 %collective-permute-start.24 = (bf16[2,512,128]{2,1,0:T(8,128)(2,1)}, bf16[2,512,128]{2,1,0:T(8,128)(2,1)S(1)}, u32[]{:S(2)}, u32[]{:S(2)}) collective-permute-start(bf16[2,512,128]{2,1,0:T(8,128)(2,1)} %get-tuple-element.39), channel_id=1, source_target_pairs={{16,0},{20,4},{24,8},{28,12},{0,16},{4,20},{8,24},{12,28},{48,32},... | collective-permute-start | bytes 786440 | tf_op jit(solution)/shard_map/ppermute | solution.py:319
  90.8 9.2 %collective-permute-start.29 = (bf16[2,512,128]{2,1,0:T(8,128)(2,1)}, bf16[2,512,128]{2,1,0:T(8,128)(2,1)S(1)}, u32[]{:S(2)}, u32[]{:S(2)}) collective-permute-start(bf16[2,512,128]{2,1,0:T(8,128)(2,1)} %get-tuple-element.44), channel_id=1, source_target_pairs={{12,0},{0,4},{4,8},{8,12},{28,16},{16,20},{20,24},{24,28},{44,32},... | collective-permute-start | bytes 786440 | tf_op jit(solution)/shard_map/ppermute | solution.py:319
  91.8 3.1 %collective-permute-start.23 = (f32[8,128]{1,0:T(8,128)}, f32[8,128]{1,0:T(8,128)S(1)}, u32[]{:S(2)}, u32[]{:S(2)}) collective-permute-start(f32[8,128]{1,0:T(8,128)} %get-tuple-element.37), channel_id=1, source_target_pairs={{0,16},{16,0},{32,48},{48,32},{64,80},{80,64},{96,112},{112,96},{1... | collective-permute-start | bytes 12296 | tf_op jit(solution)/shard_map/ppermute | solution.py:303
  92.2 14.6 %collective-permute-start.30 = (bf16[2,512,128]{2,1,0:T(8,128)(2,1)}, bf16[2,512,128]{2,1,0:T(8,128)(2,1)S(1)}, u32[]{:S(2)}, u32[]{:S(2)}) collective-permute-start(bf16[2,512,128]{2,1,0:T(8,128)(2,1)} %get-tuple-element.45), channel_id=1, source_target_pairs={{28,0},{16,4},{20,8},{24,12},{12,16},{0,20},{4,24},{8,28},{60,32},... | collective-permute-start | bytes 786440 | tf_op jit(solution)/shard_map/ppermute | solution.py:319
  92.7 14.0 %collective-permute-start.25 = (bf16[2,512,128]{2,1,0:T(8,128)(2,1)S(1)}, bf16[2,512,128]{2,1,0:T(8,128)(2,1)S(1)}, u32[]{:S(2)}, u32[]{:S(2)}) collective-permute-start(bf16[2,512,128]{2,1,0:T(8,128)(2,1)S(1)} %copy-done.28), channel_id=1, source_target_pairs={{4,0},{8,4},{12,8},{0,12},{20,16},{24,20},{28,24},{16,28},{36,32},... | collective-permute-start | bytes 786440 | tf_op jit(solution)/shard_map/ppermute | solution.py:319
  94.9 12.6 %collective-permute-start.26 = (bf16[2,512,128]{2,1,0:T(8,128)(2,1)S(1)}, bf16[2,512,128]{2,1,0:T(8,128)(2,1)S(1)}, u32[]{:S(2)}, u32[]{:S(2)}) collective-permute-start(bf16[2,512,128]{2,1,0:T(8,128)(2,1)S(1)} %copy-done.26), channel_id=1, source_target_pairs={{20,0},{24,4},{28,8},{16,12},{4,16},{8,20},{12,24},{0,28},{52,32},... | collective-permute-start | bytes 786440 | tf_op jit(solution)/shard_map/ppermute | solution.py:319
  95.9 21.2 %copy-start.16 = (bf16[2,512,128]{2,1,0:T(8,128)(2,1)}, bf16[2,512,128]{2,1,0:T(8,128)(2,1)S(1)}, u32[]{:S(2)}) copy-start(bf16[2,512,128]{2,1,0:T(8,128)(2,1)S(1)} %collective-permute-done.24.refs_1_) | copy-start | bytes 786436
  95.9 15.3 %collective-permute-start.27 = (bf16[2,512,128]{2,1,0:T(8,128)(2,1)S(1)}, bf16[2,512,128]{2,1,0:T(8,128)(2,1)S(1)}, u32[]{:S(2)}, u32[]{:S(2)}) collective-permute-start(bf16[2,512,128]{2,1,0:T(8,128)(2,1)S(1)} %copy-done.25), channel_id=1, source_target_pairs={{8,0},{12,4},{0,8},{4,12},{24,16},{28,20},{16,24},{20,28},{40,32},... | collective-permute-start | bytes 786440 | tf_op jit(solution)/shard_map/ppermute | solution.py:319
  100.0 17.1 %copy-start.17 = (bf16[2,512,128]{2,1,0:T(8,128)(2,1)}, bf16[2,512,128]{2,1,0:T(8,128)(2,1)S(1)}, u32[]{:S(2)}) copy-start(bf16[2,512,128]{2,1,0:T(8,128)(2,1)S(1)} %collective-permute-done.29.refs_6_) | copy-start | bytes 786436
  100.0 17.1 %collective-permute-start.28 = (bf16[2,512,128]{2,1,0:T(8,128)(2,1)S(1)}, bf16[2,512,128]{2,1,0:T(8,128)(2,1)S(1)}, u32[]{:S(2)}, u32[]{:S(2)}) collective-permute-start(bf16[2,512,128]{2,1,0:T(8,128)(2,1)S(1)} %copy-done.24), channel_id=1, source_target_pairs={{24,0},{28,4},{16,8},{20,12},{8,16},{12,20},{0,24},{4,28},{56,32},... | collective-permute-start | bytes 786440 | tf_op jit(solution)/shard_map/ppermute | solution.py:319
  106.8 10.4 %copy-start.18 = (bf16[2,512,128]{2,1,0:T(8,128)(2,1)}, bf16[2,512,128]{2,1,0:T(8,128)(2,1)S(1)}, u32[]{:S(2)}) copy-start(bf16[2,512,128]{2,1,0:T(8,128)(2,1)S(1)} %collective-permute-done.30.refs_7_) | copy-start | bytes 786436
  106.8 10.4 %copy-start.19 = (bf16[2,512,128]{2,1,0:T(8,128)(2,1)}, bf16[2,512,128]{2,1,0:T(8,128)(2,1)S(1)}, u32[]{:S(2)}) copy-start(bf16[2,512,128]{2,1,0:T(8,128)(2,1)S(1)} %collective-permute-done.25.refs_2_) | copy-start | bytes 786436
  107.5 9.7 %copy-start.20 = (bf16[2,512,128]{2,1,0:T(8,128)(2,1)}, bf16[2,512,128]{2,1,0:T(8,128)(2,1)S(1)}, u32[]{:S(2)}) copy-start(bf16[2,512,128]{2,1,0:T(8,128)(2,1)S(1)} %collective-permute-done.26.refs_3_) | copy-start | bytes 786436
  111.2 5.9 %copy-start.21 = (bf16[2,512,128]{2,1,0:T(8,128)(2,1)}, bf16[2,512,128]{2,1,0:T(8,128)(2,1)S(1)}, u32[]{:S(2)}) copy-start(bf16[2,512,128]{2,1,0:T(8,128)(2,1)S(1)} %collective-permute-done.27.refs_4_) | copy-start | bytes 786436
  117.1 0.7 copy-start.22

commit v2 on v1

--- a/solution.py
+++ b/solution.py
@@ -23,8 +23,8 @@
 COMP_PAD = 16
 PIECE = 2 * TOK + COMP_PAD
 PARTS = 8
-POOL_TOK = 128
-JOIN_TOK = 64
+POOL_TOK = 512
+JOIN_TOK = 256
 CHUNKS = ((1, 2), (3, 0))
 WIDE = 2
 KEYS = TOPN * BLOCK
@@ -116,22 +116,25 @@
         out[pl.ds(i * 512 + 256, 256), :] = got[:, DH:]
 
 
-def attend(follows, place, picks, *refs):
-    pieces = refs[: 2 * CHIPS]
-    refs = refs[2 * CHIPS :]
+def attend(follows, place, picks, owns, *refs):
     count = 2 * WIDE
-    queries, refs = refs[:count], refs[count:]
+    pieces, refs = refs[: 2 * CHIPS], refs[2 * CHIPS :]
+    given, refs = refs[:count], refs[count:]
     sofar, refs = (refs[:2], refs[2:]) if follows else (None, refs)
     outs, refs = refs[:count], refs[count:]
     pooled, refs = refs[:2], refs[2:]
-    pool, comp, mask, *rest, sems = refs
+    pool, queries, results, comp, mask, *rest, sems, ask_sems, out_sems = refs
     turned, scores, logits, tops = rest[0:2], rest[2:4], rest[4:6], rest[6:8]
     core, chip = place[1], place[2]
+    asks = [pltpu.make_async_copy(given[k], queries.at[k], ask_sems.at[k]) for k in range(count)]
+    for copy in asks:
+        copy.start()
     copies = []
     for k in range(CHIPS):
         for h in range(2):
             slot = 2 * ((chip + k) % CHIPS) + (core + h) % 2
-            copies.append(pltpu.make_async_copy(pieces[2 * k + h], pool.at[slot], sems.at[2 * k + h]))
+            rows = pl.ds(pl.multiple_of(slot * PIECE, COMP_PAD), PIECE)
+            copies.append(pltpu.make_async_copy(pieces[2 * k + h], pool.at[rows, :], sems.at[2 * k + h]))
     for copy in copies:
         copy.start()
     shape = (2 * BLOCK, DH)
@@ -143,10 +146,6 @@
         turned[half][pl.ds(DH, DH), :] = one_hot(iota(shape, 0) == iota(shape, 1) % BLOCK)
     shape = (NBLK, COMP_ROWS)
     take = one_hot(iota(shape, 1) == iota(shape, 0) // TILES * COMP_PAD + iota(shape, 0) % TILES)
-    for copy in copies:
-        copy.wait()
-    padded = jnp.concatenate([pool[s, pl.ds(2 * TOK, COMP_PAD), :] for s in range(SHARDS)], axis=0)
-    comp[...] = dot(take, padded).astype(jnp.bfloat16)
     block_row = iota((NBLK, ROWS), 0)
     ones = jnp.full((ONES, STEP_KEYS), 1.0, jnp.bfloat16)
 
@@ -156,38 +155,42 @@
     def number_of(local, half):
         return (2 * chip + (core + half) % 2) * TILES + local
 
-    def pick_of(local, half, b):
-        return picks[(half * TILES + local) * TOPN + b]
-
-    def block_of(n, offset):
-        return pool[n // TILES, pl.ds(pl.multiple_of(offset + n % TILES * BLOCK, BLOCK), BLOCK), :]
+    def block_of(local, half, b, offset):
+        start = picks[(half * TILES + local) * TOPN + b] + offset
+        return pool[pl.ds(pl.multiple_of(start, COMP_PAD), BLOCK), :]
+
+    def mask_of(local, half, b):
+        start = owns[(half * TILES + local) * TOPN + b]
+        return mask[pl.ds(pl.multiple_of(start, BLOCK), BLOCK), :]
 
     def turn(local, half):
         at = spot(local)
-        query = jnp.concatenate([queries[2 * w + half][j, at, :] for w in range(WIDE) for j in range(2)], axis=0)
+        query = jnp.concatenate([queries[2 * w + half, j, at, :] for w in range(WIDE) for j in range(2)], axis=0)
         turned[half][pl.ds(0, DH), :] = query.T
 
     def score(local, half, i):
-        number = number_of(local, half)
         keys = []
-        for b in range(STEP_BLOCKS):
-            n = pick_of(local, half, i * STEP_BLOCKS + b)
-            own = jnp.where(n == number, BLOCK, 0)
-            keys.append(jnp.concatenate([block_of(n, 0), mask[pl.ds(pl.multiple_of(own, BLOCK), BLOCK), :]], axis=1))
+        for b in range(i * STEP_BLOCKS, (i + 1) * STEP_BLOCKS):
+            keys.append(jnp.concatenate([block_of(local, half, b, 0), mask_of(local, half, b)], axis=1))
         some = comp[pl.ds(i * STEP_COMP, STEP_COMP), :]
         keys.append(jnp.concatenate([some, jnp.zeros_like(some)], axis=1))
         got = dot(jnp.concatenate(keys, axis=0), turned[half][...])
         near = got[:STEP_KEYS]
         scores[half][pl.ds(i * STEP_KEYS, STEP_KEYS), :] = near
         logits[half][pl.ds(i * STEP_COMP, STEP_COMP), :] = got[STEP_KEYS:]
-        top = jnp.max(near.reshape(STEP_KEYS // 8, 8, ROWS), axis=0)
-        tops[half][...] = top if i == 0 else jnp.maximum(tops[half][...], top)
+        return jnp.max(near.reshape(STEP_KEYS // 8, 8, ROWS), axis=0)
 
     def weigh(local, half, i, top):
         weight = jnp.exp2((scores[half][pl.ds(i * STEP_KEYS, STEP_KEYS), :] - top) * EXP2_SCALE).astype(jnp.bfloat16)
-        blocks = [block_of(pick_of(local, half, i * STEP_BLOCKS + b), TOK) for b in range(STEP_BLOCKS)]
+        blocks = [block_of(local, half, b, TOK) for b in range(i * STEP_BLOCKS, (i + 1) * STEP_BLOCKS)]
         values = jnp.concatenate([jnp.concatenate(blocks, axis=0).T, ones], axis=0)
         return dot(values, weight)
+
+    def sending(local, half, w):
+        at = spot(local)
+        return pltpu.make_async_copy(
+            results.at[2 * w + half, :, at, :], outs[2 * w + half].at[:, at, :], out_sems.at[2 * w + half, local]
+        )
 
     def finish(local, half, mixed):
         result = (mixed[:DH] * (1.0 / mixed[DH : DH + 1])).astype(jnp.bfloat16).T
@@ -195,7 +198,8 @@
         for w in range(WIDE):
             for j in range(2):
                 r = (w * 2 + j) * BLOCK
-                outs[2 * w + half][j, at, :] = result[r : r + BLOCK]
+                results[2 * w + half, j, at, :] = result[r : r + BLOCK]
+            sending(local, half, w).start()
         number = number_of(local, half)
         known = jnp.where(block_row <= number, logits[half][...], -jnp.inf)
         raised = jnp.exp2((known - jnp.max(known, axis=0, keepdims=True)) * EXP2_SCALE)
@@ -208,11 +212,13 @@
 
     def pair(this, half, that, other):
         top = jnp.max(tops[half][...], axis=0, keepdims=True)
-        mixed = None
+        mixed, peak = None, None
         for i in range(STEPS):
-            score(that, other, i)
+            near = score(that, other, i)
+            peak = near if peak is None else jnp.maximum(peak, near)
             got = weigh(this, half, i, top)
             mixed = got if mixed is None else mixed + got
+        tops[other][...] = peak
         finish(this, half, mixed)
 
     def step(local, carry):
@@ -223,16 +229,32 @@
         turn(following, 1)
         return carry
 
+    for copy in asks:
+        copy.wait()
     turn(0, 0)
     turn(0, 1)
-    for i in range(STEPS):
-        score(0, 0, i)
+    for copy in copies:
+        copy.wait()
+    padded = [pool[pl.ds(s * PIECE + 2 * TOK, COMP_PAD), :] for s in range(SHARDS)]
+    comp[...] = dot(take, jnp.concatenate(padded, axis=0)).astype(jnp.bfloat16)
+    peak = score(0, 0, 0)
+    for i in range(1, STEPS):
+        peak = jnp.maximum(peak, score(0, 0, i))
+    tops[0][...] = peak
     lax.fori_loop(0, TILES, step, 0)
+    for w in range(WIDE):
+        for half in range(2):
+            for local in range(TILES):
+                sending(local, half, w).wait()
 
 
 SMEM = pl.BlockSpec(memory_space=pltpu.SMEM)
 VMEM = pl.BlockSpec(memory_space=pltpu.VMEM)
 ANY = pl.BlockSpec(memory_space=pl.ANY)
+
+
+def grant(mib):
+    return pltpu.CompilerParams(vmem_limit_bytes=mib * 2**20)
 
 
 def bf16(*shape):
@@ -248,6 +270,7 @@
         in_specs=[SMEM, rows, rows, pl.BlockSpec((TILES * GROUPS, DH), lambda i: (0, 0))],
         out_specs=[piece, piece],
         out_shape=[bf16(PIECE, DH)] * 2,
+        compiler_params=grant(12),
         name="split_pools",
     )(place, keys, values, comp)
 
@@ -261,21 +284,21 @@
         in_specs=[SMEM, pl.BlockSpec((tokens * 16, DH), lambda i: (i, 0))],
         out_specs=[pl.BlockSpec((2, tokens, DH), lambda i: (0, i, 0))] * PARTS,
         out_shape=[bf16(2, TOK, DH)] * PARTS,
+        compiler_params=grant(12),
         name="split_queries",
     )(place, queries)
 
 
-def call_attend(chunk, place, picks, pieces, queries, sofar):
-    parts = pl.BlockSpec((2, TOK, DH), lambda i: (0, 0, 0))
-    sums = pl.BlockSpec((TILES, NBLK), lambda i: (0, 0))
+def call_attend(chunk, place, picks, owns, pieces, queries, sofar):
     return pl.pallas_call(
         functools.partial(attend, bool(sofar)),
-        grid=(1,),
-        in_specs=[SMEM, SMEM] + [ANY] * (2 * CHIPS) + [parts] * (2 * WIDE) + [sums] * len(sofar),
-        out_specs=[parts] * (2 * WIDE) + [sums] * 2,
+        in_specs=[SMEM] * 3 + [ANY] * (2 * CHIPS + 2 * WIDE) + [VMEM] * len(sofar),
+        out_specs=[ANY] * (2 * WIDE) + [VMEM] * 2,
         out_shape=[bf16(2, TOK, DH)] * (2 * WIDE) + [jax.ShapeDtypeStruct((TILES, NBLK), jnp.float32)] * 2,
         scratch_shapes=[
-            pltpu.VMEM((SHARDS, PIECE, DH), jnp.bfloat16),
+            pltpu.VMEM((SHARDS * PIECE, DH), jnp.bfloat16),
+            pltpu.VMEM((2 * WIDE, 2, TOK, DH), jnp.bfloat16),
+            pltpu.VMEM((2 * WIDE, 2, TOK, DH), jnp.bfloat16),
             pltpu.VMEM((NBLK, DH), jnp.bfloat16),
             pltpu.VMEM((2 * BLOCK, DH), jnp.bfloat16),
         ]
@@ -283,9 +306,14 @@
         + [pltpu.VMEM((KEYS, ROWS), jnp.float32)] * 2
         + [pltpu.VMEM((NBLK, ROWS), jnp.float32)] * 2
         + [pltpu.VMEM((8, ROWS), jnp.float32)] * 2
-        + [pltpu.SemaphoreType.DMA((2 * CHIPS,))],
+        + [
+            pltpu.SemaphoreType.DMA((2 * CHIPS,)),
+            pltpu.SemaphoreType.DMA((2 * WIDE,)),
+            pltpu.SemaphoreType.DMA((2 * WIDE, TILES)),
+        ],
+        compiler_params=grant(28),
         name="attend",
-    )(place, picks, *pieces, *[queries[2 * dx + half] for dx in chunk for half in range(2)], *sofar)
+    )(place, picks, owns, *pieces, *[queries[2 * dx + half] for dx in chunk for half in range(2)], *sofar)
 
 
 def call_join_outputs(place, parts):
@@ -295,6 +323,7 @@
         in_specs=[SMEM] + [pl.BlockSpec((2, JOIN_TOK, DH), lambda i: (0, i, 0))] * PARTS,
         out_specs=pl.BlockSpec((JOIN_TOK * 16, DH), lambda i: (i, 0)),
         out_shape=bf16(TOK * 16, DH),
+        compiler_params=grant(12),
         name="join_outputs",
     )(place, *parts)
 
@@ -348,10 +377,14 @@
     mine = lax.dynamic_index_in_dim(groups, 2 * col + core, 0, False)
     theirs = lax.dynamic_index_in_dim(groups, 2 * col + 1 - core, 0, False)
     theirs = by_seq(theirs, lambda z, c: to_seq(z, c + 1))
-    picks = jnp.concatenate([mine, theirs]).reshape(-1)
+    blocks = jnp.stack([mine, theirs])
+    shard = 2 * chip + (core + jnp.arange(2, dtype=jnp.int32)) % 2
+    number = shard[:, None] * TILES + jnp.arange(TILES, dtype=jnp.int32)
+    picks = (blocks // TILES * PIECE + blocks % TILES * BLOCK).reshape(-1)
+    owns = jnp.where(blocks == number[..., None], BLOCK, 0).reshape(-1)
     joined, sums = [None] * PARTS, []
     for chunk in CHUNKS:
-        *outs, keep, send = call_attend(chunk, place, picks, pieces, moved, sums)
+        *outs, keep, send = call_attend(chunk, place, picks, owns, pieces, moved, sums)
         sums = [keep, send]
         for w, dx in enumerate(chunk):
             for half in range(2):

time: 126 us -> 134 us (1.063)
  local copies, waits for them, and re-layouts: 2.84 us -> 12.9 us
  Pallas kernels: 41.8 us -> 32.4 us
  waiting for transfers between devices: 34.2 us -> 42.1 us
  starting transfers between devices: 42.8 us -> 44.6 us
    unnamed x59 -> x39, local copies, waits for them, and re-layouts: 1.38 us -> 11.9 us
    ppermute x17, waiting for transfers between devices: 11 us -> 15.3 us  [by_seq(): lax.ppermute(value, 'seq', [(s, move(s // 2, s % 2)) for s in range(SHARD...]
    pallas_call x1, Pallas kernels: 6.18 us -> 2.51 us  [call_join_outputs(): pl.pallas_call(functools.partial(join_outputs, JOIN_TOK), grid=(TOK // JO...]
    ppermute x14, waiting for transfers between devices: 23.2 us -> 26.8 us  [by_part(): return lax.ppermute(value, ('seq', 'head'), pairs)]
    ppermute x17, starting transfers between devices: 22.4 us -> 24.9 us  [by_seq(): lax.ppermute(value, 'seq', [(s, move(s // 2, s % 2)) for s in range(SHARD...]
    pallas_call x2, Pallas kernels: 27.4 us -> 25 us  [call_attend(): pl.pallas_call(functools.partial(attend, bool(sofar)), in_specs=[SMEM] *...]
    pallas_call x1, Pallas kernels: 3.66 us -> 1.74 us  [call_split_pools(): pl.pallas_call(split_pools, grid=(TOK // POOL_TOK,), in_specs=[SMEM, rows...]
    pallas_call x1, Pallas kernels: 4.54 us -> 3.14 us  [call_split_queries(): pl.pallas_call(functools.partial(split_queries, tokens), grid=(steps,), i...]
  transfers between devices with their start and end apart: 31 -> 31, of which waited for: 10 -> 11; matrix products, arithmetic and copies ran while one was open for 2% -> 1% of each run, Pallas kernels for 14% -> 10%
where the time goes in v2:
time: 134 us; the launch traced here: 133 us
  starting transfers between devices  44.6 us (33%)
  waiting for transfers between devices  42.1 us (31%)
  Pallas kernels  32.4 us (24%)
  local copies, waits for them, and re-layouts  12.9 us (10%)
    ppermute x14, waiting for transfers between devices, by_part(): return lax.ppermute(value, ('seq', 'head'), pairs)  26.8 us
    pallas_call x2, Pallas kernels, call_attend(): pl.pallas_call(functools.partial(attend, bool(sofar)), in_specs=[SMEM] *...  25 us
    ppermute x17, starting transfers between devices, by_seq(): lax.ppermute(value, 'seq', [(s, move(s // 2, s % 2)) for s in range(SHARD...  24.9 us
    ppermute x14, starting transfers between devices, by_part(): return lax.ppermute(value, ('seq', 'head'), pairs)  19.7 us
    ppermute x17, waiting for transfers between devices, by_seq(): lax.ppermute(value, 'seq', [(s, move(s // 2, s % 2)) for s in range(SHARD...  15.3 us
    unnamed x39, local copies, waits for them, and re-layouts  11.9 us
    pallas_call x1, Pallas kernels, call_split_queries(): pl.pallas_call(functools.partial(split_queries, tokens), grid=(steps,), i...  3.14 us
  transfers between devices with their start and end apart: 31, of which 11 were waited for; matrix products, arithmetic and copies ran while one was open for 1% of the time, Pallas kernels for 10%

profile of v2, /device:TPU:1, one launch (start us, length us, event | category | flops | bytes accessed | tf_op | source)
XLA Modules:
  0.0 133.1 jit_solution(15269110355801968969)
XLA Ops:
  0.7 0.1 pad_add_fusion.1.place
  0.7 1.6 %copy-done = bf16[1,512,2,8,128]{4,3,2,1,0:T(8,128)(2,1)S(1)} copy-done((bf16[1,512,2,8,128]{4,3,2,1,0:T(8,128)(2,1)S(1)}, bf16[1,512,2,8,128]{4,3,2,1,0:T(8,128)(2,1)}, u32[]{:S(2)}) %copy-start) | copy-done | bytes 2097176
  2.3 3.1 %split_queries.1 = (bf16[2,512,128]{2,1,0:T(8,128)(2,1)S(1)}, bf16[2,512,128]{2,1,0:T(8,128)(2,1)S(1)}, bf16[2,512,128]{2,1,0:T(8,128)(2,1)}, bf16[2,512,128]{2,...) custom-call(s32[3]{0:T(128)S(1)} %pad_add_fusion.1.place, ...), custom_call_target="tpu_custom_call" | custom-call | tf_op jit(solution)/shard_map/split_queries/pallas_call | solution.py:281
  5.5 0.7 copy-done.3
  6.2 0.7 copy-done.17
  6.9 2.0 %collective-permute-start.19 = (bf16[2,512,128]{2,1,0:T(8,128)(2,1)}, bf16[2,512,128]{2,1,0:T(8,128)(2,1)S(1)}, u32[]{:S(2)}, u32[]{:S(2)}) collective-permute-start(bf16[2,512,128]{2,1,0:T(8,128)(2,1)} %get-tuple-element.30), channel_id=1, source_target_pairs={{0,4},{4,8},{8,12},{12,0},{16,20},{20,24},{24,28},{28,16},{32,36},... | collective-permute-start | bytes 786440 | tf_op jit(solution)/shard_map/ppermute | solution.py:348
  8.9 2.1 %collective-permute-start.20 = (bf16[2,512,128]{2,1,0:T(8,128)(2,1)}, bf16[2,512,128]{2,1,0:T(8,128)(2,1)S(1)}, u32[]{:S(2)}, u32[]{:S(2)}) collective-permute-start(bf16[2,512,128]{2,1,0:T(8,128)(2,1)} %get-tuple-element.31), channel_id=1, source_target_pairs={{0,20},{4,24},{8,28},{12,16},{16,4},{20,8},{24,12},{28,0},{32,52},... | collective-permute-start | bytes 786440 | tf_op jit(solution)/shard_map/ppermute | solution.py:348
  11.0 0.8 constant_dynamic-slice_fusion.1
  11.8 0.1 collective-permute-start
  12.0 1.7 %split_pools.1 = (bf16[1040,128]{1,0:T(8,128)(2,1)S(1)}, bf16[1040,128]{1,0:T(8,128)(2,1)}) custom-call(s32[3]{0:T(128)S(1)} %pad_add_fusion.1.place, bf16[4096,128]{1,0:T(8,128)(2,1)S(1)} %bitcast.18, bf16[4096,128]{1,0:T(8,128)(2,1)S(1)} %bitcast.19, bf16[64,128]{1,0:T(8,128)(2,1)S(1)} %bitcast.20), custom_call_target="tpu_custom_call" | custom-call | tf_op jit(solution)/shard_map/split_pools/pallas_call | solution.py:267
  13.7 2.0 %collective-permute-start.13 = (bf16[1040,128]{1,0:T(8,128)(2,1)}, bf16[1040,128]{1,0:T(8,128)(2,1)S(1)}, u32[]{:S(2)}, u32[]{:S(2)}) collective-permute-start(bf16[1040,128]{1,0:T(8,128)(2,1)} %get-tuple-element.25), channel_id=1, source_target_pairs={{0,48},{16,32},{32,80},{48,64},{64,112},{80,96},{96,144},{112,128}... | collective-permute-start | bytes 798728 | tf_op jit(solution)/shard_map/ppermute | solution.py:332
  15.7 3.9 %collective-permute-start.3 = (bf16[1040,128]{1,0:T(8,128)(2,1)}, bf16[1040,128]{1,0:T(8,128)(2,1)S(1)}, u32[]{:S(2)}, u32[]{:S(2)}) collective-permute-start(bf16[1040,128]{1,0:T(8,128)(2,1)} %get-tuple-element.25), channel_id=1, source_target_pairs={{0,240},{16,224},{32,16},{48,0},{64,48},{80,32},{96,80},{112,64},{... | collective-permute-start | bytes 798728 | tf_op jit(solution)/shard_map/ppermute | solution.py:332
  19.6 0.0 collective-permute-done
  19.7 0.0 collective-permute-start.8
  19.7 0.7 copy-done.5
  20.4 2.7 %collective-permute-start.2 = (bf16[1040,128]{1,0:T(8,128)(2,1)S(1)}, bf16[1040,128]{1,0:T(8,128)(2,1)S(1)}, u32[]{:S(2)}, u32[]{:S(2)}) collective-permute-start(bf16[1040,128]{1,0:T(8,128)(2,1)S(1)} %get-tuple-element.24.refs_0_), channel_id=1, source_target_pairs={{0,224},{16,240},{32,0},{48,16},{64,32},{80,48},{96,64},{112,80},{... | collective-permute-start | bytes 798728 | tf_op jit(solution)/shard_map/ppermute | solution.py:332
  23.0 0.1 collective-permute-done.20.refs_17_
  23.1 0.7 copy-done.7
  23.8 1.7 %collective-permute-start.21 = (bf16[2,512,128]{2,1,0:T(8,128)(2,1)S(1)}, bf16[2,512,128]{2,1,0:T(8,128)(2,1)S(1)}, u32[]{:S(2)}, u32[]{:S(2)}) collective-permute-start(bf16[2,512,128]{2,1,0:T(8,128)(2,1)S(1)} %get-tuple-element.32), channel_id=1, source_target_pairs={{0,8},{4,12},{8,0},{12,4},{16,24},{20,28},{24,16},{28,20},{32,40},... | collective-permute-start | bytes 786440 | tf_op jit(solution)/shard_map/ppermute | solution.py:348
  25.5 1.3 collective-permute-done.13.refs_15_
  26.8 0.2 collective-permute-start.14
  27.0 0.0 collective-permute-done.3.refs_3_
  27.0 4.0 %collective-permute-start.5 = (bf16[1040,128]{1,0:T(8,128)(2,1)S(1)}, bf16[1040,128]{1,0:T(8,128)(2,1)S(1)}, u32[]{:S(2)}, u32[]{:S(2)}) collective-permute-start(bf16[1040,128]{1,0:T(8,128)(2,1)S(1)} %collective-permute-done.3.refs_3_), channel_id=1, source_target_pairs={{0,224},{16,240},{32,0},{48,16},{64,32},{80,48},{96,64},{112,80},{... | collective-permute-start | bytes 798728 | tf_op jit(solution)/shard_map/ppermute | solution.py:332
  31.0 0.5 collective-permute-done.8.refs_14_
  31.5 0.1 collective-permute-done.2.refs_2_
  31.6 3.4 %collective-permute-start.4 = (bf16[1040,128]{1,0:T(8,128)(2,1)S(1)}, bf16[1040,128]{1,0:T(8,128)(2,1)S(1)}, u32[]{:S(2)}, u32[]{:S(2)}) collective-permute-start(bf16[1040,128]{1,0:T(8,128)(2,1)S(1)} %collective-permute-done.2.refs_2_), channel_id=1, source_target_pairs={{0,224},{16,240},{32,0},{48,16},{64,32},{80,48},{96,64},{112,80},{... | collective-permute-start | bytes 798728 | tf_op jit(solution)/shard_map/ppermute | solution.py:332
  35.0 0.7 copy-done.9
  35.7 2.8 %collective-permute-start.22 = (bf16[2,512,128]{2,1,0:T(8,128)(2,1)S(1)}, bf16[2,512,128]{2,1,0:T(8,128)(2,1)S(1)}, u32[]{:S(2)}, u32[]{:S(2)}) collective-permute-start(bf16[2,512,128]{2,1,0:T(8,128)(2,1)S(1)} %get-tuple-element.33), channel_id=1, source_target_pairs={{0,24},{4,28},{8,16},{12,20},{16,8},{20,12},{24,0},{28,4},{32,56},... | collective-permute-start | bytes 786440 | tf_op jit(solution)/shard_map/ppermute | solution.py:348
  38.4 7.2 %collective-permute-done.22.refs_19_ = bf16[2,512,128]{2,1,0:T(8,128)(2,1)S(1)} collective-permute-done((bf16[2,512,128]{2,1,0:T(8,128)(2,1)S(1)}, bf16[2,512,128]{2,1,0:T(8,128)(2,1)S(1)}, u32[]{:S(2)}, u32[]{:S(2)}) %collective-permute-start.22) | collective-permute-done | bytes 262176 | tf_op jit(solution)/shard_map/ppermute | solution.py:348
  45.6 0.7 copy-done.11
  46.3 0.8 collective-permute-start.1
  47.2 3.3 %collective-permute-start.7 = (bf16[1040,128]{1,0:T(8,128)(2,1)S(1)}, bf16[1040,128]{1,0:T(8,128)(2,1)S(1)}, u32[]{:S(2)}, u32[]{:S(2)}) collective-permute-start(bf16[1040,128]{1,0:T(8,128)(2,1)S(1)} %collective-permute-done.5.refs_5_), channel_id=1, source_target_pairs={{0,224},{16,240},{32,0},{48,16},{64,32},{80,48},{96,64},{112,80},{... | collective-permute-start | bytes 798728 | tf_op jit(solution)/shard_map/ppermute | solution.py:332
  50.5 2.7 %collective-permute-start.6 = (bf16[1040,128]{1,0:T(8,128)(2,1)S(1)}, bf16[1040,128]{1,0:T(8,128)(2,1)}, u32[]{:S(2)}, u32[]{:S(2)}) collective-permute-start(bf16[1040,128]{1,0:T(8,128)(2,1)S(1)} %collective-permute-done.4.refs_4_), channel_id=1, source_target_pairs={{0,224},{16,240},{32,0},{48,16},{64,32},{80,48},{96,64},{112,80},{... | collective-permute-start | bytes 798728 | tf_op jit(solution)/shard_map/ppermute | solution.py:332
  53.2 0.1 iota_add_fusion
  53.3 0.1 eq.21
  53.3 0.1 eq.22
  53.4 1.4 %collective-permute-start.16 = (bf16[2,512,128]{2,1,0:T(8,128)(2,1)}, bf16[2,512,128]{2,1,0:T(8,128)(2,1)}, u32[]{:S(2)}, u32[]{:S(2)}) collective-permute-start(bf16[2,512,128]{2,1,0:T(8,128)(2,1)} %copy-done.18), channel_id=1, source_target_pairs={{0,12},{4,0},{8,4},{12,8},{16,28},{20,16},{24,20},{28,24},{32,44},... | collective-permute-start | bytes 786440 | tf_op jit(solution)/shard_map/ppermute | solution.py:348
  54.8 2.1 %collective-permute-done.15.refs_11_ = bf16[1040,128]{1,0:T(8,128)(2,1)S(1)} collective-permute-done((bf16[1040,128]{1,0:T(8,128)(2,1)S(1)}, bf16[1040,128]{1,0:T(8,128)(2,1)S(1)}, u32[]{:S(2)}, u32[]{:S(2)}) %collective-permute-start.15) | collective-permute-done | bytes 266272 | tf_op jit(solution)/shard_map/ppermute | solution.py:332
  56.9 2.2 %collective-permute-start.17 = (bf16[2,512,128]{2,1,0:T(8,128)(2,1)}, bf16[2,512,128]{2,1,0:T(8,128)(2,1)}, u32[]{:S(2)}, u32[]{:S(2)}) collective-permute-start(bf16[2,512,128]{2,1,0:T(8,128)(2,1)} %copy-done.17), channel_id=1, source_target_pairs={{0,28},{4,16},{8,20},{12,24},{16,12},{20,0},{24,4},{28,8},{32,60},... | collective-permute-start | bytes 786440 | tf_op jit(solution)/shard_map/ppermute | solution.py:348
  59.0 3.5 %collective-permute-done.10.refs_10_ = bf16[1040,128]{1,0:T(8,128)(2,1)S(1)} collective-permute-done((bf16[1040,128]{1,0:T(8,128)(2,1)S(1)}, bf16[1040,128]{1,0:T(8,128)(2,1)S(1)}, u32[]{:S(2)}, u32[]{:S(2)}) %collective-permute-start.10) | collective-permute-done | bytes 266272 | tf_op jit(solution)/shard_map/ppermute | solution.py:332
  62.6 1.3 collective-permute-start.12
  63.9 0.2 collective-permute-start.11
  64.0 0.1 stack.41
  64.1 5.8 %collective-permute-done.12.refs_9_ = bf16[1040,128]{1,0:T(8,128)(2,1)} collective-permute-done((bf16[1040,128]{1,0:T(8,128)(2,1)S(1)}, bf16[1040,128]{1,0:T(8,128)(2,1)}, u32[]{:S(2)}, u32[]{:S(2)}) %collective-permute-start.12) | collective-permute-done | bytes 266272 | tf_op jit(solution)/shard_map/ppermute | solution.py:332
  69.9 2.0 %collective-permute-done.11.refs_8_ = bf16[1040,128]{1,0:T(8,128)(2,1)} collective-permute-done((bf16[1040,128]{1,0:T(8,128)(2,1)S(1)}, bf16[1040,128]{1,0:T(8,128)(2,1)}, u32[]{:S(2)}, u32[]{:S(2)}) %collective-permute-start.11) | collective-permute-done | bytes 266272 | tf_op jit(solution)/shard_map/ppermute | solution.py:332
  72.0 0.9 copy-done.6
  72.9 0.9 copy-done.8
  73.9 0.9 copy-done.10
  74.8 0.9 copy-done.12
  75.8 11.4 %attend.2 = (bf16[2,512,128]{2,1,0:T(8,128)(2,1)}, bf16[2,512,128]{2,1,0:T(8,128)(2,1)}, bf16[2,512,128]{2,1,0:T(8,128)(2,1)}, bf16[2,512,128]{2,1,0:T(8,128)(2,...) custom-call(s32[3]{0:T(128)S(1)} %pad_add_fusion.1.place, s32[256]{0:T(256)S(1)} %get-tuple-element.51.picks, ...), custom_call_target="tpu_custom_call" | custom-call | tf_op jit(solution)/shard_map/attend/pallas_call | solution.py:293
  87.2 13.6 %attend.3 = (bf16[2,512,128]{2,1,0:T(8,128)(2,1)S(1)}, bf16[2,512,128]{2,1,0:T(8,128)(2,1)}, bf16[2,512,128]{2,1,0:T(8,128)(2,1)S(1)}, bf16[2,512,128]{2,1,0:T(8...) custom-call(s32[3]{0:T(128)S(1)} %pad_add_fusion.1.place, s32[256]{0:T(256)S(1)} %get-tuple-element.51.picks, ...), custom_call_target="tpu_custom_call" | custom-call | tf_op jit(solution)/shard_map/attend/pallas_call | solution.py:293
  100.8 0.7 copy-done.13
  101.5 1.9 %collective-permute-start.24 = (bf16[2,512,128]{2,1,0:T(8,128)(2,1)S(1)}, bf16[2,512,128]{2,1,0:T(8,128)(2,1)S(1)}, u32[]{:S(2)}, u32[]{:S(2)}) collective-permute-start(bf16[2,512,128]{2,1,0:T(8,128)(2,1)S(1)} %get-tuple-element.39), channel_id=1, source_target_pairs={{16,0},{20,4},{24,8},{28,12},{0,16},{4,20},{8,24},{12,28},{48,32},... | collective-permute-start | bytes 786440 | tf_op jit(solution)/shard_map/ppermute | solution.py:348
  103.5 0.5 collective-permute-start.29
  103.9 0.3 collective-permute-start.23
  104.2 0.4 collective-permute-start.30
  104.6 2.4 %collective-permute-start.25 = (bf16[2,512,128]{2,1,0:T(8,128)(2,1)}, bf16[2,512,128]{2,1,0:T(8,128)(2,1)S(1)}, u32[]{:S(2)}, u32[]{:S(2)}) collective-permute-start(bf16[2,512,128]{2,1,0:T(8,128)(2,1)} %get-tuple-element.40), channel_id=1, source_target_pairs={{4,0},{8,4},{12,8},{0,12},{20,16},{24,20},{28,24},{16,28},{36,32},... | collective-permute-start | bytes 786440 | tf_op jit(solution)/shard_map/ppermute | solution.py:348
  107.0 1.5 %collective-permute-start.26 = (bf16[2,512,128]{2,1,0:T(8,128)(2,1)}, bf16[2,512,128]{2,1,0:T(8,128)(2,1)S(1)}, u32[]{:S(2)}, u32[]{:S(2)}) collective-permute-start(bf16[2,512,128]{2,1,0:T(8,128)(2,1)} %get-tuple-element.41), channel_id=1, source_target_pairs={{20,0},{24,4},{28,8},{16,12},{4,16},{8,20},{12,24},{0,28},{52,32},... | collective-permute-start | bytes 786440 | tf_op jit(solution)/shard_map/ppermute | solution.py:348
  108.5 4.1 %collective-permute-done.29.refs_6_ = bf16[2,512,128]{2,1,0:T(8,128)(2,1)S(1)} collective-permute-done((bf16[2,512,128]{2,1,0:T(8,128)(2,1)S(1)}, bf16[2,512,128]{2,1,0:T(8,128)(2,1)S(1)}, u32[]{:S(2)}, u32[]{:S(2)}) %collective-permute-start.29) | collective-permute-done | bytes 262176 | tf_op jit(solution)/shard_map/ppermute | solution.py:348
  112.5 1.0 collective-permute-start.28
  113.6 0.6 copy.9
  114.2 15.4 %collective-permute-done.30.refs_7_ = bf16[2,512,128]{2,1,0:T(8,128)(2,1)S(1)} collective-permute-done((bf16[2,512,128]{2,1,0:T(8,128)(2,1)}, bf16[2,512,128]{2,1,0:T(8,128)(2,1)S(1)}, u32[]{:S(2)}, u32[]{:S(2)}) %collective-permute-start.30) | collective-permute-done | bytes 262176 | tf_op jit(solution)/shard_map/ppermute | solution.py:348
  129.6 0.9 copy-done.14
  130.5 2.5 %join_outputs.1 = bf16[8192,128]{1,0:T(8,128)(2,1)} custom-call(s32[3]{0:T(128)S(1)} %pad_add_fusion.1.place, bf16[2,512,128]{2,1,0:T(8,128)(2,1)S(1)} %copy-done.14, bf16[2,512,128]{2,1,0:T(8,128)(2,1)S(1)} %collective-permute-done.24.refs_1_, bf16[2,512,128]{2,1,0:T(8,128)(2,1)S(1)} %collective-permute-done.25.refs_2_, ...), custom_call_target="tpu_custom_call" | custom-call | tf_op jit(solution)/shard_map/join_outputs/pallas_call | solution.py:320
  (52 shorter events, 0.1 us)
Async XLA Ops:
  0.6 11.3 %copy-start.15 = (bf16[1,8,8,128]{3,2,1,0:T(8,128)(2,1)S(1)}, bf16[1,8,8,128]{3,2,1,0:T(8,128)(2,1)}, u32[]{:S(2)}) copy-start(bf16[1,8,8,128]{3,2,1,0:T(8,128)(2,1)} %param.8) | copy-start | bytes 49156
  0.7 1.6 %copy-start = (bf16[1,512,2,8,128]{4,3,2,1,0:T(8,128)(2,1)S(1)}, bf16[1,512,2,8,128]{4,3,2,1,0:T(8,128)(2,1)}, u32[]{:S(2)}) copy-start(bf16[1,512,2,8,128]{4,3,2,1,0:T(8,128)(2,1)} %param.5) | copy-start | bytes 6291460
  2.3 9.6 %copy-start.1 = (bf16[1,512,8,128]{3,2,1,0:T(8,128)(2,1)S(1)}, bf16[1,512,8,128]{3,2,1,0:T(8,128)(2,1)}, u32[]{:S(2)}) copy-start(bf16[1,512,8,128]{3,2,1,0:T(8,128)(2,1)} %param.6) | copy-start | bytes 3145732
  2.3 9.6 %copy-start.2 = (bf16[1,512,8,128]{3,2,1,0:T(8,128)(2,1)S(1)}, bf16[1,512,8,128]{3,2,1,0:T(8,128)(2,1)}, u32[]{:S(2)}) copy-start(bf16[1,512,8,128]{3,2,1,0:T(8,128)(2,1)} %param.7) | copy-start | bytes 3145732
  5.5 0.7 copy-start.3
  6.2 0.7 copy-start.17
  6.9 2.0 %copy-start.16 = (bf16[2,512,128]{2,1,0:T(8,128)(2,1)}, bf16[2,512,128]{2,1,0:T(8,128)(2,1)S(1)}, u32[]{:S(2)}) copy-start(bf16[2,512,128]{2,1,0:T(8,128)(2,1)S(1)} %get-tuple-element.29) | copy-start | bytes 786436
  6.9 2.0 %copy-start.18 = (bf16[2,512,128]{2,1,0:T(8,128)(2,1)}, bf16[2,512,128]{2,1,0:T(8,128)(2,1)S(1)}, u32[]{:S(2)}) copy-start(bf16[2,512,128]{2,1,0:T(8,128)(2,1)S(1)} %get-tuple-element.26) | copy-start | bytes 786436
  6.9 12.8 %collective-permute-start.19 = (bf16[2,512,128]{2,1,0:T(8,128)(2,1)}, bf16[2,512,128]{2,1,0:T(8,128)(2,1)S(1)}, u32[]{:S(2)}, u32[]{:S(2)}) collective-permute-start(bf16[2,512,128]{2,1,0:T(8,128)(2,1)} %get-tuple-element.30), channel_id=1, source_target_pairs={{0,4},{4,8},{8,12},{12,0},{16,20},{20,24},{24,28},{28,16},{32,36},... | collective-permute-start | bytes 786440 | tf_op jit(solution)/shard_map/ppermute | solution.py:348
  8.9 14.2 %collective-permute-start.20 = (bf16[2,512,128]{2,1,0:T(8,128)(2,1)}, bf16[2,512,128]{2,1,0:T(8,128)(2,1)S(1)}, u32[]{:S(2)}, u32[]{:S(2)}) collective-permute-start(bf16[2,512,128]{2,1,0:T(8,128)(2,1)} %get-tuple-element.31), channel_id=1, source_target_pairs={{0,20},{4,24},{8,28},{12,16},{16,4},{20,8},{24,12},{28,0},{32,52},... | collective-permute-start | bytes 786440 | tf_op jit(solution)/shard_map/ppermute | solution.py:348
  11.8 7.8 %collective-permute-start = (s32[8,16]{1,0:T(8,128)S(1)}, s32[8,16]{1,0:T(8,128)S(1)}, u32[]{:S(2)}, u32[]{:S(2)}) collective-permute-start(s32[8,16]{1,0:T(8,128)S(1)} %bitcast.24), channel_id=1, source_target_pairs={{0,16},{16,0},{32,48},{48,32},{64,80},{80,64},{96,112},{112,96},{1... | collective-permute-start | bytes 1544 | tf_op jit(solution)/shard_map/ppermute | solution.py:332
  13.7 13.1 %collective-permute-start.13 = (bf16[1040,128]{1,0:T(8,128)(2,1)}, bf16[1040,128]{1,0:T(8,128)(2,1)S(1)}, u32[]{:S(2)}, u32[]{:S(2)}) collective-permute-start(bf16[1040,128]{1,0:T(8,128)(2,1)} %get-tuple-element.25), channel_id=1, source_target_pairs={{0,48},{16,32},{32,80},{48,64},{64,112},{80,96},{96,144},{112,128}... | collective-permute-start | bytes 798728 | tf_op jit(solution)/shard_map/ppermute | solution.py:332
  15.7 11.3 %collective-permute-start.3 = (bf16[1040,128]{1,0:T(8,128)(2,1)}, bf16[1040,128]{1,0:T(8,128)(2,1)S(1)}, u32[]{:S(2)}, u32[]{:S(2)}) collective-permute-start(bf16[1040,128]{1,0:T(8,128)(2,1)} %get-tuple-element.25), channel_id=1, source_target_pairs={{0,240},{16,224},{32,16},{48,0},{64,48},{80,32},{96,80},{112,64},{... | collective-permute-start | bytes 798728 | tf_op jit(solution)/shard_map/ppermute | solution.py:332
  19.7 11.8 %collective-permute-start.8 = (bf16[1040,128]{1,0:T(8,128)(2,1)S(1)}, bf16[1040,128]{1,0:T(8,128)(2,1)S(1)}, u32[]{:S(2)}, u32[]{:S(2)}) collective-permute-start(bf16[1040,128]{1,0:T(8,128)(2,1)S(1)} %get-tuple-element.24.refs_0_), channel_id=1, source_target_pairs={{0,32},{16,48},{32,64},{48,80},{64,96},{80,112},{96,128},{112,144}... | collective-permute-start | bytes 798728 | tf_op jit(solution)/shard_map/ppermute | solution.py:332
  19.7 0.7 copy-start.5
  20.4 11.2 %collective-permute-start.2 = (bf16[1040,128]{1,0:T(8,128)(2,1)S(1)}, bf16[1040,128]{1,0:T(8,128)(2,1)S(1)}, u32[]{:S(2)}, u32[]{:S(2)}) collective-permute-start(bf16[1040,128]{1,0:T(8,128)(2,1)S(1)} %get-tuple-element.24.refs_0_), channel_id=1, source_target_pairs={{0,224},{16,240},{32,0},{48,16},{64,32},{80,48},{96,64},{112,80},{... | collective-permute-start | bytes 798728 | tf_op jit(solution)/shard_map/ppermute | solution.py:332
  23.1 0.7 copy-start.7
  23.8 11.1 %collective-permute-start.21 = (bf16[2,512,128]{2,1,0:T(8,128)(2,1)S(1)}, bf16[2,512,128]{2,1,0:T(8,128)(2,1)S(1)}, u32[]{:S(2)}, u32[]{:S(2)}) collective-permute-start(bf16[2,512,128]{2,1,0:T(8,128)(2,1)S(1)} %get-tuple-element.32), channel_id=1, source_target_pairs={{0,8},{4,12},{8,0},{12,4},{16,24},{20,28},{24,16},{28,20},{32,40},... | collective-permute-start | bytes 786440 | tf_op jit(solution)/shard_map/ppermute | solution.py:348
  26.8 20.4 %collective-permute-start.14 = (bf16[1040,128]{1,0:T(8,128)(2,1)S(1)}, bf16[1040,128]{1,0:T(8,128)(2,1)S(1)}, u32[]{:S(2)}, u32[]{:S(2)}) collective-permute-start(bf16[1040,128]{1,0:T(8,128)(2,1)S(1)} %collective-permute-done.13.refs_15_), channel_id=1, source_target_pairs={{0,32},{16,48},{32,64},{48,80},{64,96},{80,112},{96,128},{112,144}... | collective-permute-start | bytes 798728 | tf_op jit(solution)/shard_map/ppermute | solution.py:332
  27.0 20.2 %collective-permute-start.5 = (bf16[1040,128]{1,0:T(8,128)(2,1)S(1)}, bf16[1040,128]{1,0:T(8,128)(2,1)S(1)}, u32[]{:S(2)}, u32[]{:S(2)}) collective-permute-start(bf16[1040,128]{1,0:T(8,128)(2,1)S(1)} %collective-permute-done.3.refs_3_), channel_id=1, source_target_pairs={{0,224},{16,240},{32,0},{48,16},{64,32},{80,48},{96,64},{112,80},{... | collective-permute-start | bytes 798728 | tf_op jit(solution)/shard_map/ppermute | solution.py:332
  31.5 19.0 %collective-permute-start.9 = (bf16[1040,128]{1,0:T(8,128)(2,1)S(1)}, bf16[1040,128]{1,0:T(8,128)(2,1)S(1)}, u32[]{:S(2)}, u32[]{:S(2)}) collective-permute-start(bf16[1040,128]{1,0:T(8,128)(2,1)S(1)} %collective-permute-done.8.refs_14_), channel_id=1, source_target_pairs={{0,32},{16,48},{32,64},{48,80},{64,96},{80,112},{96,128},{112,144}... | collective-permute-start | bytes 798728 | tf_op jit(solution)/shard_map/ppermute | solution.py:332
  31.6 18.9 %collective-permute-start.4 = (bf16[1040,128]{1,0:T(8,128)(2,1)S(1)}, bf16[1040,128]{1,0:T(8,128)(2,1)S(1)}, u32[]{:S(2)}, u32[]{:S(2)}) collective-permute-start(bf16[1040,128]{1,0:T(8,128)(2,1)S(1)} %collective-permute-done.2.refs_2_), channel_id=1, source_target_pairs={{0,224},{16,240},{32,0},{48,16},{64,32},{80,48},{96,64},{112,80},{... | collective-permute-start | bytes 798728 | tf_op jit(solution)/shard_map/ppermute | solution.py:332
  35.0 0.7 copy-start.9
  35.7 10.0 %collective-permute-start.22 = (bf16[2,512,128]{2,1,0:T(8,128)(2,1)S(1)}, bf16[2,512,128]{2,1,0:T(8,128)(2,1)S(1)}, u32[]{:S(2)}, u32[]{:S(2)}) collective-permute-start(bf16[2,512,128]{2,1,0:T(8,128)(2,1)S(1)} %get-tuple-element.33), channel_id=1, source_target_pairs={{0,24},{4,28},{8,16},{12,20},{16,8},{20,12},{24,0},{28,4},{32,56},... | collective-permute-start | bytes 786440 | tf_op jit(solution)/shard_map/ppermute | solution.py:348
  45.6 0.7 copy-start.11
  46.3 7.1 %collective-permute-start.1 = (bf16[1040,128]{1,0:T(8,128)(2,1)}, bf16[1040,128]{1,0:T(8,128)(2,1)S(1)}, u32[]{:S(2)}, u32[]{:S(2)}) collective-permute-start(bf16[1040,128]{1,0:T(8,128)(2,1)} %get-tuple-element.25), channel_id=1, source_target_pairs={{0,16},{16,0},{32,48},{48,32},{64,80},{80,64},{96,112},{112,96},{1... | collective-permute-start | bytes 798728 | tf_op jit(solution)/shard_map/ppermute | solution.py:332
  47.2 9.7 %collective-permute-start.15 = (bf16[1040,128]{1,0:T(8,128)(2,1)S(1)}, bf16[1040,128]{1,0:T(8,128)(2,1)S(1)}, u32[]{:S(2)}, u32[]{:S(2)}) collective-permute-start(bf16[1040,128]{1,0:T(8,128)(2,1)S(1)} %collective-permute-done.14.refs_13_), channel_id=1, source_target_pairs={{0,32},{16,48},{32,64},{48,80},{64,96},{80,112},{96,128},{112,144}... | collective-permute-start | bytes 798728 | tf_op jit(solution)/shard_map/ppermute | solution.py:332
  47.2 11.9 %collective-permute-start.7 = (bf16[1040,128]{1,0:T(8,128)(2,1)S(1)}, bf16[1040,128]{1,0:T(8,128)(2,1)S(1)}, u32[]{:S(2)}, u32[]{:S(2)}) collective-permute-start(bf16[1040,128]{1,0:T(8,128)(2,1)S(1)} %collective-permute-done.5.refs_5_), channel_id=1, source_target_pairs={{0,224},{16,240},{32,0},{48,16},{64,32},{80,48},{96,64},{112,80},{... | collective-permute-start | bytes 798728 | tf_op jit(solution)/shard_map/ppermute | solution.py:332
  50.5 12.1 %collective-permute-start.10 = (bf16[1040,128]{1,0:T(8,128)(2,1)S(1)}, bf16[1040,128]{1,0:T(8,128)(2,1)S(1)}, u32[]{:S(2)}, u32[]{:S(2)}) collective-permute-start(bf16[1040,128]{1,0:T(8,128)(2,1)S(1)} %collective-permute-done.9.refs_12_), channel_id=1, source_target_pairs={{0,32},{16,48},{32,64},{48,80},{64,96},{80,112},{96,128},{112,144}... | collective-permute-start | bytes 798728 | tf_op jit(solution)/shard_map/ppermute | solution.py:332
  50.5 13.4 %collective-permute-start.6 = (bf16[1040,128]{1,0:T(8,128)(2,1)S(1)}, bf16[1040,128]{1,0:T(8,128)(2,1)}, u32[]{:S(2)}, u32[]{:S(2)}) collective-permute-start(bf16[1040,128]{1,0:T(8,128)(2,1)S(1)} %collective-permute-done.4.refs_4_), channel_id=1, source_target_pairs={{0,224},{16,240},{32,0},{48,16},{64,32},{80,48},{96,64},{112,80},{... | collective-permute-start | bytes 798728 | tf_op jit(solution)/shard_map/ppermute | solution.py:332
  53.4 33.8 %collective-permute-start.16 = (bf16[2,512,128]{2,1,0:T(8,128)(2,1)}, bf16[2,512,128]{2,1,0:T(8,128)(2,1)}, u32[]{:S(2)}, u32[]{:S(2)}) collective-permute-start(bf16[2,512,128]{2,1,0:T(8,128)(2,1)} %copy-done.18), channel_id=1, source_target_pairs={{0,12},{4,0},{8,4},{12,8},{16,28},{20,16},{24,20},{28,24},{32,44},... | collective-permute-start | bytes 786440 | tf_op jit(solution)/shard_map/ppermute | solution.py:348
  56.9 30.4 %collective-permute-start.17 = (bf16[2,512,128]{2,1,0:T(8,128)(2,1)}, bf16[2,512,128]{2,1,0:T(8,128)(2,1)}, u32[]{:S(2)}, u32[]{:S(2)}) collective-permute-start(bf16[2,512,128]{2,1,0:T(8,128)(2,1)} %copy-done.17), channel_id=1, source_target_pairs={{0,28},{4,16},{8,20},{12,24},{16,12},{20,0},{24,4},{28,8},{32,60},... | collective-permute-start | bytes 786440 | tf_op jit(solution)/shard_map/ppermute | solution.py:348
  59.0 28.2 %collective-permute-start.18 = (bf16[2,512,128]{2,1,0:T(8,128)(2,1)}, bf16[2,512,128]{2,1,0:T(8,128)(2,1)}, u32[]{:S(2)}, u32[]{:S(2)}) collective-permute-start(bf16[2,512,128]{2,1,0:T(8,128)(2,1)} %copy-done.16), channel_id=1, source_target_pairs={{0,16},{4,20},{8,24},{12,28},{16,0},{20,4},{24,8},{28,12},{32,48},... | collective-permute-start | bytes 786440 | tf_op jit(solution)/shard_map/ppermute | solution.py:348
  62.6 7.4 %collective-permute-start.12 = (bf16[1040,128]{1,0:T(8,128)(2,1)S(1)}, bf16[1040,128]{1,0:T(8,128)(2,1)}, u32[]{:S(2)}, u32[]{:S(2)}) collective-permute-start(bf16[1040,128]{1,0:T(8,128)(2,1)S(1)} %collective-permute-done.7.refs_7_), channel_id=1, source_target_pairs={{0,224},{16,240},{32,0},{48,16},{64,32},{80,48},{96,64},{112,80},{... | collective-permute-start | bytes 798728 | tf_op jit(solution)/shard_map/ppermute | solution.py:332
  63.9 8.1 %collective-permute-start.11 = (bf16[1040,128]{1,0:T(8,128)(2,1)S(1)}, bf16[1040,128]{1,0:T(8,128)(2,1)}, u32[]{:S(2)}, u32[]{:S(2)}) collective-permute-start(bf16[1040,128]{1,0:T(8,128)(2,1)S(1)} %collective-permute-done.10.refs_10_), channel_id=1, source_target_pairs={{0,32},{16,48},{32,64},{48,80},{64,96},{80,112},{96,128},{112,144}... | collective-permute-start | bytes 798728 | tf_op jit(solution)/shard_map/ppermute | solution.py:332
  72.0 1.0 copy-start.6
  72.9 0.9 copy-start.8
  73.9 0.9 copy-start.10
  74.8 0.9 copy-start.12
  75.8 11.5 %copy-start.4 = (bf16[2,512,128]{2,1,0:T(8,128)(2,1)S(1)}, bf16[2,512,128]{2,1,0:T(8,128)(2,1)}, u32[]{:S(2)}) copy-start(bf16[2,512,128]{2,1,0:T(8,128)(2,1)} %copy-done.3) | copy-start | bytes 786436
  100.8 0.7 copy-start.13
  101.5 6.9 %collective-permute-start.24 = (bf16[2,512,128]{2,1,0:T(8,128)(2,1)S(1)}, bf16[2,512,128]{2,1,0:T(8,128)(2,1)S(1)}, u32[]{:S(2)}, u32[]{:S(2)}) collective-permute-start(bf16[2,512,128]{2,1,0:T(8,128)(2,1)S(1)} %get-tuple-element.39), channel_id=1, source_target_pairs={{16,0},{20,4},{24,8},{28,12},{0,16},{4,20},{8,24},{12,28},{48,32},... | collective-permute-start | bytes 786440 | tf_op jit(solution)/shard_map/ppermute | solution.py:348
  103.5 9.1 %collective-permute-start.29 = (bf16[2,512,128]{2,1,0:T(8,128)(2,1)S(1)}, bf16[2,512,128]{2,1,0:T(8,128)(2,1)S(1)}, u32[]{:S(2)}, u32[]{:S(2)}) collective-permute-start(bf16[2,512,128]{2,1,0:T(8,128)(2,1)S(1)} %get-tuple-element.44), channel_id=1, source_target_pairs={{12,0},{0,4},{4,8},{8,12},{28,16},{16,20},{20,24},{24,28},{44,32},... | collective-permute-start | bytes 786440 | tf_op jit(solution)/shard_map/ppermute | solution.py:348
  103.9 3.1 %collective-permute-start.23 = (f32[8,128]{1,0:T(8,128)S(1)}, f32[8,128]{1,0:T(8,128)S(1)}, u32[]{:S(2)}, u32[]{:S(2)}) collective-permute-start(f32[8,128]{1,0:T(8,128)S(1)} %get-tuple-element.37), channel_id=1, source_target_pairs={{0,16},{16,0},{32,48},{48,32},{64,80},{80,64},{96,112},{112,96},{1... | collective-permute-start | bytes 12296 | tf_op jit(solution)/shard_map/ppermute | solution.py:332
  104.2 25.3 %collective-permute-start.30 = (bf16[2,512,128]{2,1,0:T(8,128)(2,1)}, bf16[2,512,128]{2,1,0:T(8,128)(2,1)S(1)}, u32[]{:S(2)}, u32[]{:S(2)}) collective-permute-start(bf16[2,512,128]{2,1,0:T(8,128)(2,1)} %get-tuple-element.45), channel_id=1, source_target_pairs={{28,0},{16,4},{20,8},{24,12},{12,16},{0,20},{4,24},{8,28},{60,32},... | collective-permute-start | bytes 786440 | tf_op jit(solution)/shard_map/ppermute | solution.py:348
  104.6 25.0 %collective-permute-start.25 = (bf16[2,512,128]{2,1,0:T(8,128)(2,1)}, bf16[2,512,128]{2,1,0:T(8,128)(2,1)S(1)}, u32[]{:S(2)}, u32[]{:S(2)}) collective-permute-start(bf16[2,512,128]{2,1,0:T(8,128)(2,1)} %get-tuple-element.40), channel_id=1, source_target_pairs={{4,0},{8,4},{12,8},{0,12},{20,16},{24,20},{28,24},{16,28},{36,32},... | collective-permute-start | bytes 786440 | tf_op jit(solution)/shard_map/ppermute | solution.py:348
  107.0 22.6 %collective-permute-start.26 = (bf16[2,512,128]{2,1,0:T(8,128)(2,1)}, bf16[2,512,128]{2,1,0:T(8,128)(2,1)S(1)}, u32[]{:S(2)}, u32[]{:S(2)}) collective-permute-start(bf16[2,512,128]{2,1,0:T(8,128)(2,1)} %get-tuple-element.41), channel_id=1, source_target_pairs={{20,0},{24,4},{28,8},{16,12},{4,16},{8,20},{12,24},{0,28},{52,32},... | collective-permute-start | bytes 786440 | tf_op jit(solution)/shard_map/ppermute | solution.py:348
  108.5 21.1 %collective-permute-start.27 = (bf16[2,512,128]{2,1,0:T(8,128)(2,1)}, bf16[2,512,128]{2,1,0:T(8,128)(2,1)S(1)}, u32[]{:S(2)}, u32[]{:S(2)}) collective-permute-start(bf16[2,512,128]{2,1,0:T(8,128)(2,1)} %get-tuple-element.42), channel_id=1, source_target_pairs={{8,0},{12,4},{0,8},{4,12},{24,16},{28,20},{16,24},{20,28},{40,32},... | collective-permute-start | bytes 786440 | tf_op jit(solution)/shard_map/ppermute | solution.py:348
  112.5 17.0 %collective-permute-start.28 = (bf16[2,512,128]{2,1,0:T(8,128)(2,1)}, bf16[2,512,128]{2,1,0:T(8,128)(2,1)S(1)}, u32[]{:S(2)}, u32[]{:S(2)}) collective-permute-start(bf16[2,512,128]{2,1,0:T(8,128)(2,1)} %get-tuple-element.43), channel_id=1, source_target_pairs={{24,0},{28,4},{16,8},{20,12},{8,16},{12,20},{0,24},{4,28},{56,32},... | collective-permute-start | bytes 786440 | tf_op jit(solution)/shard_map/ppermute | solution.py:348
  129.6 1.0 copy-start.14

commit v3 on v2

v3 whole, which is shorter than its diff:
```python
import functools
import math

import jax
import jax.numpy as jnp
from jax import lax
from jax.experimental import pallas as pl
from jax.experimental.pallas import tpu as pltpu
from jax.sharding import PartitionSpec as P


HPG = 8
GROUPS = 8
DH = 128
BLOCK = 64
TOPN = 16
NBLK = 128
SHARDS = 16
CHIPS = 8
COLS = 4
TOK = 512
TILES = 8
COMP_PAD = 16
PIECE = 2 * TOK + COMP_PAD
PARTS = 8
LOADS = 4
HALVES = (1, 0)
KEYS = TOPN * BLOCK
ROWS = HPG * BLOCK
COMP_ROWS = SHARDS * COMP_PAD
STEPS = 4
STEP_BLOCKS = TOPN // STEPS
STEP_KEYS = KEYS // STEPS
STEP_COMP = NBLK // STEPS
ONES = 16
FAR = -1.0e9
EXP2_SCALE = DH**-0.5 * math.log2(math.e)


def iota(shape, dim):
    return lax.broadcasted_iota(jnp.int32, shape, dim)


def dot(lhs, rhs, dims=(((1,), (0,)), ((), ()))):
    return lax.dot_general(lhs, rhs, dims, preferred_element_type=jnp.float32)


def one_hot(cond):
    return jnp.where(cond, 1.0, 0.0).astype(jnp.bfloat16)


def split_pools(place, keys, values, comp, own, other, stage, sems):
    mine = place[0] * 2 + place[1]
    theirs = place[0] * 2 + 1 - place[1]
    size = TOK * GROUPS // LOADS
    copies = []
    for i in range(LOADS):
        rows = pl.ds(i * size, size)
        copies.append([pltpu.make_async_copy(ref.at[rows, :], stage.at[k, rows, :], sems.at[k, i]) for k, ref in enumerate((keys, values))])
    for pair in copies:
        for copy in pair:
            copy.start()
    step = 32
    row = iota((2 * step, step * GROUPS), 0)
    col = iota((2 * step, step * GROUPS), 1)
    group = jnp.where(row < step, mine, theirs)
    pick = one_hot(col == (row % step) * GROUPS + group)
    row = iota((2 * COMP_PAD, TILES * GROUPS), 0)
    col = iota((2 * COMP_PAD, TILES * GROUPS), 1)
    group = jnp.where(row < COMP_PAD, mine, theirs)
    block = row % COMP_PAD
    got = dot(one_hot((col == block * GROUPS + group) & (block < TILES)), comp[...]).astype(jnp.bfloat16)
    own[pl.ds(2 * TOK, COMP_PAD), :] = got[:COMP_PAD]
    other[pl.ds(2 * TOK, COMP_PAD), :] = got[COMP_PAD:]
    for i in range(TOK // step):
        if i % (TOK // step // LOADS) == 0:
            for copy in copies[i // (TOK // step // LOADS)]:
                copy.wait()
        rows = pl.ds(i * step * GROUPS, step * GROUPS)
        got = dot(pick, jnp.concatenate([stage[0, rows, :], stage[1, rows, :]], axis=1)).astype(jnp.bfloat16)
        own[pl.ds(i * step, step), :] = got[:step, :DH]
        own[pl.ds(TOK + i * step, step), :] = got[:step, DH:]
        other[pl.ds(i * step, step), :] = got[step:, :DH]
        other[pl.ds(TOK + i * step, step), :] = got[step:, DH:]


def row_of(r, place):
    part = r // 32
    head = (r // 16) % 2
    token = r % 16
    group = 2 * ((place[0] + part // 2) % COLS) + (place[1] + part % 2) % 2
    return token * 16 + head * GROUPS + group


def split_queries(tokens, place, queries, *parts):
    shape = (256, 256)
    pick = one_hot(iota(shape, 1) == row_of(iota(shape, 0), place))
    for i in range(tokens // 32):
        pair = jnp.concatenate([queries[pl.ds(i * 512, 256), :], queries[pl.ds(i * 512 + 256, 256), :]], axis=1)
        got = dot(pick, pair).astype(jnp.bfloat16)
        for k in range(PARTS):
            for j in range(2):
                rows = got[k * 32 + j * 16 : k * 32 + j * 16 + 16]
                parts[k][j, pl.ds(i * 32, 16), :] = rows[:, :DH]
                parts[k][j, pl.ds(i * 32 + 16, 16), :] = rows[:, DH:]


def join_outputs(place, *refs):
    parts, (out, result, sems) = refs[:PARTS], refs[PARTS:]
    shape = (256, 256)
    pick = one_hot(iota(shape, 0) == row_of(iota(shape, 1), place))
    copies = []
    for i in range(TOK // 32):
        halves = []
        for h in range(2):
            at = pl.ds(i * 32 + h * 16, 16)
            halves.append(jnp.concatenate([parts[k][j, at, :] for k in range(PARTS) for j in range(2)], axis=0))
        got = dot(pick, jnp.concatenate(halves, axis=1)).astype(jnp.bfloat16)
        result[pl.ds(i * 512, 256), :] = got[:, :DH]
        result[pl.ds(i * 512 + 256, 256), :] = got[:, DH:]
        if i % 4 == 3:
            rows = pl.ds((i - 3) * 512, 2048)
            copies.append(pltpu.make_async_copy(result.at[rows, :], out.at[rows, :], sems.at[i // 4]))
            copies[-1].start()
    for copy in copies:
        copy.wait()


def attend(half, place, picks, owns, *refs):
    pieces, refs = refs[: 2 * CHIPS], refs[2 * CHIPS :]
    queries, refs = refs[:COLS], refs[COLS:]
    outs, refs = refs[:COLS], refs[COLS:]
    pooled, pool, comp, mask, *rest, sems = refs
    turned, scores, logits, tops = rest[0:2], rest[2:4], rest[4:6], rest[6:8]
    core, chip = place[1], place[2]
    copies = []
    for k in range(CHIPS):
        for h in range(2):
            slot = 2 * ((chip + k) % CHIPS) + (core + h) % 2
            rows = pl.ds(pl.multiple_of(slot * PIECE, COMP_PAD), PIECE)
            copies.append(pltpu.make_async_copy(pieces[2 * k + h], pool.at[rows, :], sems.at[2 * k + h]))
    for copy in copies:
        copy.start()
    shape = (2 * BLOCK, DH)
    row = iota(shape, 0)
    hidden = (row >= BLOCK) & (row - BLOCK > iota(shape, 1))
    mask[...] = jnp.where(hidden, FAR, 0.0).astype(jnp.bfloat16)
    shape = (DH, ROWS)
    for stream in range(2):
        turned[stream][pl.ds(DH, DH), :] = one_hot(iota(shape, 0) == iota(shape, 1) % BLOCK)
    shape = (NBLK, COMP_ROWS)
    take = one_hot(iota(shape, 1) == iota(shape, 0) // TILES * COMP_PAD + iota(shape, 0) % TILES)
    block_row = iota((NBLK, ROWS), 0)
    ones = jnp.full((ONES, STEP_KEYS), 1.0, jnp.bfloat16)

    def spot(local):
        return pl.ds(pl.multiple_of(local * BLOCK, BLOCK), BLOCK)

    def block_of(local, b, offset):
        start = picks[(half * TILES + local) * TOPN + b] + offset
        return pool[pl.ds(pl.multiple_of(start, COMP_PAD), BLOCK), :]

    def mask_of(local, b):
        start = owns[(half * TILES + local) * TOPN + b]
        return mask[pl.ds(pl.multiple_of(start, BLOCK), BLOCK), :]

    def turn(local, stream):
        at = spot(local)
        query = jnp.concatenate([queries[dx][j, at, :] for dx in range(COLS) for j in range(2)], axis=0)
        turned[stream][pl.ds(0, DH), :] = query.T

    def score(local, stream, i):
        keys = []
        for b in range(i * STEP_BLOCKS, (i + 1) * STEP_BLOCKS):
            keys.append(jnp.concatenate([block_of(local, b, 0), mask_of(local, b)], axis=1))
        some = comp[pl.ds(i * STEP_COMP, STEP_COMP), :]
        keys.append(jnp.concatenate([some, jnp.zeros_like(some)], axis=1))
        got = dot(jnp.concatenate(keys, axis=0), turned[stream][...])
        near = got[:STEP_KEYS]
        scores[stream][pl.ds(i * STEP_KEYS, STEP_KEYS), :] = near
        logits[stream][pl.ds(i * STEP_COMP, STEP_COMP), :] = got[STEP_KEYS:]
        return jnp.max(near.reshape(STEP_KEYS // 8, 8, ROWS), axis=0)

    def weigh(local, stream, i, top):
        weight = jnp.exp2((scores[stream][pl.ds(i * STEP_KEYS, STEP_KEYS), :] - top) * EXP2_SCALE).astype(jnp.bfloat16)
        blocks = [block_of(local, b, TOK) for b in range(i * STEP_BLOCKS, (i + 1) * STEP_BLOCKS)]
        values = jnp.concatenate([jnp.concatenate(blocks, axis=0).T, ones], axis=0)
        return dot(values, weight)

    def finish(local, stream, mixed):
        result = (mixed[:DH] * (1.0 / mixed[DH : DH + 1])).astype(jnp.bfloat16).T
        at = spot(local)
        for dx in range(COLS):
            for j in range(2):
                r = (dx * 2 + j) * BLOCK
                outs[dx][j, at, :] = result[r : r + BLOCK]
        number = (2 * chip + (core + half) % 2) * TILES + local
        known = jnp.where(block_row <= number, logits[stream][...], -jnp.inf)
        raised = jnp.exp2((known - jnp.max(known, axis=0, keepdims=True)) * EXP2_SCALE)
        prob = raised * (1.0 / jnp.sum(raised, axis=0, keepdims=True))
        folded = prob[:, :128] + prob[:, 128:256] + prob[:, 256:384] + prob[:, 384:]
        factor = (number + 1).astype(jnp.float32) * (1.0 / (BLOCK * HPG))
        pooled[pl.ds(local, 1), :] = jnp.sum(folded.T, axis=0, keepdims=True) * factor

    def pair(this, stream, that, other):
        top = jnp.max(tops[stream][...], axis=0, keepdims=True)
        mixed, peak = None, None
        for i in range(STEPS):
            near = score(that, other, i)
            peak = near if peak is None else jnp.maximum(peak, near)
            got = weigh(this, stream, i, top)
            mixed = got if mixed is None else mixed + got
        tops[other][...] = peak
        finish(this, stream, mixed)

    def step(i, carry):
        even = 2 * i
        pair(even, 0, even + 1, 1)
        turn(jnp.minimum(even + 2, TILES - 2), 0)
        pair(even + 1, 1, jnp.minimum(even + 2, TILES - 2), 0)
        turn(jnp.minimum(even + 3, TILES - 1), 1)
        return carry

    turn(0, 0)
    turn(1, 1)
    for copy in copies:
        copy.wait()
    padded = [pool[pl.ds(s * PIECE + 2 * TOK, COMP_PAD), :] for s in range(SHARDS)]
    comp[...] = dot(take, jnp.concatenate(padded, axis=0)).astype(jnp.bfloat16)
    peak = score(0, 0, 0)
    for i in range(1, STEPS):
        peak = jnp.maximum(peak, score(0, 0, i))
    tops[0][...] = peak
    lax.fori_loop(0, TILES // 2, step, 0)


SMEM = pl.BlockSpec(memory_space=pltpu.SMEM)
VMEM = pl.BlockSpec(memory_space=pltpu.VMEM)
ANY = pl.BlockSpec(memory_space=pl.ANY)


def grant(mib):
    return pltpu.CompilerParams(vmem_limit_bytes=mib * 2**20)


def bf16(*shape):
    return jax.ShapeDtypeStruct(shape, jnp.bfloat16)


def call_split_pools(place, keys, values, comp):
    return pl.pallas_call(
        split_pools,
        in_specs=[SMEM, ANY, ANY, VMEM],
        out_specs=[VMEM, VMEM],
        out_shape=[bf16(PIECE, DH)] * 2,
        scratch_shapes=[pltpu.VMEM((2, TOK * GROUPS, DH), jnp.bfloat16), pltpu.SemaphoreType.DMA((2, LOADS))],
        name="split_pools",
    )(place, keys, values, comp)


def call_split_queries(place, queries):
    steps = 4
    tokens = TOK // steps
    return pl.pallas_call(
        functools.partial(split_queries, tokens),
        grid=(steps,),
        in_specs=[SMEM, pl.BlockSpec((tokens * 16, DH), lambda i: (i, 0))],
        out_specs=[pl.BlockSpec((2, tokens, DH), lambda i: (0, i, 0))] * PARTS,
        out_shape=[bf16(2, TOK, DH)] * PARTS,
        name="split_queries",
    )(place, queries)


def call_attend(half, place, picks, owns, pieces, queries):
    return pl.pallas_call(
        functools.partial(attend, half),
        in_specs=[SMEM] * 3 + [ANY] * (2 * CHIPS) + [VMEM] * COLS,
        out_specs=[VMEM] * (COLS + 1),
        out_shape=[bf16(2, TOK, DH)] * COLS + [jax.ShapeDtypeStruct((TILES, NBLK), jnp.float32)],
        scratch_shapes=[
            pltpu.VMEM((SHARDS * PIECE, DH), jnp.bfloat16),
            pltpu.VMEM((NBLK, DH), jnp.bfloat16),
            pltpu.VMEM((2 * BLOCK, DH), jnp.bfloat16),
        ]
        + [pltpu.VMEM((2 * DH, ROWS), jnp.bfloat16)] * 2
        + [pltpu.VMEM((KEYS, ROWS), jnp.float32)] * 2
        + [pltpu.VMEM((NBLK, ROWS), jnp.float32)] * 2
        + [pltpu.VMEM((8, ROWS), jnp.float32)] * 2
        + [pltpu.SemaphoreType.DMA((2 * CHIPS,))],
        compiler_params=grant(28),
        name="attend",
    )(place, picks, owns, *pieces, *[queries[2 * dx + half] for dx in range(COLS)])


def call_join_outputs(place, parts):
    return pl.pallas_call(
        join_outputs,
        in_specs=[SMEM] + [VMEM] * PARTS,
        out_specs=ANY,
        out_shape=bf16(TOK * 16, DH),
        scratch_shapes=[pltpu.VMEM((TOK * 16, DH), jnp.bfloat16), pltpu.SemaphoreType.DMA((TOK // 128,))],
        compiler_params=grant(16),
        name="join_outputs",
    )(place, *parts)


def by_seq(value, move):
    return lax.ppermute(value, "seq", [(s, move(s // 2, s % 2)) for s in range(SHARDS)])


def to_seq(chip, core):
    return chip % CHIPS * 2 + core % 2


def by_part(value, dx, dc, back):
    if dx == 0 and dc == 0:
        return value
    pairs = []
    for s in range(SHARDS):
        for x in range(COLS):
            there = (s ^ dc) * COLS + (x + dx) % COLS
            here = s * COLS + x
            pairs.append((there, here) if back else (here, there))
    return lax.ppermute(value, ("seq", "head"), pairs)


def whole(queries, key_rows, value_rows, compressed, chosen):
    seq = lax.axis_index("seq")
    col = lax.axis_index("head")
    chip, core = seq // 2, seq % 2
    place = jnp.stack([col, core, chip]).astype(jnp.int32)
    own, other = call_split_pools(
        place, key_rows.reshape(TOK * GROUPS, DH), value_rows.reshape(TOK * GROUPS, DH), compressed.reshape(TILES * GROUPS, DH)
    )
    pieces = [None] * (2 * CHIPS)
    pieces[0] = own
    pieces[1] = by_seq(other, lambda z, c: to_seq(z, c + 1))
    up, down = [own, other], [own, other]
    for k in range(1, 4):
        for h in range(2):
            turn = h if k == 1 else 0
            up[h] = by_seq(up[h], lambda z, c: to_seq(z + 1, c + turn))
            down[h] = by_seq(down[h], lambda z, c: to_seq(z - 1, c + turn))
            pieces[2 * (CHIPS - k) + h] = up[h]
            pieces[2 * k + h] = down[h]
    pieces[2 * 4] = by_seq(up[0], lambda z, c: to_seq(z + 1, c))
    pieces[2 * 4 + 1] = by_seq(down[1], lambda z, c: to_seq(z - 1, c))
    parts = call_split_queries(place, queries.reshape(TOK * 16, DH))
    moved = []
    for k in range(PARTS):
        moved.append(by_part(parts[k], k // 2, k % 2, False))
    groups = chosen[0].transpose(1, 0, 2)
    mine = lax.dynamic_index_in_dim(groups, 2 * col + core, 0, False)
    theirs = lax.dynamic_index_in_dim(groups, 2 * col + 1 - core, 0, False)
    theirs = by_seq(theirs, lambda z, c: to_seq(z, c + 1))
    blocks = jnp.stack([mine, theirs])
    shard = 2 * chip + (core + jnp.arange(2, dtype=jnp.int32)) % 2
    number = shard[:, None] * TILES + jnp.arange(TILES, dtype=jnp.int32)
    picks = (blocks // TILES * PIECE + blocks % TILES * BLOCK).reshape(-1)
    owns = jnp.where(blocks == number[..., None], BLOCK, 0).reshape(-1)
    joined, sums = [None] * PARTS, [None] * 2
    for half in HALVES:
        *outs, sums[half] = call_attend(half, place, picks, owns, pieces, moved)
        for dx in (2, 1, 3, 0):
            joined[2 * dx + half] = by_part(outs[dx], dx, half, True)
    came = by_seq(sums[1], lambda z, c: to_seq(z, c + 1))
    attended = call_join_outputs(place, joined)
    keep = sums[0]
    both = jnp.where(core == 0, jnp.stack([keep, came], axis=1), jnp.stack([came, keep], axis=1))
    return both[None], attended.reshape(1, TOK, 2, GROUPS, DH)


def solution(mesh):
    placed = (
        P("batch", "seq", "head", None, None),
        P("batch", "seq", None, None),
        P("batch", "seq", None, None),
        P("batch", "seq", None, None),
        P("batch", "seq", None, None),
    )
    return jax.shard_map(
        whole,
        mesh=mesh,
        in_specs=placed,
        out_specs=(P("batch", "seq", "head", None), P("batch", "seq", "head", None, None)),
        check_vma=False,
    )
```

time: 134 us -> 120 us (0.90)
  waiting for transfers between devices: 42.1 us -> 33.5 us
  starting transfers between devices: 44.6 us -> 42.2 us
  Pallas kernels: 32.4 us -> 30.5 us
    ppermute x14, waiting for transfers between devices: 26.8 us -> 21.4 us  [by_part(): return lax.ppermute(value, ('seq', 'head'), pairs)]
    pallas_call x4, Pallas kernels: 29.3 us -> 25.8 us  [the longest x2 20.2 us: call_attend(): pl.pallas_call(functools.partial(attend, half), in_specs=[SMEM] * 3 + [AN...]
    ppermute x17, waiting for transfers between devices: 15.3 us -> 12.1 us  [by_seq(): lax.ppermute(value, 'seq', [(s, move(s // 2, s % 2)) for s in range(SHARD...]
    ppermute x17, starting transfers between devices: 24.9 us -> 23.3 us  [by_seq(): lax.ppermute(value, 'seq', [(s, move(s // 2, s % 2)) for s in range(SHARD...]
    pallas_call x1, Pallas kernels: 3.14 us -> 4.65 us  [call_split_queries(): pl.pallas_call(functools.partial(split_queries, tokens), grid=(steps,), i...]
    unnamed x39 -> x31, local copies, waits for them, and re-layouts: 11.9 us -> 10.8 us
  transfers between devices with their start and end apart: 31 -> 31, of which waited for: 11 -> 13; matrix products, arithmetic and copies ran while one was open for 1% -> 1% of each run, Pallas kernels for 10% -> 21%
where the time goes in v3:
time: 120 us
  starting transfers between devices  42.2 us (35%)
  waiting for transfers between devices  33.5 us (28%)
  Pallas kernels  30.5 us (25%)
  local copies, waits for them, and re-layouts  11.9 us (10%)
    ppermute x17, starting transfers between devices, by_seq(): lax.ppermute(value, 'seq', [(s, move(s // 2, s % 2)) for s in range(SHARD...  23.3 us
    ppermute x14, waiting for transfers between devices, by_part(): return lax.ppermute(value, ('seq', 'head'), pairs)  21.4 us
    pallas_call x2, Pallas kernels, call_attend(): pl.pallas_call(functools.partial(attend, half), in_specs=[SMEM] * 3 + [AN...  20.2 us
    ppermute x14, starting transfers between devices, by_part(): return lax.ppermute(value, ('seq', 'head'), pairs)  18.9 us
    ppermute x17, waiting for transfers between devices, by_seq(): lax.ppermute(value, 'seq', [(s, move(s // 2, s % 2)) for s in range(SHARD...  12.1 us
    unnamed x31, local copies, waits for them, and re-layouts  10.8 us
    pallas_call x1, Pallas kernels, call_split_queries(): pl.pallas_call(functools.partial(split_queries, tokens), grid=(steps,), i...  4.65 us
    pallas_call x1, Pallas kernels, call_split_pools(): pl.pallas_call(split_pools, in_specs=[SMEM, ANY, ANY, VMEM], out_specs=[V...  3.46 us
  transfers between devices with their start and end apart: 31, of which 13 were waited for; matrix products, arithmetic and copies ran while one was open for 1% of the time, Pallas kernels for 21%

profile of v3, /device:TPU:1, one launch (start us, length us, event | category | flops | bytes accessed | tf_op | source)
XLA Modules:
  0.0 119.8 jit_solution(17016666263645374556)
XLA Ops:
  0.6 0.6 pad_add_fusion.1.place
  1.3 3.5 %split_pools.1 = (bf16[1040,128]{1,0:T(8,128)(2,1)}, bf16[1040,128]{1,0:T(8,128)(2,1)}) custom-call(s32[3]{0:T(128)} %pad_add_fusion.1.place, bf16[4096,128]{1,0:T(8,128)(2,1)} %bitcast.20, bf16[4096,128]{1,0:T(8,128)(2,1)} %bitcast.21, bf16[64,128]{1,0:T(8,128)(2,1)} %bitcast.22), custom_call_target="tpu_custom_call" | custom-call | tf_op jit(solution)/shard_map/split_pools/pallas_call | solution.py:251
  4.8 0.0 copy-start
  4.8 7.0 %collective-permute-start.3 = (bf16[1040,128]{1,0:T(8,128)(2,1)}, bf16[1040,128]{1,0:T(8,128)(2,1)S(1)}, u32[]{:S(2)}, u32[]{:S(2)}) collective-permute-start(bf16[1040,128]{1,0:T(8,128)(2,1)} %get-tuple-element.23), channel_id=1, source_target_pairs={{0,240},{16,224},{32,16},{48,0},{64,48},{80,32},{96,80},{112,64},{... | collective-permute-start | bytes 798728 | tf_op jit(solution)/shard_map/ppermute | solution.py:308
  11.8 4.7 %split_queries.1 = (bf16[2,512,128]{2,1,0:T(8,128)(2,1)}, bf16[2,512,128]{2,1,0:T(8,128)(2,1)}, bf16[2,512,128]{2,1,0:T(8,128)(2,1)}, bf16[2,512,128]{2,1,0:T(8,...) custom-call(s32[3]{0:T(128)} %pad_add_fusion.1.place, ...), custom_call_target="tpu_custom_call" | custom-call | tf_op jit(solution)/shard_map/split_queries/pallas_call | solution.py:264
  16.5 1.2 %collective-permute-start.16 = (bf16[2,512,128]{2,1,0:T(8,128)(2,1)}, bf16[2,512,128]{2,1,0:T(8,128)(2,1)S(1)}, u32[]{:S(2)}, u32[]{:S(2)}) collective-permute-start(bf16[2,512,128]{2,1,0:T(8,128)(2,1)} %get-tuple-element.25), channel_id=1, source_target_pairs={{0,4},{4,8},{8,12},{12,0},{16,20},{20,24},{24,28},{28,16},{32,36},... | collective-permute-start | bytes 786440 | tf_op jit(solution)/shard_map/ppermute | solution.py:324
  17.7 0.0 collective-permute-start.8
  17.7 2.4 %collective-permute-start.17 = (bf16[2,512,128]{2,1,0:T(8,128)(2,1)}, bf16[2,512,128]{2,1,0:T(8,128)(2,1)S(1)}, u32[]{:S(2)}, u32[]{:S(2)}) collective-permute-start(bf16[2,512,128]{2,1,0:T(8,128)(2,1)} %get-tuple-element.26), channel_id=1, source_target_pairs={{0,8},{4,12},{8,0},{12,4},{16,24},{20,28},{24,16},{28,20},{32,40},... | collective-permute-start | bytes 786440 | tf_op jit(solution)/shard_map/ppermute | solution.py:324
  20.2 0.8 constant_dynamic-slice_fusion.1
  21.0 0.5 collective-permute-start
  21.5 0.8 collective-permute-done
  22.3 3.6 %collective-permute-done.16.refs_17_ = bf16[2,512,128]{2,1,0:T(8,128)(2,1)S(1)} collective-permute-done((bf16[2,512,128]{2,1,0:T(8,128)(2,1)}, bf16[2,512,128]{2,1,0:T(8,128)(2,1)S(1)}, u32[]{:S(2)}, u32[]{:S(2)}) %collective-permute-start.16) | collective-permute-done | bytes 262176 | tf_op jit(solution)/shard_map/ppermute | solution.py:324
  25.9 0.7 copy-done.2
  26.6 0.7 collective-permute-start.2
  27.4 0.7 collective-permute-start.5
  28.1 0.7 collective-permute-start.9
  28.8 3.7 %collective-permute-done.17.refs_18_ = bf16[2,512,128]{2,1,0:T(8,128)(2,1)S(1)} collective-permute-done((bf16[2,512,128]{2,1,0:T(8,128)(2,1)}, bf16[2,512,128]{2,1,0:T(8,128)(2,1)S(1)}, u32[]{:S(2)}, u32[]{:S(2)}) %collective-permute-start.17) | collective-permute-done | bytes 262176 | tf_op jit(solution)/shard_map/ppermute | solution.py:324
  32.5 0.7 copy-done.4
  33.2 0.1 collective-permute-done.13.refs_15_
  33.3 0.6 collective-permute-done.2.refs_2_
  33.9 2.1 %collective-permute-start.4 = (bf16[1040,128]{1,0:T(8,128)(2,1)S(1)}, bf16[1040,128]{1,0:T(8,128)(2,1)S(1)}, u32[]{:S(2)}, u32[]{:S(2)}) collective-permute-start(bf16[1040,128]{1,0:T(8,128)(2,1)S(1)} %collective-permute-done.2.refs_2_), channel_id=1, source_target_pairs={{0,224},{16,240},{32,0},{48,16},{64,32},{80,48},{96,64},{112,80},{... | collective-permute-start | bytes 798728 | tf_op jit(solution)/shard_map/ppermute | solution.py:308
  36.0 3.6 %collective-permute-done.5.refs_5_ = bf16[1040,128]{1,0:T(8,128)(2,1)S(1)} collective-permute-done((bf16[1040,128]{1,0:T(8,128)(2,1)S(1)}, bf16[1040,128]{1,0:T(8,128)(2,1)S(1)}, u32[]{:S(2)}, u32[]{:S(2)}) %collective-permute-start.5) | collective-permute-done | bytes 266272 | tf_op jit(solution)/shard_map/ppermute | solution.py:308
  39.6 1.9 %collective-permute-start.7 = (bf16[1040,128]{1,0:T(8,128)(2,1)S(1)}, bf16[1040,128]{1,0:T(8,128)(2,1)S(1)}, u32[]{:S(2)}, u32[]{:S(2)}) collective-permute-start(bf16[1040,128]{1,0:T(8,128)(2,1)S(1)} %collective-permute-done.5.refs_5_), channel_id=1, source_target_pairs={{0,224},{16,240},{32,0},{48,16},{64,32},{80,48},{96,64},{112,80},{... | collective-permute-start | bytes 798728 | tf_op jit(solution)/shard_map/ppermute | solution.py:308
  41.5 0.7 copy-done.6
  42.2 3.0 %collective-permute-start.1 = (bf16[1040,128]{1,0:T(8,128)(2,1)}, bf16[1040,128]{1,0:T(8,128)(2,1)S(1)}, u32[]{:S(2)}, u32[]{:S(2)}) collective-permute-start(bf16[1040,128]{1,0:T(8,128)(2,1)} %get-tuple-element.23), channel_id=1, source_target_pairs={{0,16},{16,0},{32,48},{48,32},{64,80},{80,64},{96,112},{112,96},{1... | collective-permute-start | bytes 798728 | tf_op jit(solution)/shard_map/ppermute | solution.py:308
  45.2 0.3 collective-permute-start.15
  45.5 2.7 %collective-permute-start.6 = (bf16[1040,128]{1,0:T(8,128)(2,1)S(1)}, bf16[1040,128]{1,0:T(8,128)(2,1)}, u32[]{:S(2)}, u32[]{:S(2)}) collective-permute-start(bf16[1040,128]{1,0:T(8,128)(2,1)S(1)} %collective-permute-done.4.refs_4_), channel_id=1, source_target_pairs={{0,224},{16,240},{32,0},{48,16},{64,32},{80,48},{96,64},{112,80},{... | collective-permute-start | bytes 798728 | tf_op jit(solution)/shard_map/ppermute | solution.py:308
  48.3 2.7 %collective-permute-done.7.refs_7_ = bf16[1040,128]{1,0:T(8,128)(2,1)S(1)} collective-permute-done((bf16[1040,128]{1,0:T(8,128)(2,1)S(1)}, bf16[1040,128]{1,0:T(8,128)(2,1)S(1)}, u32[]{:S(2)}, u32[]{:S(2)}) %collective-permute-start.7) | collective-permute-done | bytes 266272 | tf_op jit(solution)/shard_map/ppermute | solution.py:308
  51.0 1.9 %collective-permute-start.12 = (bf16[1040,128]{1,0:T(8,128)(2,1)S(1)}, bf16[1040,128]{1,0:T(8,128)(2,1)}, u32[]{:S(2)}, u32[]{:S(2)}) collective-permute-start(bf16[1040,128]{1,0:T(8,128)(2,1)S(1)} %collective-permute-done.7.refs_7_), channel_id=1, source_target_pairs={{0,224},{16,240},{32,0},{48,16},{64,32},{80,48},{96,64},{112,80},{... | collective-permute-start | bytes 798728 | tf_op jit(solution)/shard_map/ppermute | solution.py:308
  53.0 0.1 iota_add_fusion
  53.0 0.1 eq.21
  53.1 0.1 eq.22
  53.2 3.1 %collective-permute-start.19 = (bf16[2,512,128]{2,1,0:T(8,128)(2,1)}, bf16[2,512,128]{2,1,0:T(8,128)(2,1)}, u32[]{:S(2)}, u32[]{:S(2)}) collective-permute-start(bf16[2,512,128]{2,1,0:T(8,128)(2,1)} %get-tuple-element.29), channel_id=1, source_target_pairs={{0,16},{4,20},{8,24},{12,28},{16,0},{20,4},{24,8},{28,12},{32,48},... | collective-permute-start | bytes 786440 | tf_op jit(solution)/shard_map/ppermute | solution.py:324
  56.3 0.1 stack.41
  56.3 3.7 %collective-permute-done.15.refs_11_ = bf16[1040,128]{1,0:T(8,128)(2,1)S(1)} collective-permute-done((bf16[1040,128]{1,0:T(8,128)(2,1)S(1)}, bf16[1040,128]{1,0:T(8,128)(2,1)S(1)}, u32[]{:S(2)}, u32[]{:S(2)}) %collective-permute-start.15) | collective-permute-done | bytes 266272 | tf_op jit(solution)/shard_map/ppermute | solution.py:308
  60.1 1.4 %collective-permute-start.20 = (bf16[2,512,128]{2,1,0:T(8,128)(2,1)}, bf16[2,512,128]{2,1,0:T(8,128)(2,1)S(1)}, u32[]{:S(2)}, u32[]{:S(2)}) collective-permute-start(bf16[2,512,128]{2,1,0:T(8,128)(2,1)} %get-tuple-element.30), channel_id=1, source_target_pairs={{0,20},{4,24},{8,28},{12,16},{16,4},{20,8},{24,12},{28,0},{32,52},... | collective-permute-start | bytes 786440 | tf_op jit(solution)/shard_map/ppermute | solution.py:324
  61.5 1.7 %collective-permute-start.21 = (bf16[2,512,128]{2,1,0:T(8,128)(2,1)}, bf16[2,512,128]{2,1,0:T(8,128)(2,1)S(1)}, u32[]{:S(2)}, u32[]{:S(2)}) collective-permute-start(bf16[2,512,128]{2,1,0:T(8,128)(2,1)} %get-tuple-element.31), channel_id=1, source_target_pairs={{0,24},{4,28},{8,16},{12,20},{16,8},{20,12},{24,0},{28,4},{32,56},... | collective-permute-start | bytes 786440 | tf_op jit(solution)/shard_map/ppermute | solution.py:324
  63.1 2.3 %collective-permute-start.22 = (bf16[2,512,128]{2,1,0:T(8,128)(2,1)}, bf16[2,512,128]{2,1,0:T(8,128)(2,1)S(1)}, u32[]{:S(2)}, u32[]{:S(2)}) collective-permute-start(bf16[2,512,128]{2,1,0:T(8,128)(2,1)} %get-tuple-element.32), channel_id=1, source_target_pairs={{0,28},{4,16},{8,20},{12,24},{16,12},{20,0},{24,4},{28,8},{32,60},... | collective-permute-start | bytes 786440 | tf_op jit(solution)/shard_map/ppermute | solution.py:324
  65.4 0.6 collective-permute-done.11.refs_8_
  66.0 0.9 copy-done.1
  66.9 0.9 copy-done.3
  67.9 0.9 copy-done.5
  68.8 0.9 copy-done.7
  69.8 9.8 %attend.2 = (bf16[2,512,128]{2,1,0:T(8,128)(2,1)S(1)}, bf16[2,512,128]{2,1,0:T(8,128)(2,1)S(1)}, bf16[2,512,128]{2,1,0:T(8,128)(2,1)S(1)}, bf16[2,512,128]{2,1,0:T(8,128)(2,1)}, f32[8,128]{1,0:T(8,128)S(1)}) custom-call(s32[3]{0:T(128)S(1)} %copy-done.14, s32[256]{0:T(256)S(1)} %get-tuple-element.47.picks, s32[256]{0:T(256)S(1)} %get-tuple-element.46.owns, ...), custom_call_target="tpu_custom_call" | custom-call | tf_op jit(solution)/shard_map/attend/pallas_call | solution.py:275
  79.6 1.7 %collective-permute-start.25 = (bf16[2,512,128]{2,1,0:T(8,128)(2,1)S(1)}, bf16[2,512,128]{2,1,0:T(8,128)(2,1)S(1)}, u32[]{:S(2)}, u32[]{:S(2)}) collective-permute-start(bf16[2,512,128]{2,1,0:T(8,128)(2,1)S(1)} %get-tuple-element.36), channel_id=1, source_target_pairs={{4,0},{8,4},{12,8},{0,12},{20,16},{24,20},{28,24},{16,28},{36,32},... | collective-permute-start | bytes 786440 | tf_op jit(solution)/shard_map/ppermute | solution.py:324
  81.3 0.5 collective-permute-start.27
  81.8 10.4 %attend.3 = (bf16[2,512,128]{2,1,0:T(8,128)(2,1)}, bf16[2,512,128]{2,1,0:T(8,128)(2,1)}, bf16[2,512,128]{2,1,0:T(8,128)(2,1)}, bf16[2,512,128]{2,1,0:T(8,128)(2,1)}, f32[8,128]{1,0:T(8,128)S(1)}) custom-call(s32[3]{0:T(128)S(1)} %copy-done.14, s32[256]{0:T(256)S(1)} %get-tuple-element.47.picks, s32[256]{0:T(256)S(1)} %get-tuple-element.46.owns, ...), custom_call_target="tpu_custom_call" | custom-call | tf_op jit(solution)/shard_map/attend/pallas_call | solution.py:275
  92.2 1.6 %collective-permute-start.23 = (f32[8,128]{1,0:T(8,128)S(1)}, f32[8,128]{1,0:T(8,128)S(1)}, u32[]{:S(2)}, u32[]{:S(2)}) collective-permute-start(f32[8,128]{1,0:T(8,128)S(1)} %get-tuple-element.33), channel_id=1, source_target_pairs={{0,16},{16,0},{32,48},{48,32},{64,80},{80,64},{96,112},{112,96},{1... | collective-permute-start | bytes 12296 | tf_op jit(solution)/shard_map/ppermute | solution.py:308
  93.8 0.7 collective-permute-start.29
  94.5 0.4 collective-permute-start.24
  94.9 2.0 %collective-permute-start.26 = (bf16[2,512,128]{2,1,0:T(8,128)(2,1)}, bf16[2,512,128]{2,1,0:T(8,128)(2,1)S(1)}, u32[]{:S(2)}, u32[]{:S(2)}) collective-permute-start(bf16[2,512,128]{2,1,0:T(8,128)(2,1)} %get-tuple-element.37), channel_id=1, source_target_pairs={{20,0},{24,4},{28,8},{16,12},{4,16},{8,20},{12,24},{0,28},{52,32},... | collective-permute-start | bytes 786440 | tf_op jit(solution)/shard_map/ppermute | solution.py:324
  96.9 0.7 copy-done.10
  97.6 1.6 %collective-permute-start.28 = (bf16[2,512,128]{2,1,0:T(8,128)(2,1)}, bf16[2,512,128]{2,1,0:T(8,128)(2,1)S(1)}, u32[]{:S(2)}, u32[]{:S(2)}) collective-permute-start(bf16[2,512,128]{2,1,0:T(8,128)(2,1)} %get-tuple-element.39), channel_id=1, source_target_pairs={{24,0},{28,4},{16,8},{20,12},{8,16},{12,20},{0,24},{4,28},{56,32},... | collective-permute-start | bytes 786440 | tf_op jit(solution)/shard_map/ppermute | solution.py:324
  99.1 0.7 copy-done.12
  99.9 0.1 collective-permute-start.30
  99.9 0.6 copy.9
  100.6 2.4 %collective-permute-done.29.refs_6_ = bf16[2,512,128]{2,1,0:T(8,128)(2,1)S(1)} collective-permute-done((bf16[2,512,128]{2,1,0:T(8,128)(2,1)}, bf16[2,512,128]{2,1,0:T(8,128)(2,1)S(1)}, u32[]{:S(2)}, u32[]{:S(2)}) %collective-permute-start.29) | collective-permute-done | bytes 262176 | tf_op jit(solution)/shard_map/ppermute | solution.py:324
  103.0 1.0 collective-permute-done.26.refs_3_
  104.0 5.8 %collective-permute-done.28.refs_5_ = bf16[2,512,128]{2,1,0:T(8,128)(2,1)S(1)} collective-permute-done((bf16[2,512,128]{2,1,0:T(8,128)(2,1)}, bf16[2,512,128]{2,1,0:T(8,128)(2,1)S(1)}, u32[]{:S(2)}, u32[]{:S(2)}) %collective-permute-start.28) | collective-permute-done | bytes 262176 | tf_op jit(solution)/shard_map/ppermute | solution.py:324
  109.8 4.8 %collective-permute-done.30.refs_7_ = bf16[2,512,128]{2,1,0:T(8,128)(2,1)S(1)} collective-permute-done((bf16[2,512,128]{2,1,0:T(8,128)(2,1)}, bf16[2,512,128]{2,1,0:T(8,128)(2,1)S(1)}, u32[]{:S(2)}, u32[]{:S(2)}) %collective-permute-start.30) | collective-permute-done | bytes 262176 | tf_op jit(solution)/shard_map/ppermute | solution.py:324
  114.6 0.9 copy-done.9
  115.6 0.9 copy-done.11
  116.5 0.9 copy-done.13
  117.5 2.2 %join_outputs.1 = bf16[8192,128]{1,0:T(8,128)(2,1)} custom-call(s32[3]{0:T(128)S(1)} %copy-done.14, bf16[2,512,128]{2,1,0:T(8,128)(2,1)S(1)} %copy-done.9, bf16[2,512,128]{2,1,0:T(8,128)(2,1)S(1)} %collective-permute-done.24.refs_1_, bf16[2,512,128]{2,1,0:T(8,128)(2,1)S(1)} %copy-done.11, bf16[2,512,128]{2,1,0:T(8,128)(2,1)S(1)} %collective-permute-done.26.refs_3_, ...), custom_call_target="tpu_custom_call" | custom-call | tf_op jit(solution)/shard_map/join_outputs/pallas_call | solution.py:296
  (44 shorter events, 0.1 us)
Async XLA Ops:
  1.3 64.7 %copy-start.14 = (s32[3]{0:T(128)S(1)}, s32[3]{0:T(128)}, u32[]{:S(2)}) copy-start(s32[3]{0:T(128)} %pad_add_fusion.1.place) | copy-start | bytes 40
  4.8 12.9 %copy-start = (bf16[1040,128]{1,0:T(8,128)(2,1)S(1)}, bf16[1040,128]{1,0:T(8,128)(2,1)}, u32[]{:S(2)}) copy-start(bf16[1040,128]{1,0:T(8,128)(2,1)} %get-tuple-element.22.refs_0_) | copy-start | bytes 798724
  4.8 22.6 %collective-permute-start.3 = (bf16[1040,128]{1,0:T(8,128)(2,1)}, bf16[1040,128]{1,0:T(8,128)(2,1)S(1)}, u32[]{:S(2)}, u32[]{:S(2)}) collective-permute-start(bf16[1040,128]{1,0:T(8,128)(2,1)} %get-tuple-element.23), channel_id=1, source_target_pairs={{0,240},{16,224},{32,16},{48,0},{64,48},{80,32},{96,80},{112,64},{... | collective-permute-start | bytes 798728 | tf_op jit(solution)/shard_map/ppermute | solution.py:308
  16.5 9.5 %collective-permute-start.16 = (bf16[2,512,128]{2,1,0:T(8,128)(2,1)}, bf16[2,512,128]{2,1,0:T(8,128)(2,1)S(1)}, u32[]{:S(2)}, u32[]{:S(2)}) collective-permute-start(bf16[2,512,128]{2,1,0:T(8,128)(2,1)} %get-tuple-element.25), channel_id=1, source_target_pairs={{0,4},{4,8},{8,12},{12,0},{16,20},{20,24},{24,28},{28,16},{32,36},... | collective-permute-start | bytes 786440 | tf_op jit(solution)/shard_map/ppermute | solution.py:324
  17.7 10.4 %collective-permute-start.8 = (bf16[1040,128]{1,0:T(8,128)(2,1)S(1)}, bf16[1040,128]{1,0:T(8,128)(2,1)S(1)}, u32[]{:S(2)}, u32[]{:S(2)}) collective-permute-start(bf16[1040,128]{1,0:T(8,128)(2,1)S(1)} %copy-done), channel_id=1, source_target_pairs={{0,32},{16,48},{32,64},{48,80},{64,96},{80,112},{96,128},{112,144}... | collective-permute-start | bytes 798728 | tf_op jit(solution)/shard_map/ppermute | solution.py:308
  17.7 14.8 %collective-permute-start.17 = (bf16[2,512,128]{2,1,0:T(8,128)(2,1)}, bf16[2,512,128]{2,1,0:T(8,128)(2,1)S(1)}, u32[]{:S(2)}, u32[]{:S(2)}) collective-permute-start(bf16[2,512,128]{2,1,0:T(8,128)(2,1)} %get-tuple-element.26), channel_id=1, source_target_pairs={{0,8},{4,12},{8,0},{12,4},{16,24},{20,28},{24,16},{28,20},{32,40},... | collective-permute-start | bytes 786440 | tf_op jit(solution)/shard_map/ppermute | solution.py:324
  21.0 1.3 %collective-permute-start = (s32[8,16]{1,0:T(8,128)S(1)}, s32[8,16]{1,0:T(8,128)S(1)}, u32[]{:S(2)}, u32[]{:S(2)}) collective-permute-start(s32[8,16]{1,0:T(8,128)S(1)} %bitcast.24), channel_id=1, source_target_pairs={{0,16},{16,0},{32,48},{48,32},{64,80},{80,64},{96,112},{112,96},{1... | collective-permute-start | bytes 1544 | tf_op jit(solution)/shard_map/ppermute | solution.py:308
  22.3 11.0 %collective-permute-start.13 = (bf16[1040,128]{1,0:T(8,128)(2,1)}, bf16[1040,128]{1,0:T(8,128)(2,1)S(1)}, u32[]{:S(2)}, u32[]{:S(2)}) collective-permute-start(bf16[1040,128]{1,0:T(8,128)(2,1)} %get-tuple-element.23), channel_id=1, source_target_pairs={{0,48},{16,32},{32,80},{48,64},{64,112},{80,96},{96,144},{112,128}... | collective-permute-start | bytes 798728 | tf_op jit(solution)/shard_map/ppermute | solution.py:308
  25.9 0.7 copy-start.2
  26.6 7.3 %collective-permute-start.2 = (bf16[1040,128]{1,0:T(8,128)(2,1)S(1)}, bf16[1040,128]{1,0:T(8,128)(2,1)S(1)}, u32[]{:S(2)}, u32[]{:S(2)}) collective-permute-start(bf16[1040,128]{1,0:T(8,128)(2,1)S(1)} %copy-done), channel_id=1, source_target_pairs={{0,224},{16,240},{32,0},{48,16},{64,32},{80,48},{96,64},{112,80},{... | collective-permute-start | bytes 798728 | tf_op jit(solution)/shard_map/ppermute | solution.py:308
  27.4 12.2 %collective-permute-start.5 = (bf16[1040,128]{1,0:T(8,128)(2,1)S(1)}, bf16[1040,128]{1,0:T(8,128)(2,1)S(1)}, u32[]{:S(2)}, u32[]{:S(2)}) collective-permute-start(bf16[1040,128]{1,0:T(8,128)(2,1)S(1)} %collective-permute-done.3.refs_3_), channel_id=1, source_target_pairs={{0,224},{16,240},{32,0},{48,16},{64,32},{80,48},{96,64},{112,80},{... | collective-permute-start | bytes 798728 | tf_op jit(solution)/shard_map/ppermute | solution.py:308
  28.1 17.1 %collective-permute-start.9 = (bf16[1040,128]{1,0:T(8,128)(2,1)S(1)}, bf16[1040,128]{1,0:T(8,128)(2,1)S(1)}, u32[]{:S(2)}, u32[]{:S(2)}) collective-permute-start(bf16[1040,128]{1,0:T(8,128)(2,1)S(1)} %collective-permute-done.8.refs_14_), channel_id=1, source_target_pairs={{0,32},{16,48},{32,64},{48,80},{64,96},{80,112},{96,128},{112,144}... | collective-permute-start | bytes 798728 | tf_op jit(solution)/shard_map/ppermute | solution.py:308
  32.5 0.7 copy-start.4
  33.2 8.3 %collective-permute-start.18 = (bf16[2,512,128]{2,1,0:T(8,128)(2,1)}, bf16[2,512,128]{2,1,0:T(8,128)(2,1)S(1)}, u32[]{:S(2)}, u32[]{:S(2)}) collective-permute-start(bf16[2,512,128]{2,1,0:T(8,128)(2,1)} %get-tuple-element.27), channel_id=1, source_target_pairs={{0,12},{4,0},{8,4},{12,8},{16,28},{20,16},{24,20},{28,24},{32,44},... | collective-permute-start | bytes 786440 | tf_op jit(solution)/shard_map/ppermute | solution.py:324
  33.3 11.9 %collective-permute-start.14 = (bf16[1040,128]{1,0:T(8,128)(2,1)S(1)}, bf16[1040,128]{1,0:T(8,128)(2,1)S(1)}, u32[]{:S(2)}, u32[]{:S(2)}) collective-permute-start(bf16[1040,128]{1,0:T(8,128)(2,1)S(1)} %collective-permute-done.13.refs_15_), channel_id=1, source_target_pairs={{0,32},{16,48},{32,64},{48,80},{64,96},{80,112},{96,128},{112,144}... | collective-permute-start | bytes 798728 | tf_op jit(solution)/shard_map/ppermute | solution.py:308
  33.9 11.6 %collective-permute-start.4 = (bf16[1040,128]{1,0:T(8,128)(2,1)S(1)}, bf16[1040,128]{1,0:T(8,128)(2,1)S(1)}, u32[]{:S(2)}, u32[]{:S(2)}) collective-permute-start(bf16[1040,128]{1,0:T(8,128)(2,1)S(1)} %collective-permute-done.2.refs_2_), channel_id=1, source_target_pairs={{0,224},{16,240},{32,0},{48,16},{64,32},{80,48},{96,64},{112,80},{... | collective-permute-start | bytes 798728 | tf_op jit(solution)/shard_map/ppermute | solution.py:308
  39.6 11.4 %collective-permute-start.7 = (bf16[1040,128]{1,0:T(8,128)(2,1)S(1)}, bf16[1040,128]{1,0:T(8,128)(2,1)S(1)}, u32[]{:S(2)}, u32[]{:S(2)}) collective-permute-start(bf16[1040,128]{1,0:T(8,128)(2,1)S(1)} %collective-permute-done.5.refs_5_), channel_id=1, source_target_pairs={{0,224},{16,240},{32,0},{48,16},{64,32},{80,48},{96,64},{112,80},{... | collective-permute-start | bytes 798728 | tf_op jit(solution)/shard_map/ppermute | solution.py:308
  41.5 0.7 copy-start.6
  42.2 10.9 %collective-permute-start.1 = (bf16[1040,128]{1,0:T(8,128)(2,1)}, bf16[1040,128]{1,0:T(8,128)(2,1)S(1)}, u32[]{:S(2)}, u32[]{:S(2)}) collective-permute-start(bf16[1040,128]{1,0:T(8,128)(2,1)} %get-tuple-element.23), channel_id=1, source_target_pairs={{0,16},{16,0},{32,48},{48,32},{64,80},{80,64},{96,112},{112,96},{1... | collective-permute-start | bytes 798728 | tf_op jit(solution)/shard_map/ppermute | solution.py:308
  45.2 11.0 %collective-permute-start.10 = (bf16[1040,128]{1,0:T(8,128)(2,1)S(1)}, bf16[1040,128]{1,0:T(8,128)(2,1)S(1)}, u32[]{:S(2)}, u32[]{:S(2)}) collective-permute-start(bf16[1040,128]{1,0:T(8,128)(2,1)S(1)} %collective-permute-done.9.refs_12_), channel_id=1, source_target_pairs={{0,32},{16,48},{32,64},{48,80},{64,96},{80,112},{96,128},{112,144}... | collective-permute-start | bytes 798728 | tf_op jit(solution)/shard_map/ppermute | solution.py:308
  45.2 14.8 %collective-permute-start.15 = (bf16[1040,128]{1,0:T(8,128)(2,1)S(1)}, bf16[1040,128]{1,0:T(8,128)(2,1)S(1)}, u32[]{:S(2)}, u32[]{:S(2)}) collective-permute-start(bf16[1040,128]{1,0:T(8,128)(2,1)S(1)} %collective-permute-done.14.refs_13_), channel_id=1, source_target_pairs={{0,32},{16,48},{32,64},{48,80},{64,96},{80,112},{96,128},{112,144}... | collective-permute-start | bytes 798728 | tf_op jit(solution)/shard_map/ppermute | solution.py:308
  45.5 15.9 %collective-permute-start.6 = (bf16[1040,128]{1,0:T(8,128)(2,1)S(1)}, bf16[1040,128]{1,0:T(8,128)(2,1)}, u32[]{:S(2)}, u32[]{:S(2)}) collective-permute-start(bf16[1040,128]{1,0:T(8,128)(2,1)S(1)} %collective-permute-done.4.refs_4_), channel_id=1, source_target_pairs={{0,224},{16,240},{32,0},{48,16},{64,32},{80,48},{96,64},{112,80},{... | collective-permute-start | bytes 798728 | tf_op jit(solution)/shard_map/ppermute | solution.py:308
  51.0 12.1 %collective-permute-start.12 = (bf16[1040,128]{1,0:T(8,128)(2,1)S(1)}, bf16[1040,128]{1,0:T(8,128)(2,1)}, u32[]{:S(2)}, u32[]{:S(2)}) collective-permute-start(bf16[1040,128]{1,0:T(8,128)(2,1)S(1)} %collective-permute-done.7.refs_7_), channel_id=1, source_target_pairs={{0,224},{16,240},{32,0},{48,16},{64,32},{80,48},{96,64},{112,80},{... | collective-permute-start | bytes 798728 | tf_op jit(solution)/shard_map/ppermute | solution.py:308
  53.2 28.1 %collective-permute-start.19 = (bf16[2,512,128]{2,1,0:T(8,128)(2,1)}, bf16[2,512,128]{2,1,0:T(8,128)(2,1)}, u32[]{:S(2)}, u32[]{:S(2)}) collective-permute-start(bf16[2,512,128]{2,1,0:T(8,128)(2,1)} %get-tuple-element.29), channel_id=1, source_target_pairs={{0,16},{4,20},{8,24},{12,28},{16,0},{20,4},{24,8},{28,12},{32,48},... | collective-permute-start | bytes 786440 | tf_op jit(solution)/shard_map/ppermute | solution.py:324
  56.3 9.7 %collective-permute-start.11 = (bf16[1040,128]{1,0:T(8,128)(2,1)S(1)}, bf16[1040,128]{1,0:T(8,128)(2,1)}, u32[]{:S(2)}, u32[]{:S(2)}) collective-permute-start(bf16[1040,128]{1,0:T(8,128)(2,1)S(1)} %collective-permute-done.10.refs_10_), channel_id=1, source_target_pairs={{0,32},{16,48},{32,64},{48,80},{64,96},{80,112},{96,128},{112,144}... | collective-permute-start | bytes 798728 | tf_op jit(solution)/shard_map/ppermute | solution.py:308
  60.1 21.7 %collective-permute-start.20 = (bf16[2,512,128]{2,1,0:T(8,128)(2,1)}, bf16[2,512,128]{2,1,0:T(8,128)(2,1)S(1)}, u32[]{:S(2)}, u32[]{:S(2)}) collective-permute-start(bf16[2,512,128]{2,1,0:T(8,128)(2,1)} %get-tuple-element.30), channel_id=1, source_target_pairs={{0,20},{4,24},{8,28},{12,16},{16,4},{20,8},{24,12},{28,0},{32,52},... | collective-permute-start | bytes 786440 | tf_op jit(solution)/shard_map/ppermute | solution.py:324
  61.5 20.3 %collective-permute-start.21 = (bf16[2,512,128]{2,1,0:T(8,128)(2,1)}, bf16[2,512,128]{2,1,0:T(8,128)(2,1)S(1)}, u32[]{:S(2)}, u32[]{:S(2)}) collective-permute-start(bf16[2,512,128]{2,1,0:T(8,128)(2,1)} %get-tuple-element.31), channel_id=1, source_target_pairs={{0,24},{4,28},{8,16},{12,20},{16,8},{20,12},{24,0},{28,4},{32,56},... | collective-permute-start | bytes 786440 | tf_op jit(solution)/shard_map/ppermute | solution.py:324
  63.1 18.7 %collective-permute-start.22 = (bf16[2,512,128]{2,1,0:T(8,128)(2,1)}, bf16[2,512,128]{2,1,0:T(8,128)(2,1)S(1)}, u32[]{:S(2)}, u32[]{:S(2)}) collective-permute-start(bf16[2,512,128]{2,1,0:T(8,128)(2,1)} %get-tuple-element.32), channel_id=1, source_target_pairs={{0,28},{4,16},{8,20},{12,24},{16,12},{20,0},{24,4},{28,8},{32,60},... | collective-permute-start | bytes 786440 | tf_op jit(solution)/shard_map/ppermute | solution.py:324
  66.0 1.0 copy-start.1
  66.9 0.9 copy-start.3
  67.9 0.9 copy-start.5
  68.8 0.9 copy-start.7
  79.6 12.5 %copy-start.8 = (bf16[2,512,128]{2,1,0:T(8,128)(2,1)}, bf16[2,512,128]{2,1,0:T(8,128)(2,1)S(1)}, u32[]{:S(2)}) copy-start(bf16[2,512,128]{2,1,0:T(8,128)(2,1)S(1)} %get-tuple-element.34.refs_0_) | copy-start | bytes 786436
  79.6 17.2 %collective-permute-start.25 = (bf16[2,512,128]{2,1,0:T(8,128)(2,1)S(1)}, bf16[2,512,128]{2,1,0:T(8,128)(2,1)S(1)}, u32[]{:S(2)}, u32[]{:S(2)}) collective-permute-start(bf16[2,512,128]{2,1,0:T(8,128)(2,1)S(1)} %get-tuple-element.36), channel_id=1, source_target_pairs={{4,0},{8,4},{12,8},{0,12},{20,16},{24,20},{28,24},{16,28},{36,32},... | collective-permute-start | bytes 786440 | tf_op jit(solution)/shard_map/ppermute | solution.py:324
  81.3 17.9 %collective-permute-start.27 = (bf16[2,512,128]{2,1,0:T(8,128)(2,1)S(1)}, bf16[2,512,128]{2,1,0:T(8,128)(2,1)S(1)}, u32[]{:S(2)}, u32[]{:S(2)}) collective-permute-start(bf16[2,512,128]{2,1,0:T(8,128)(2,1)S(1)} %get-tuple-element.38), channel_id=1, source_target_pairs={{8,0},{12,4},{0,8},{4,12},{24,16},{28,20},{16,24},{20,28},{40,32},... | collective-permute-start | bytes 786440 | tf_op jit(solution)/shard_map/ppermute | solution.py:324
  92.2 2.7 %collective-permute-start.23 = (f32[8,128]{1,0:T(8,128)S(1)}, f32[8,128]{1,0:T(8,128)S(1)}, u32[]{:S(2)}, u32[]{:S(2)}) collective-permute-start(f32[8,128]{1,0:T(8,128)S(1)} %get-tuple-element.33), channel_id=1, source_target_pairs={{0,16},{16,0},{32,48},{48,32},{64,80},{80,64},{96,112},{112,96},{1... | collective-permute-start | bytes 12296 | tf_op jit(solution)/shard_map/ppermute | solution.py:308
  93.8 9.2 %collective-permute-start.29 = (bf16[2,512,128]{2,1,0:T(8,128)(2,1)}, bf16[2,512,128]{2,1,0:T(8,128)(2,1)S(1)}, u32[]{:S(2)}, u32[]{:S(2)}) collective-permute-start(bf16[2,512,128]{2,1,0:T(8,128)(2,1)} %get-tuple-element.40), channel_id=1, source_target_pairs={{12,0},{0,4},{4,8},{8,12},{28,16},{16,20},{20,24},{24,28},{44,32},... | collective-permute-start | bytes 786440 | tf_op jit(solution)/shard_map/ppermute | solution.py:324
  94.5 8.5 %collective-permute-start.24 = (bf16[2,512,128]{2,1,0:T(8,128)(2,1)}, bf16[2,512,128]{2,1,0:T(8,128)(2,1)S(1)}, u32[]{:S(2)}, u32[]{:S(2)}) collective-permute-start(bf16[2,512,128]{2,1,0:T(8,128)(2,1)} %get-tuple-element.35), channel_id=1, source_target_pairs={{16,0},{20,4},{24,8},{28,12},{0,16},{4,20},{8,24},{12,28},{48,32},... | collective-permute-start | bytes 786440 | tf_op jit(solution)/shard_map/ppermute | solution.py:324
  94.9 9.1 %collective-permute-start.26 = (bf16[2,512,128]{2,1,0:T(8,128)(2,1)}, bf16[2,512,128]{2,1,0:T(8,128)(2,1)S(1)}, u32[]{:S(2)}, u32[]{:S(2)}) collective-permute-start(bf16[2,512,128]{2,1,0:T(8,128)(2,1)} %get-tuple-element.37), channel_id=1, source_target_pairs={{20,0},{24,4},{28,8},{16,12},{4,16},{8,20},{12,24},{0,28},{52,32},... | collective-permute-start | bytes 786440 | tf_op jit(solution)/shard_map/ppermute | solution.py:324
  96.9 0.7 copy-start.10
  97.6 12.2 %collective-permute-start.28 = (bf16[2,512,128]{2,1,0:T(8,128)(2,1)}, bf16[2,512,128]{2,1,0:T(8,128)(2,1)S(1)}, u32[]{:S(2)}, u32[]{:S(2)}) collective-permute-start(bf16[2,512,128]{2,1,0:T(8,128)(2,1)} %get-tuple-element.39), channel_id=1, source_target_pairs={{24,0},{28,4},{16,8},{20,12},{8,16},{12,20},{0,24},{4,28},{56,32},... | collective-permute-start | bytes 786440 | tf_op jit(solution)/shard_map/ppermute | solution.py:324
  99.1 0.7 copy-start.12
  99.9 14.7 %collective-permute-start.30 = (bf16[2,512,128]{2,1,0:T(8,128)(2,1)}, bf16[2,512,128]{2,1,0:T(8,128)(2,1)S(1)}, u32[]{:S(2)}, u32[]{:S(2)}) collective-permute-start(bf16[2,512,128]{2,1,0:T(8,128)(2,1)} %get-tuple-element.41), channel_id=1, source_target_pairs={{28,0},{16,4},{20,8},{24,12},{12,16},{0,20},{4,24},{8,28},{60,32},... | collective-permute-start | bytes 786440 | tf_op jit(solution)/shard_map/ppermute | solution.py:324
  114.6 1.0 copy-start.9
  115.6 0.9 copy-start.11
  116.5 0.9 copy-start.13

commit v4 on v3

--- a/solution.py
+++ b/solution.py
@@ -23,8 +23,7 @@
 COMP_PAD = 16
 PIECE = 2 * TOK + COMP_PAD
 PARTS = 8
-LOADS = 4
-HALVES = (1, 0)
+CHUNKS = ((1, 0, 8), (0, 0, 6), (0, 6, 2))
 KEYS = TOPN * BLOCK
 ROWS = HPG * BLOCK
 COMP_ROWS = SHARDS * COMP_PAD
@@ -49,22 +48,22 @@
     return jnp.where(cond, 1.0, 0.0).astype(jnp.bfloat16)
 
 
-def split_pools(place, keys, values, comp, own, other, stage, sems):
+def split_pools(place, keys, values, comp, own, other):
     mine = place[0] * 2 + place[1]
     theirs = place[0] * 2 + 1 - place[1]
-    size = TOK * GROUPS // LOADS
-    copies = []
-    for i in range(LOADS):
-        rows = pl.ds(i * size, size)
-        copies.append([pltpu.make_async_copy(ref.at[rows, :], stage.at[k, rows, :], sems.at[k, i]) for k, ref in enumerate((keys, values))])
-    for pair in copies:
-        for copy in pair:
-            copy.start()
     step = 32
     row = iota((2 * step, step * GROUPS), 0)
     col = iota((2 * step, step * GROUPS), 1)
     group = jnp.where(row < step, mine, theirs)
     pick = one_hot(col == (row % step) * GROUPS + group)
+    for i in range(TOK // step):
+        rows = pl.ds(i * step * GROUPS, step * GROUPS)
+        both = jnp.concatenate([keys[rows, :], values[rows, :]], axis=1)
+        got = dot(pick, both).astype(jnp.bfloat16)
+        own[pl.ds(i * step, step), :] = got[:step, :DH]
+        own[pl.ds(TOK + i * step, step), :] = got[:step, DH:]
+        other[pl.ds(i * step, step), :] = got[step:, :DH]
+        other[pl.ds(TOK + i * step, step), :] = got[step:, DH:]
     row = iota((2 * COMP_PAD, TILES * GROUPS), 0)
     col = iota((2 * COMP_PAD, TILES * GROUPS), 1)
     group = jnp.where(row < COMP_PAD, mine, theirs)
@@ -72,16 +71,6 @@
     got = dot(one_hot((col == block * GROUPS + group) & (block < TILES)), comp[...]).astype(jnp.bfloat16)
     own[pl.ds(2 * TOK, COMP_PAD), :] = got[:COMP_PAD]
     other[pl.ds(2 * TOK, COMP_PAD), :] = got[COMP_PAD:]
-    for i in range(TOK // step):
-        if i % (TOK // step // LOADS) == 0:
-            for copy in copies[i // (TOK // step // LOADS)]:
-                copy.wait()
-        rows = pl.ds(i * step * GROUPS, step * GROUPS)
-        got = dot(pick, jnp.concatenate([stage[0, rows, :], stage[1, rows, :]], axis=1)).astype(jnp.bfloat16)
-        own[pl.ds(i * step, step), :] = got[:step, :DH]
-        own[pl.ds(TOK + i * step, step), :] = got[:step, DH:]
-        other[pl.ds(i * step, step), :] = got[step:, :DH]
-        other[pl.ds(TOK + i * step, step), :] = got[step:, DH:]
 
 
 def row_of(r, place):
@@ -106,15 +95,23 @@
 
 
 def join_outputs(place, *refs):
-    parts, (out, result, sems) = refs[:PARTS], refs[PARTS:]
+    *parts, out, result, sems = refs
+    chunks = [parts[c * COLS : (c + 1) * COLS] for c in range(len(CHUNKS))]
+
+    def some(k, j, token):
+        for (half, begin, count), group in zip(CHUNKS, chunks):
+            at = token - begin * BLOCK
+            if half == k % 2 and 0 <= at < count * BLOCK:
+                return group[k // 2][j, pl.ds(at, 16), :]
+
     shape = (256, 256)
     pick = one_hot(iota(shape, 0) == row_of(iota(shape, 1), place))
     copies = []
     for i in range(TOK // 32):
         halves = []
         for h in range(2):
-            at = pl.ds(i * 32 + h * 16, 16)
-            halves.append(jnp.concatenate([parts[k][j, at, :] for k in range(PARTS) for j in range(2)], axis=0))
+            token = i * 32 + h * 16
+            halves.append(jnp.concatenate([some(k, j, token) for k in range(PARTS) for j in range(2)], axis=0))
         got = dot(pick, jnp.concatenate(halves, axis=1)).astype(jnp.bfloat16)
         result[pl.ds(i * 512, 256), :] = got[:, :DH]
         result[pl.ds(i * 512 + 256, 256), :] = got[:, DH:]
@@ -126,7 +123,7 @@
         copy.wait()
 
 
-def attend(half, place, picks, owns, *refs):
+def attend(half, begin, count, place, picks, owns, *refs):
     pieces, refs = refs[: 2 * CHIPS], refs[2 * CHIPS :]
     queries, refs = refs[:COLS], refs[COLS:]
     outs, refs = refs[:COLS], refs[COLS:]
@@ -154,7 +151,7 @@
     ones = jnp.full((ONES, STEP_KEYS), 1.0, jnp.bfloat16)
 
     def spot(local):
-        return pl.ds(pl.multiple_of(local * BLOCK, BLOCK), BLOCK)
+        return pl.ds(local * BLOCK if isinstance(local, int) else pl.multiple_of(local * BLOCK, BLOCK), BLOCK)
 
     def block_of(local, b, offset):
         start = picks[(half * TILES + local) * TOPN + b] + offset
@@ -189,7 +186,7 @@
 
     def finish(local, stream, mixed):
         result = (mixed[:DH] * (1.0 / mixed[DH : DH + 1])).astype(jnp.bfloat16).T
-        at = spot(local)
+        at = spot(local - begin)
         for dx in range(COLS):
             for j in range(2):
                 r = (dx * 2 + j) * BLOCK
@@ -199,39 +196,45 @@
         raised = jnp.exp2((known - jnp.max(known, axis=0, keepdims=True)) * EXP2_SCALE)
         prob = raised * (1.0 / jnp.sum(raised, axis=0, keepdims=True))
         folded = prob[:, :128] + prob[:, 128:256] + prob[:, 256:384] + prob[:, 384:]
-        factor = (number + 1).astype(jnp.float32) * (1.0 / (BLOCK * HPG))
-        pooled[pl.ds(local, 1), :] = jnp.sum(folded.T, axis=0, keepdims=True) * factor
+        factor = jnp.asarray(number + 1).astype(jnp.float32) * (1.0 / (BLOCK * HPG))
+        pooled[pl.ds(local - begin, 1), :] = jnp.sum(folded.T, axis=0, keepdims=True) * factor
 
     def pair(this, stream, that, other):
         top = jnp.max(tops[stream][...], axis=0, keepdims=True)
         mixed, peak = None, None
         for i in range(STEPS):
-            near = score(that, other, i)
-            peak = near if peak is None else jnp.maximum(peak, near)
+            if that is not None:
+                near = score(that, other, i)
+                peak = near if peak is None else jnp.maximum(peak, near)
             got = weigh(this, stream, i, top)
             mixed = got if mixed is None else mixed + got
-        tops[other][...] = peak
+        if that is not None:
+            tops[other][...] = peak
         finish(this, stream, mixed)
 
     def step(i, carry):
-        even = 2 * i
+        even = begin + 2 * i
         pair(even, 0, even + 1, 1)
-        turn(jnp.minimum(even + 2, TILES - 2), 0)
-        pair(even + 1, 1, jnp.minimum(even + 2, TILES - 2), 0)
-        turn(jnp.minimum(even + 3, TILES - 1), 1)
+        turn(even + 2, 0)
+        pair(even + 1, 1, even + 2, 0)
+        turn(even + 3, 1)
         return carry
 
-    turn(0, 0)
-    turn(1, 1)
+    last = begin + count - 2
+    turn(begin, 0)
+    turn(begin + 1, 1)
     for copy in copies:
         copy.wait()
     padded = [pool[pl.ds(s * PIECE + 2 * TOK, COMP_PAD), :] for s in range(SHARDS)]
     comp[...] = dot(take, jnp.concatenate(padded, axis=0)).astype(jnp.bfloat16)
-    peak = score(0, 0, 0)
+    peak = score(begin, 0, 0)
     for i in range(1, STEPS):
-        peak = jnp.maximum(peak, score(0, 0, i))
+        peak = jnp.maximum(peak, score(begin, 0, i))
     tops[0][...] = peak
-    lax.fori_loop(0, TILES // 2, step, 0)
+    if count > 2:
+        lax.fori_loop(0, count // 2 - 1, step, 0)
+    pair(last, 0, last + 1, 1)
+    pair(last + 1, 1, None, 0)
 
 
 SMEM = pl.BlockSpec(memory_space=pltpu.SMEM)
@@ -250,10 +253,9 @@
 def call_split_pools(place, keys, values, comp):
     return pl.pallas_call(
         split_pools,
-        in_specs=[SMEM, ANY, ANY, VMEM],
+        in_specs=[SMEM, VMEM, VMEM, VMEM],
         out_specs=[VMEM, VMEM],
         out_shape=[bf16(PIECE, DH)] * 2,
-        scratch_shapes=[pltpu.VMEM((2, TOK * GROUPS, DH), jnp.bfloat16), pltpu.SemaphoreType.DMA((2, LOADS))],
         name="split_pools",
     )(place, keys, values, comp)
 
@@ -271,12 +273,12 @@
     )(place, queries)
 
 
-def call_attend(half, place, picks, owns, pieces, queries):
+def call_attend(half, begin, count, place, picks, owns, pieces, queries):
     return pl.pallas_call(
-        functools.partial(attend, half),
+        functools.partial(attend, half, begin, count),
         in_specs=[SMEM] * 3 + [ANY] * (2 * CHIPS) + [VMEM] * COLS,
         out_specs=[VMEM] * (COLS + 1),
-        out_shape=[bf16(2, TOK, DH)] * COLS + [jax.ShapeDtypeStruct((TILES, NBLK), jnp.float32)],
+        out_shape=[bf16(2, count * BLOCK, DH)] * COLS + [jax.ShapeDtypeStruct((count, NBLK), jnp.float32)],
         scratch_shapes=[
             pltpu.VMEM((SHARDS * PIECE, DH), jnp.bfloat16),
             pltpu.VMEM((NBLK, DH), jnp.bfloat16),
@@ -295,7 +297,7 @@
 def call_join_outputs(place, parts):
     return pl.pallas_call(
         join_outputs,
-        in_specs=[SMEM] + [VMEM] * PARTS,
+        in_specs=[SMEM] + [VMEM] * len(parts),
         out_specs=ANY,
         out_shape=bf16(TOK * 16, DH),
         scratch_shapes=[pltpu.VMEM((TOK * 16, DH), jnp.bfloat16), pltpu.SemaphoreType.DMA((TOK // 128,))],
@@ -358,14 +360,17 @@
     number = shard[:, None] * TILES + jnp.arange(TILES, dtype=jnp.int32)
     picks = (blocks // TILES * PIECE + blocks % TILES * BLOCK).reshape(-1)
     owns = jnp.where(blocks == number[..., None], BLOCK, 0).reshape(-1)
-    joined, sums = [None] * PARTS, [None] * 2
-    for half in HALVES:
-        *outs, sums[half] = call_attend(half, place, picks, owns, pieces, moved)
+    joined, sums = [], []
+    for half, begin, count in CHUNKS:
+        *outs, rows = call_attend(half, begin, count, place, picks, owns, pieces, moved)
+        back = [None] * COLS
         for dx in (2, 1, 3, 0):
-            joined[2 * dx + half] = by_part(outs[dx], dx, half, True)
-    came = by_seq(sums[1], lambda z, c: to_seq(z, c + 1))
+            back[dx] = by_part(outs[dx], dx, half, True)
+        joined += back
+        sums.append(rows)
+    came = by_seq(sums[0], lambda z, c: to_seq(z, c + 1))
     attended = call_join_outputs(place, joined)
-    keep = sums[0]
+    keep = jnp.concatenate(sums[1:])
     both = jnp.where(core == 0, jnp.stack([keep, came], axis=1), jnp.stack([came, keep], axis=1))
     return both[None], attended.reshape(1, TOK, 2, GROUPS, DH)
 

time: 120 us -> 127 us (1.058)
  starting transfers between devices: 42.2 us -> 47.6 us
  waiting for transfers between devices: 33.5 us -> 35.2 us
    ppermute x14 -> x17, starting transfers between devices: 18.9 us -> 25.3 us  [by_part(): return lax.ppermute(value, ('seq', 'head'), pairs)]
    ppermute x14 -> x17, waiting for transfers between devices: 21.4 us -> 24.4 us  [by_part(): return lax.ppermute(value, ('seq', 'head'), pairs)]
    ppermute x17, waiting for transfers between devices: 12.1 us -> 10.8 us  [by_seq(): lax.ppermute(value, 'seq', [(s, move(s // 2, s % 2)) for s in range(SHARD...]
    pallas_call x4 -> x5, Pallas kernels: 25.8 us -> 26.3 us  [the longest x3 20.9 us: call_attend(): pl.pallas_call(functools.partial(attend, half, begin, count), in_specs=[S...]
    unnamed x31 -> x37, local copies, waits for them, and re-layouts: 10.8 us -> 10.4 us
  transfers between devices with their start and end apart: 31 -> 34, of which waited for: 13 -> 9; matrix products, arithmetic and copies ran while one was open for 1% -> 1% of each run, Pallas kernels for 21% -> 20%
where the time goes in v4:
time: 127 us
  starting transfers between devices  47.6 us (37%)
  waiting for transfers between devices  35.2 us (28%)
  Pallas kernels  30.8 us (24%)
  local copies, waits for them, and re-layouts  11.5 us (9%)
    ppermute x17, starting transfers between devices, by_part(): return lax.ppermute(value, ('seq', 'head'), pairs)  25.3 us
    ppermute x17, waiting for transfers between devices, by_part(): return lax.ppermute(value, ('seq', 'head'), pairs)  24.4 us
    ppermute x17, starting transfers between devices, by_seq(): lax.ppermute(value, 'seq', [(s, move(s // 2, s % 2)) for s in range(SHARD...  22.3 us
    pallas_call x3, Pallas kernels, call_attend(): pl.pallas_call(functools.partial(attend, half, begin, count), in_specs=[S...  20.9 us
    ppermute x17, waiting for transfers between devices, by_seq(): lax.ppermute(value, 'seq', [(s, move(s // 2, s % 2)) for s in range(SHARD...  10.8 us
    unnamed x37, local copies, waits for them, and re-layouts  10.4 us
    pallas_call x1, Pallas kernels, call_split_queries(): pl.pallas_call(functools.partial(split_queries, tokens), grid=(steps,), i...  4.56 us
    pallas_call x1, Pallas kernels, call_split_pools(): pl.pallas_call(split_pools, in_specs=[SMEM, VMEM, VMEM, VMEM], out_specs=...  2.84 us
  transfers between devices with their start and end apart: 34, of which 9 were waited for; matrix products, arithmetic and copies ran while one was open for 1% of the time, Pallas kernels for 20%

profile of v4, /device:TPU:1, one launch (start us, length us, event | category | flops | bytes accessed | tf_op | source)
XLA Modules:
  0.0 126.8 jit_solution(3522288274083426256)
XLA Ops:
  0.6 0.6 pad_add_fusion.1.place
  1.2 2.8 %split_pools.1 = (bf16[1040,128]{1,0:T(8,128)(2,1)}, bf16[1040,128]{1,0:T(8,128)(2,1)}) custom-call(s32[3]{0:T(128)} %pad_add_fusion.1.place, bf16[4096,128]{1,0:T(8,128)(2,1)} %bitcast.20, bf16[4096,128]{1,0:T(8,128)(2,1)} %bitcast.21, bf16[64,128]{1,0:T(8,128)(2,1)} %bitcast.22), custom_call_target="tpu_custom_call" | custom-call | tf_op jit(solution)/shard_map/split_pools/pallas_call | solution.py:254
  4.1 7.0 %collective-permute-start.3 = (bf16[1040,128]{1,0:T(8,128)(2,1)}, bf16[1040,128]{1,0:T(8,128)(2,1)S(1)}, u32[]{:S(2)}, u32[]{:S(2)}) collective-permute-start(bf16[1040,128]{1,0:T(8,128)(2,1)} %get-tuple-element.28), channel_id=1, source_target_pairs={{0,240},{16,224},{32,16},{48,0},{64,48},{80,32},{96,80},{112,64},{... | collective-permute-start | bytes 798728 | tf_op jit(solution)/shard_map/ppermute | solution.py:310
  11.0 4.6 %split_queries.1 = (bf16[2,512,128]{2,1,0:T(8,128)(2,1)}, bf16[2,512,128]{2,1,0:T(8,128)(2,1)}, bf16[2,512,128]{2,1,0:T(8,128)(2,1)}, bf16[2,512,128]{2,1,0:T(8,...) custom-call(s32[3]{0:T(128)} %pad_add_fusion.1.place, ...), custom_call_target="tpu_custom_call" | custom-call | tf_op jit(solution)/shard_map/split_queries/pallas_call | solution.py:266
  15.6 1.3 collective-permute-start.16
  16.9 0.0 collective-permute-start.8
  16.9 0.8 constant_dynamic-slice_fusion.1
  17.7 0.2 collective-permute-start
  17.9 0.0 collective-permute-start.13
  17.9 1.1 collective-permute-done
  19.0 2.7 %collective-permute-start.2 = (bf16[1040,128]{1,0:T(8,128)(2,1)S(1)}, bf16[1040,128]{1,0:T(8,128)(2,1)S(1)}, u32[]{:S(2)}, u32[]{:S(2)}) collective-permute-start(bf16[1040,128]{1,0:T(8,128)(2,1)S(1)} %copy-done), channel_id=1, source_target_pairs={{0,224},{16,240},{32,0},{48,16},{64,32},{80,48},{96,64},{112,80},{... | collective-permute-start | bytes 798728 | tf_op jit(solution)/shard_map/ppermute | solution.py:310
  21.7 0.7 collective-permute-start.5
  22.3 2.8 %collective-permute-done.16.refs_17_ = bf16[2,512,128]{2,1,0:T(8,128)(2,1)S(1)} collective-permute-done((bf16[2,512,128]{2,1,0:T(8,128)(2,1)}, bf16[2,512,128]{2,1,0:T(8,128)(2,1)S(1)}, u32[]{:S(2)}, u32[]{:S(2)}) %collective-permute-start.16) | collective-permute-done | bytes 262176 | tf_op jit(solution)/shard_map/ppermute | solution.py:326
  25.1 0.7 copy-done.3
  25.8 1.5 %collective-permute-start.17 = (bf16[2,512,128]{2,1,0:T(8,128)(2,1)}, bf16[2,512,128]{2,1,0:T(8,128)(2,1)S(1)}, u32[]{:S(2)}, u32[]{:S(2)}) collective-permute-start(bf16[2,512,128]{2,1,0:T(8,128)(2,1)} %get-tuple-element.31), channel_id=1, source_target_pairs={{0,8},{4,12},{8,0},{12,4},{16,24},{20,28},{24,16},{28,20},{32,40},... | collective-permute-start | bytes 786440 | tf_op jit(solution)/shard_map/ppermute | solution.py:326
  27.3 5.4 %collective-permute-done.13.refs_15_ = bf16[1040,128]{1,0:T(8,128)(2,1)S(1)} collective-permute-done((bf16[1040,128]{1,0:T(8,128)(2,1)}, bf16[1040,128]{1,0:T(8,128)(2,1)S(1)}, u32[]{:S(2)}, u32[]{:S(2)}) %collective-permute-start.13) | collective-permute-done | bytes 266272 | tf_op jit(solution)/shard_map/ppermute | solution.py:310
  32.8 2.7 %collective-permute-start.4 = (bf16[1040,128]{1,0:T(8,128)(2,1)S(1)}, bf16[1040,128]{1,0:T(8,128)(2,1)S(1)}, u32[]{:S(2)}, u32[]{:S(2)}) collective-permute-start(bf16[1040,128]{1,0:T(8,128)(2,1)S(1)} %collective-permute-done.2.refs_2_), channel_id=1, source_target_pairs={{0,224},{16,240},{32,0},{48,16},{64,32},{80,48},{96,64},{112,80},{... | collective-permute-start | bytes 798728 | tf_op jit(solution)/shard_map/ppermute | solution.py:310
  35.4 0.8 collective-permute-start.7
  36.2 0.7 copy-done.6
  36.9 1.5 %collective-permute-start.18 = (bf16[2,512,128]{2,1,0:T(8,128)(2,1)}, bf16[2,512,128]{2,1,0:T(8,128)(2,1)S(1)}, u32[]{:S(2)}, u32[]{:S(2)}) collective-permute-start(bf16[2,512,128]{2,1,0:T(8,128)(2,1)} %get-tuple-element.32), channel_id=1, source_target_pairs={{0,12},{4,0},{8,4},{12,8},{16,28},{20,16},{24,20},{28,24},{32,44},... | collective-permute-start | bytes 786440 | tf_op jit(solution)/shard_map/ppermute | solution.py:326
  38.4 0.7 collective-permute-start.10
  39.1 4.4 %collective-permute-done.18.refs_19_ = bf16[2,512,128]{2,1,0:T(8,128)(2,1)S(1)} collective-permute-done((bf16[2,512,128]{2,1,0:T(8,128)(2,1)}, bf16[2,512,128]{2,1,0:T(8,128)(2,1)S(1)}, u32[]{:S(2)}, u32[]{:S(2)}) %collective-permute-start.18) | collective-permute-done | bytes 262176 | tf_op jit(solution)/shard_map/ppermute | solution.py:326
  43.5 0.7 copy-done.9
  44.2 2.3 %collective-permute-start.1 = (bf16[1040,128]{1,0:T(8,128)(2,1)}, bf16[1040,128]{1,0:T(8,128)(2,1)S(1)}, u32[]{:S(2)}, u32[]{:S(2)}) collective-permute-start(bf16[1040,128]{1,0:T(8,128)(2,1)} %get-tuple-element.28), channel_id=1, source_target_pairs={{0,16},{16,0},{32,48},{48,32},{64,80},{80,64},{96,112},{112,96},{1... | collective-permute-start | bytes 798728 | tf_op jit(solution)/shard_map/ppermute | solution.py:310
  46.5 0.7 collective-permute-start.15
  47.2 2.0 %collective-permute-start.6 = (bf16[1040,128]{1,0:T(8,128)(2,1)S(1)}, bf16[1040,128]{1,0:T(8,128)(2,1)}, u32[]{:S(2)}, u32[]{:S(2)}) collective-permute-start(bf16[1040,128]{1,0:T(8,128)(2,1)S(1)} %collective-permute-done.4.refs_4_), channel_id=1, source_target_pairs={{0,224},{16,240},{32,0},{48,16},{64,32},{80,48},{96,64},{112,80},{... | collective-permute-start | bytes 798728 | tf_op jit(solution)/shard_map/ppermute | solution.py:310
  49.2 1.5 %collective-permute-start.12 = (bf16[1040,128]{1,0:T(8,128)(2,1)S(1)}, bf16[1040,128]{1,0:T(8,128)(2,1)}, u32[]{:S(2)}, u32[]{:S(2)}) collective-permute-start(bf16[1040,128]{1,0:T(8,128)(2,1)S(1)} %collective-permute-done.7.refs_7_), channel_id=1, source_target_pairs={{0,224},{16,240},{32,0},{48,16},{64,32},{80,48},{96,64},{112,80},{... | collective-permute-start | bytes 798728 | tf_op jit(solution)/shard_map/ppermute | solution.py:310
  50.7 0.1 iota_add_fusion
  50.8 0.1 eq.21
  50.9 0.1 eq.22
  51.0 0.1 collective-permute-start.11
  51.1 0.1 stack.41
  51.2 1.1 collective-permute-start.19
  52.3 3.4 %collective-permute-done.15.refs_11_ = bf16[1040,128]{1,0:T(8,128)(2,1)S(1)} collective-permute-done((bf16[1040,128]{1,0:T(8,128)(2,1)S(1)}, bf16[1040,128]{1,0:T(8,128)(2,1)S(1)}, u32[]{:S(2)}, u32[]{:S(2)}) %collective-permute-start.15) | collective-permute-done | bytes 266272 | tf_op jit(solution)/shard_map/ppermute | solution.py:310
  55.7 2.4 %collective-permute-start.20 = (bf16[2,512,128]{2,1,0:T(8,128)(2,1)}, bf16[2,512,128]{2,1,0:T(8,128)(2,1)S(1)}, u32[]{:S(2)}, u32[]{:S(2)}) collective-permute-start(bf16[2,512,128]{2,1,0:T(8,128)(2,1)} %get-tuple-element.36), channel_id=1, source_target_pairs={{0,20},{4,24},{8,28},{12,16},{16,4},{20,8},{24,12},{28,0},{32,52},... | collective-permute-start | bytes 786440 | tf_op jit(solution)/shard_map/ppermute | solution.py:326
  58.1 1.7 %collective-permute-start.21 = (bf16[2,512,128]{2,1,0:T(8,128)(2,1)}, bf16[2,512,128]{2,1,0:T(8,128)(2,1)S(1)}, u32[]{:S(2)}, u32[]{:S(2)}) collective-permute-start(bf16[2,512,128]{2,1,0:T(8,128)(2,1)} %get-tuple-element.37), channel_id=1, source_target_pairs={{0,24},{4,28},{8,16},{12,20},{16,8},{20,12},{24,0},{28,4},{32,56},... | collective-permute-start | bytes 786440 | tf_op jit(solution)/shard_map/ppermute | solution.py:326
  59.8 0.9 collective-permute-done.12.refs_9_
  60.7 3.7 %collective-permute-start.22 = (bf16[2,512,128]{2,1,0:T(8,128)(2,1)}, bf16[2,512,128]{2,1,0:T(8,128)(2,1)S(1)}, u32[]{:S(2)}, u32[]{:S(2)}) collective-permute-start(bf16[2,512,128]{2,1,0:T(8,128)(2,1)} %get-tuple-element.38), channel_id=1, source_target_pairs={{0,28},{4,16},{8,20},{12,24},{16,12},{20,0},{24,4},{28,8},{32,60},... | collective-permute-start | bytes 786440 | tf_op jit(solution)/shard_map/ppermute | solution.py:326
  64.5 0.9 copy-done.1
  65.4 0.9 copy-done.4
  66.4 0.9 copy-done.7
  67.3 0.9 copy-done.10
  68.3 7.4 %attend.3 = (bf16[2,384,128]{2,1,0:T(8,128)(2,1)S(1)}, bf16[2,384,128]{2,1,0:T(8,128)(2,1)S(1)}, bf16[2,384,128]{2,1,0:T(8,128)(2,1)}, bf16[2,384,128]{2,1,0:T(8,128)(2,1)S(1)}, f32[6,128]{1,0:T(8,128)S(1)}) custom-call(s32[3]{0:T(128)S(1)} %copy-done.16, s32[256]{0:T(256)S(1)} %get-tuple-element.57.picks, s32[256]{0:T(256)S(1)} %get-tuple-element.56.owns, ...), custom_call_target="tpu_custom_call" | custom-call | tf_op jit(solution)/shard_map/attend/pallas_call | solution.py:277
  75.7 0.7 copy-done.12
  76.4 0.7 copy-done.17
  77.1 0.8 collective-permute-start.29
  78.0 9.2 %attend.5 = (bf16[2,512,128]{2,1,0:T(8,128)(2,1)}, bf16[2,512,128]{2,1,0:T(8,128)(2,1)}, bf16[2,512,128]{2,1,0:T(8,128)(2,1)}, bf16[2,512,128]{2,1,0:T(8,128)(2,1)}, f32[8,128]{1,0:T(8,128)S(1)}) custom-call(s32[3]{0:T(128)S(1)} %copy-done.16, s32[256]{0:T(256)S(1)} %get-tuple-element.57.picks, s32[256]{0:T(256)S(1)} %get-tuple-element.56.owns, ...), custom_call_target="tpu_custom_call" | custom-call | tf_op jit(solution)/shard_map/attend/pallas_call | solution.py:277
  87.2 1.0 collective-permute-start.23
  88.2 4.2 %attend.4 = (bf16[2,128,128]{2,1,0:T(8,128)(2,1)S(1)}, bf16[2,128,128]{2,1,0:T(8,128)(2,1)S(1)}, bf16[2,128,128]{2,1,0:T(8,128)(2,1)S(1)}, bf16[2,128,128]{2,1,0:T(8,128)(2,1)S(1)}, f32[2,128]{1,0:T(2,128)S(1)}) custom-call(s32[3]{0:T(128)S(1)} %copy-done.16, s32[256]{0:T(256)S(1)} %get-tuple-element.57.picks, s32[256]{0:T(256)S(1)} %get-tuple-element.56.owns, ...), custom_call_target="tpu_custom_call" | custom-call | tf_op jit(solution)/shard_map/attend/pallas_call | solution.py:277
  92.4 2.6 %collective-permute-start.31 = (bf16[2,128,128]{2,1,0:T(8,128)(2,1)S(1)}, bf16[2,128,128]{2,1,0:T(8,128)(2,1)S(1)}, u32[]{:S(2)}, u32[]{:S(2)}) collective-permute-start(bf16[2,128,128]{2,1,0:T(8,128)(2,1)S(1)} %get-tuple-element.49), channel_id=1, source_target_pairs={{4,0},{8,4},{12,8},{0,12},{20,16},{24,20},{28,24},{16,28},{36,32},... | collective-permute-start | bytes 196616 | tf_op jit(solution)/shard_map/ppermute | solution.py:326
  94.9 0.3 collective-permute-start.32
  95.2 0.8 collective-permute-start.33
  96.0 0.3 collective-permute-done.31.refs_9_
  96.3 2.4 %collective-permute-start.24 = (bf16[2,512,128]{2,1,0:T(8,128)(2,1)}, bf16[2,512,128]{2,1,0:T(8,128)(2,1)S(1)}, u32[]{:S(2)}, u32[]{:S(2)}) collective-permute-start(bf16[2,512,128]{2,1,0:T(8,128)(2,1)} %get-tuple-element.40), channel_id=1, source_target_pairs={{16,0},{20,4},{24,8},{28,12},{0,16},{4,20},{8,24},{12,28},{48,32},... | collective-permute-start | bytes 786440 | tf_op jit(solution)/shard_map/ppermute | solution.py:326
  98.7 0.9 collective-permute-done.32.refs_10_
  99.7 2.3 %collective-permute-start.25 = (bf16[2,512,128]{2,1,0:T(8,128)(2,1)}, bf16[2,512,128]{2,1,0:T(8,128)(2,1)S(1)}, u32[]{:S(2)}, u32[]{:S(2)}) collective-permute-start(bf16[2,512,128]{2,1,0:T(8,128)(2,1)} %get-tuple-element.41), channel_id=1, source_target_pairs={{20,0},{24,4},{28,8},{16,12},{4,16},{8,20},{12,24},{0,28},{52,32},... | collective-permute-start | bytes 786440 | tf_op jit(solution)/shard_map/ppermute | solution.py:326
  102.0 1.1 collective-permute-start.26
  103.1 0.7 copy-done.14
  103.8 1.8 %collective-permute-start.30 = (bf16[2,384,128]{2,1,0:T(8,128)(2,1)}, bf16[2,384,128]{2,1,0:T(8,128)(2,1)S(1)}, u32[]{:S(2)}, u32[]{:S(2)}) collective-permute-start(bf16[2,384,128]{2,1,0:T(8,128)(2,1)} %copy-done.17), channel_id=1, source_target_pairs={{12,0},{0,4},{4,8},{8,12},{28,16},{16,20},{20,24},{24,28},{44,32},... | collective-permute-start | bytes 589832 | tf_op jit(solution)/shard_map/ppermute | solution.py:326
  105.6 0.6 copy.9
  106.2 15.9 %collective-permute-done.30.refs_7_ = bf16[2,384,128]{2,1,0:T(8,128)(2,1)S(1)} collective-permute-done((bf16[2,384,128]{2,1,0:T(8,128)(2,1)}, bf16[2,384,128]{2,1,0:T(8,128)(2,1)S(1)}, u32[]{:S(2)}, u32[]{:S(2)}) %collective-permute-start.30) | collective-permute-done | bytes 196640 | tf_op jit(solution)/shard_map/ppermute | solution.py:326
  122.2 0.9 copy-done.13
  123.1 0.9 copy-done.15
  124.0 2.6 %join_outputs.1 = bf16[8192,128]{1,0:T(8,128)(2,1)} custom-call(s32[3]{0:T(128)S(1)} %copy-done.16, bf16[2,512,128]{2,1,0:T(8,128)(2,1)S(1)} %collective-permute-done.24.refs_0_, bf16[2,512,128]{2,1,0:T(8,128)(2,1)S(1)} %collective-permute-done.25.refs_1_, bf16[2,512,128]{2,1,0:T(8,128)(2,1)S(1)} %collective-permute-done.26.refs_2_, ...), custom_call_target="tpu_custom_call" | custom-call | tf_op jit(solution)/shard_map/join_outputs/pallas_call | solution.py:298
  (58 shorter events, 0.2 us)
Async XLA Ops:
  1.2 63.2 %copy-start.16 = (s32[3]{0:T(128)S(1)}, s32[3]{0:T(128)}, u32[]{:S(2)}) copy-start(s32[3]{0:T(128)} %pad_add_fusion.1.place) | copy-start | bytes 40
  4.1 12.8 %copy-start = (bf16[1040,128]{1,0:T(8,128)(2,1)S(1)}, bf16[1040,128]{1,0:T(8,128)(2,1)}, u32[]{:S(2)}) copy-start(bf16[1040,128]{1,0:T(8,128)(2,1)} %get-tuple-element.27.refs_0_) | copy-start | bytes 798724
  4.1 17.6 %collective-permute-start.3 = (bf16[1040,128]{1,0:T(8,128)(2,1)}, bf16[1040,128]{1,0:T(8,128)(2,1)S(1)}, u32[]{:S(2)}, u32[]{:S(2)}) collective-permute-start(bf16[1040,128]{1,0:T(8,128)(2,1)} %get-tuple-element.28), channel_id=1, source_target_pairs={{0,240},{16,224},{32,16},{48,0},{64,48},{80,32},{96,80},{112,64},{... | collective-permute-start | bytes 798728 | tf_op jit(solution)/shard_map/ppermute | solution.py:310
  15.6 9.5 %collective-permute-start.16 = (bf16[2,512,128]{2,1,0:T(8,128)(2,1)}, bf16[2,512,128]{2,1,0:T(8,128)(2,1)S(1)}, u32[]{:S(2)}, u32[]{:S(2)}) collective-permute-start(bf16[2,512,128]{2,1,0:T(8,128)(2,1)} %get-tuple-element.30), channel_id=1, source_target_pairs={{0,4},{4,8},{8,12},{12,0},{16,20},{20,24},{24,28},{28,16},{32,36},... | collective-permute-start | bytes 786440 | tf_op jit(solution)/shard_map/ppermute | solution.py:326
  16.9 10.5 %collective-permute-start.8 = (bf16[1040,128]{1,0:T(8,128)(2,1)S(1)}, bf16[1040,128]{1,0:T(8,128)(2,1)S(1)}, u32[]{:S(2)}, u32[]{:S(2)}) collective-permute-start(bf16[1040,128]{1,0:T(8,128)(2,1)S(1)} %copy-done), channel_id=1, source_target_pairs={{0,32},{16,48},{32,64},{48,80},{64,96},{80,112},{96,128},{112,144}... | collective-permute-start | bytes 798728 | tf_op jit(solution)/shard_map/ppermute | solution.py:310
  17.7 1.3 collective-permute-start
  17.9 14.9 %collective-permute-start.13 = (bf16[1040,128]{1,0:T(8,128)(2,1)}, bf16[1040,128]{1,0:T(8,128)(2,1)S(1)}, u32[]{:S(2)}, u32[]{:S(2)}) collective-permute-start(bf16[1040,128]{1,0:T(8,128)(2,1)} %get-tuple-element.28), channel_id=1, source_target_pairs={{0,48},{16,32},{32,80},{48,64},{64,112},{80,96},{96,144},{112,128}... | collective-permute-start | bytes 798728 | tf_op jit(solution)/shard_map/ppermute | solution.py:310
  19.0 13.8 %collective-permute-start.2 = (bf16[1040,128]{1,0:T(8,128)(2,1)S(1)}, bf16[1040,128]{1,0:T(8,128)(2,1)S(1)}, u32[]{:S(2)}, u32[]{:S(2)}) collective-permute-start(bf16[1040,128]{1,0:T(8,128)(2,1)S(1)} %copy-done), channel_id=1, source_target_pairs={{0,224},{16,240},{32,0},{48,16},{64,32},{80,48},{96,64},{112,80},{... | collective-permute-start | bytes 798728 | tf_op jit(solution)/shard_map/ppermute | solution.py:310
  21.7 13.8 %collective-permute-start.5 = (bf16[1040,128]{1,0:T(8,128)(2,1)S(1)}, bf16[1040,128]{1,0:T(8,128)(2,1)S(1)}, u32[]{:S(2)}, u32[]{:S(2)}) collective-permute-start(bf16[1040,128]{1,0:T(8,128)(2,1)S(1)} %collective-permute-done.3.refs_3_), channel_id=1, source_target_pairs={{0,224},{16,240},{32,0},{48,16},{64,32},{80,48},{96,64},{112,80},{... | collective-permute-start | bytes 798728 | tf_op jit(solution)/shard_map/ppermute | solution.py:310
  25.1 0.7 copy-start.3
  25.8 10.4 %collective-permute-start.17 = (bf16[2,512,128]{2,1,0:T(8,128)(2,1)}, bf16[2,512,128]{2,1,0:T(8,128)(2,1)S(1)}, u32[]{:S(2)}, u32[]{:S(2)}) collective-permute-start(bf16[2,512,128]{2,1,0:T(8,128)(2,1)} %get-tuple-element.31), channel_id=1, source_target_pairs={{0,8},{4,12},{8,0},{12,4},{16,24},{20,28},{24,16},{28,20},{32,40},... | collective-permute-start | bytes 786440 | tf_op jit(solution)/shard_map/ppermute | solution.py:326
  27.3 11.0 %collective-permute-start.9 = (bf16[1040,128]{1,0:T(8,128)(2,1)S(1)}, bf16[1040,128]{1,0:T(8,128)(2,1)S(1)}, u32[]{:S(2)}, u32[]{:S(2)}) collective-permute-start(bf16[1040,128]{1,0:T(8,128)(2,1)S(1)} %collective-permute-done.8.refs_14_), channel_id=1, source_target_pairs={{0,32},{16,48},{32,64},{48,80},{64,96},{80,112},{96,128},{112,144}... | collective-permute-start | bytes 798728 | tf_op jit(solution)/shard_map/ppermute | solution.py:310
  32.8 13.8 %collective-permute-start.14 = (bf16[1040,128]{1,0:T(8,128)(2,1)S(1)}, bf16[1040,128]{1,0:T(8,128)(2,1)S(1)}, u32[]{:S(2)}, u32[]{:S(2)}) collective-permute-start(bf16[1040,128]{1,0:T(8,128)(2,1)S(1)} %collective-permute-done.13.refs_15_), channel_id=1, source_target_pairs={{0,32},{16,48},{32,64},{48,80},{64,96},{80,112},{96,128},{112,144}... | collective-permute-start | bytes 798728 | tf_op jit(solution)/shard_map/ppermute | solution.py:310
  32.8 14.5 %collective-permute-start.4 = (bf16[1040,128]{1,0:T(8,128)(2,1)S(1)}, bf16[1040,128]{1,0:T(8,128)(2,1)S(1)}, u32[]{:S(2)}, u32[]{:S(2)}) collective-permute-start(bf16[1040,128]{1,0:T(8,128)(2,1)S(1)} %collective-permute-done.2.refs_2_), channel_id=1, source_target_pairs={{0,224},{16,240},{32,0},{48,16},{64,32},{80,48},{96,64},{112,80},{... | collective-permute-start | bytes 798728 | tf_op jit(solution)/shard_map/ppermute | solution.py:310
  35.4 13.8 %collective-permute-start.7 = (bf16[1040,128]{1,0:T(8,128)(2,1)S(1)}, bf16[1040,128]{1,0:T(8,128)(2,1)S(1)}, u32[]{:S(2)}, u32[]{:S(2)}) collective-permute-start(bf16[1040,128]{1,0:T(8,128)(2,1)S(1)} %collective-permute-done.5.refs_5_), channel_id=1, source_target_pairs={{0,224},{16,240},{32,0},{48,16},{64,32},{80,48},{96,64},{112,80},{... | collective-permute-start | bytes 798728 | tf_op jit(solution)/shard_map/ppermute | solution.py:310
  36.2 0.7 copy-start.6
  36.9 6.6 %collective-permute-start.18 = (bf16[2,512,128]{2,1,0:T(8,128)(2,1)}, bf16[2,512,128]{2,1,0:T(8,128)(2,1)S(1)}, u32[]{:S(2)}, u32[]{:S(2)}) collective-permute-start(bf16[2,512,128]{2,1,0:T(8,128)(2,1)} %get-tuple-element.32), channel_id=1, source_target_pairs={{0,12},{4,0},{8,4},{12,8},{16,28},{20,16},{24,20},{28,24},{32,44},... | collective-permute-start | bytes 786440 | tf_op jit(solution)/shard_map/ppermute | solution.py:326
  38.4 12.6 %collective-permute-start.10 = (bf16[1040,128]{1,0:T(8,128)(2,1)S(1)}, bf16[1040,128]{1,0:T(8,128)(2,1)S(1)}, u32[]{:S(2)}, u32[]{:S(2)}) collective-permute-start(bf16[1040,128]{1,0:T(8,128)(2,1)S(1)} %collective-permute-done.9.refs_12_), channel_id=1, source_target_pairs={{0,32},{16,48},{32,64},{48,80},{64,96},{80,112},{96,128},{112,144}... | collective-permute-start | bytes 798728 | tf_op jit(solution)/shard_map/ppermute | solution.py:310
  43.5 0.7 copy-start.9
  44.2 7.0 %collective-permute-start.1 = (bf16[1040,128]{1,0:T(8,128)(2,1)}, bf16[1040,128]{1,0:T(8,128)(2,1)S(1)}, u32[]{:S(2)}, u32[]{:S(2)}) collective-permute-start(bf16[1040,128]{1,0:T(8,128)(2,1)} %get-tuple-element.28), channel_id=1, source_target_pairs={{0,16},{16,0},{32,48},{48,32},{64,80},{80,64},{96,112},{112,96},{1... | collective-permute-start | bytes 798728 | tf_op jit(solution)/shard_map/ppermute | solution.py:310
  46.5 9.2 %collective-permute-start.15 = (bf16[1040,128]{1,0:T(8,128)(2,1)S(1)}, bf16[1040,128]{1,0:T(8,128)(2,1)S(1)}, u32[]{:S(2)}, u32[]{:S(2)}) collective-permute-start(bf16[1040,128]{1,0:T(8,128)(2,1)S(1)} %collective-permute-done.14.refs_13_), channel_id=1, source_target_pairs={{0,32},{16,48},{32,64},{48,80},{64,96},{80,112},{96,128},{112,144}... | collective-permute-start | bytes 798728 | tf_op jit(solution)/shard_map/ppermute | solution.py:310
  47.2 10.9 %collective-permute-start.6 = (bf16[1040,128]{1,0:T(8,128)(2,1)S(1)}, bf16[1040,128]{1,0:T(8,128)(2,1)}, u32[]{:S(2)}, u32[]{:S(2)}) collective-permute-start(bf16[1040,128]{1,0:T(8,128)(2,1)S(1)} %collective-permute-done.4.refs_4_), channel_id=1, source_target_pairs={{0,224},{16,240},{32,0},{48,16},{64,32},{80,48},{96,64},{112,80},{... | collective-permute-start | bytes 798728 | tf_op jit(solution)/shard_map/ppermute | solution.py:310
  49.2 11.5 %collective-permute-start.12 = (bf16[1040,128]{1,0:T(8,128)(2,1)S(1)}, bf16[1040,128]{1,0:T(8,128)(2,1)}, u32[]{:S(2)}, u32[]{:S(2)}) collective-permute-start(bf16[1040,128]{1,0:T(8,128)(2,1)S(1)} %collective-permute-done.7.refs_7_), channel_id=1, source_target_pairs={{0,224},{16,240},{32,0},{48,16},{64,32},{80,48},{96,64},{112,80},{... | collective-permute-start | bytes 798728 | tf_op jit(solution)/shard_map/ppermute | solution.py:310
  51.0 13.5 %collective-permute-start.11 = (bf16[1040,128]{1,0:T(8,128)(2,1)S(1)}, bf16[1040,128]{1,0:T(8,128)(2,1)}, u32[]{:S(2)}, u32[]{:S(2)}) collective-permute-start(bf16[1040,128]{1,0:T(8,128)(2,1)S(1)} %collective-permute-done.10.refs_10_), channel_id=1, source_target_pairs={{0,32},{16,48},{32,64},{48,80},{64,96},{80,112},{96,128},{112,144}... | collective-permute-start | bytes 798728 | tf_op jit(solution)/shard_map/ppermute | solution.py:310
  51.2 25.9 %collective-permute-start.19 = (bf16[2,512,128]{2,1,0:T(8,128)(2,1)}, bf16[2,512,128]{2,1,0:T(8,128)(2,1)S(1)}, u32[]{:S(2)}, u32[]{:S(2)}) collective-permute-start(bf16[2,512,128]{2,1,0:T(8,128)(2,1)} %get-tuple-element.35), channel_id=1, source_target_pairs={{0,16},{4,20},{8,24},{12,28},{16,0},{20,4},{24,8},{28,12},{32,48},... | collective-permute-start | bytes 786440 | tf_op jit(solution)/shard_map/ppermute | solution.py:326
  55.7 22.3 %collective-permute-start.20 = (bf16[2,512,128]{2,1,0:T(8,128)(2,1)}, bf16[2,512,128]{2,1,0:T(8,128)(2,1)S(1)}, u32[]{:S(2)}, u32[]{:S(2)}) collective-permute-start(bf16[2,512,128]{2,1,0:T(8,128)(2,1)} %get-tuple-element.36), channel_id=1, source_target_pairs={{0,20},{4,24},{8,28},{12,16},{16,4},{20,8},{24,12},{28,0},{32,52},... | collective-permute-start | bytes 786440 | tf_op jit(solution)/shard_map/ppermute | solution.py:326
  58.1 19.8 %collective-permute-start.21 = (bf16[2,512,128]{2,1,0:T(8,128)(2,1)}, bf16[2,512,128]{2,1,0:T(8,128)(2,1)S(1)}, u32[]{:S(2)}, u32[]{:S(2)}) collective-permute-start(bf16[2,512,128]{2,1,0:T(8,128)(2,1)} %get-tuple-element.37), channel_id=1, source_target_pairs={{0,24},{4,28},{8,16},{12,20},{16,8},{20,12},{24,0},{28,4},{32,56},... | collective-permute-start | bytes 786440 | tf_op jit(solution)/shard_map/ppermute | solution.py:326
  60.7 17.2 %collective-permute-start.22 = (bf16[2,512,128]{2,1,0:T(8,128)(2,1)}, bf16[2,512,128]{2,1,0:T(8,128)(2,1)S(1)}, u32[]{:S(2)}, u32[]{:S(2)}) collective-permute-start(bf16[2,512,128]{2,1,0:T(8,128)(2,1)} %get-tuple-element.38), channel_id=1, source_target_pairs={{0,28},{4,16},{8,20},{12,24},{16,12},{20,0},{24,4},{28,8},{32,60},... | collective-permute-start | bytes 786440 | tf_op jit(solution)/shard_map/ppermute | solution.py:326
  64.5 1.0 copy-start.1
  65.4 0.9 copy-start.4
  66.4 0.9 copy-start.7
  67.3 0.9 copy-start.10
  75.7 0.7 copy-start.12
  76.4 0.7 copy-start.17
  77.1 26.1 %collective-permute-start.28 = (bf16[2,384,128]{2,1,0:T(8,128)(2,1)S(1)}, bf16[2,384,128]{2,1,0:T(8,128)(2,1)S(1)}, u32[]{:S(2)}, u32[]{:S(2)}) collective-permute-start(bf16[2,384,128]{2,1,0:T(8,128)(2,1)S(1)} %get-tuple-element.45), channel_id=1, source_target_pairs={{4,0},{8,4},{12,8},{0,12},{20,16},{24,20},{28,24},{16,28},{36,32},... | collective-permute-start | bytes 589832 | tf_op jit(solution)/shard_map/ppermute | solution.py:326
  77.1 11.1 %copy-start.2 = (bf16[2,512,128]{2,1,0:T(8,128)(2,1)S(1)}, bf16[2,512,128]{2,1,0:T(8,128)(2,1)}, u32[]{:S(2)}) copy-start(bf16[2,512,128]{2,1,0:T(8,128)(2,1)} %get-tuple-element.29.refs_16_) | copy-start | bytes 786436
  77.1 11.1 %copy-start.5 = (bf16[2,512,128]{2,1,0:T(8,128)(2,1)S(1)}, bf16[2,512,128]{2,1,0:T(8,128)(2,1)}, u32[]{:S(2)}) copy-start(bf16[2,512,128]{2,1,0:T(8,128)(2,1)} %copy-done.3) | copy-start | bytes 786436
  77.1 11.1 %copy-start.8 = (bf16[2,512,128]{2,1,0:T(8,128)(2,1)S(1)}, bf16[2,512,128]{2,1,0:T(8,128)(2,1)}, u32[]{:S(2)}) copy-start(bf16[2,512,128]{2,1,0:T(8,128)(2,1)} %copy-done.6) | copy-start | bytes 786436
  77.1 11.1 %copy-start.11 = (bf16[2,512,128]{2,1,0:T(8,128)(2,1)S(1)}, bf16[2,512,128]{2,1,0:T(8,128)(2,1)}, u32[]{:S(2)}) copy-start(bf16[2,512,128]{2,1,0:T(8,128)(2,1)} %copy-done.9) | copy-start | bytes 786436
  77.1 26.7 %collective-permute-start.29 = (bf16[2,384,128]{2,1,0:T(8,128)(2,1)}, bf16[2,384,128]{2,1,0:T(8,128)(2,1)}, u32[]{:S(2)}, u32[]{:S(2)}) collective-permute-start(bf16[2,384,128]{2,1,0:T(8,128)(2,1)} %get-tuple-element.46), channel_id=1, source_target_pairs={{8,0},{12,4},{0,8},{4,12},{24,16},{28,20},{16,24},{20,28},{40,32},... | collective-permute-start | bytes 589832 | tf_op jit(solution)/shard_map/ppermute | solution.py:326
  87.2 8.0 %collective-permute-start.23 = (f32[8,128]{1,0:T(8,128)S(1)}, f32[8,128]{1,0:T(8,128)S(1)}, u32[]{:S(2)}, u32[]{:S(2)}) collective-permute-start(f32[8,128]{1,0:T(8,128)S(1)} %get-tuple-element.39), channel_id=1, source_target_pairs={{0,16},{16,0},{32,48},{48,32},{64,80},{80,64},{96,112},{112,96},{1... | collective-permute-start | bytes 12296 | tf_op jit(solution)/shard_map/ppermute | solution.py:310
  92.4 3.9 %collective-permute-start.31 = (bf16[2,128,128]{2,1,0:T(8,128)(2,1)S(1)}, bf16[2,128,128]{2,1,0:T(8,128)(2,1)S(1)}, u32[]{:S(2)}, u32[]{:S(2)}) collective-permute-start(bf16[2,128,128]{2,1,0:T(8,128)(2,1)S(1)} %get-tuple-element.49), channel_id=1, source_target_pairs={{4,0},{8,4},{12,8},{0,12},{20,16},{24,20},{28,24},{16,28},{36,32},... | collective-permute-start | bytes 196616 | tf_op jit(solution)/shard_map/ppermute | solution.py:326
  94.9 4.7 %collective-permute-start.32 = (bf16[2,128,128]{2,1,0:T(8,128)(2,1)S(1)}, bf16[2,128,128]{2,1,0:T(8,128)(2,1)S(1)}, u32[]{:S(2)}, u32[]{:S(2)}) collective-permute-start(bf16[2,128,128]{2,1,0:T(8,128)(2,1)S(1)} %get-tuple-element.50), channel_id=1, source_target_pairs={{8,0},{12,4},{0,8},{4,12},{24,16},{28,20},{16,24},{20,28},{40,32},... | collective-permute-start | bytes 196616 | tf_op jit(solution)/shard_map/ppermute | solution.py:326
  95.2 6.8 %collective-permute-start.33 = (bf16[2,128,128]{2,1,0:T(8,128)(2,1)S(1)}, bf16[2,128,128]{2,1,0:T(8,128)(2,1)S(1)}, u32[]{:S(2)}, u32[]{:S(2)}) collective-permute-start(bf16[2,128,128]{2,1,0:T(8,128)(2,1)S(1)} %get-tuple-element.51), channel_id=1, source_target_pairs={{12,0},{0,4},{4,8},{8,12},{28,16},{16,20},{20,24},{24,28},{44,32},... | collective-permute-start | bytes 196616 | tf_op jit(solution)/shard_map/ppermute | solution.py:326
  96.3 25.9 %collective-permute-start.24 = (bf16[2,512,128]{2,1,0:T(8,128)(2,1)}, bf16[2,512,128]{2,1,0:T(8,128)(2,1)S(1)}, u32[]{:S(2)}, u32[]{:S(2)}) collective-permute-start(bf16[2,512,128]{2,1,0:T(8,128)(2,1)} %get-tuple-element.40), channel_id=1, source_target_pairs={{16,0},{20,4},{24,8},{28,12},{0,16},{4,20},{8,24},{12,28},{48,32},... | collective-permute-start | bytes 786440 | tf_op jit(solution)/shard_map/ppermute | solution.py:326
  99.7 22.5 %collective-permute-start.25 = (bf16[2,512,128]{2,1,0:T(8,128)(2,1)}, bf16[2,512,128]{2,1,0:T(8,128)(2,1)S(1)}, u32[]{:S(2)}, u32[]{:S(2)}) collective-permute-start(bf16[2,512,128]{2,1,0:T(8,128)(2,1)} %get-tuple-element.41), channel_id=1, source_target_pairs={{20,0},{24,4},{28,8},{16,12},{4,16},{8,20},{12,24},{0,28},{52,32},... | collective-permute-start | bytes 786440 | tf_op jit(solution)/shard_map/ppermute | solution.py:326
  102.0 20.2 %collective-permute-start.26 = (bf16[2,512,128]{2,1,0:T(8,128)(2,1)}, bf16[2,512,128]{2,1,0:T(8,128)(2,1)S(1)}, u32[]{:S(2)}, u32[]{:S(2)}) collective-permute-start(bf16[2,512,128]{2,1,0:T(8,128)(2,1)} %get-tuple-element.42), channel_id=1, source_target_pairs={{24,0},{28,4},{16,8},{20,12},{8,16},{12,20},{0,24},{4,28},{56,32},... | collective-permute-start | bytes 786440 | tf_op jit(solution)/shard_map/ppermute | solution.py:326
  103.1 0.7 copy-start.14
  103.8 18.4 %collective-permute-start.27 = (bf16[2,512,128]{2,1,0:T(8,128)(2,1)}, bf16[2,512,128]{2,1,0:T(8,128)(2,1)S(1)}, u32[]{:S(2)}, u32[]{:S(2)}) collective-permute-start(bf16[2,512,128]{2,1,0:T(8,128)(2,1)} %get-tuple-element.43), channel_id=1, source_target_pairs={{28,0},{16,4},{20,8},{24,12},{12,16},{0,20},{4,24},{8,28},{60,32},... | collective-permute-start | bytes 786440 | tf_op jit(solution)/shard_map/ppermute | solution.py:326
  103.8 18.4 %collective-permute-start.30 = (bf16[2,384,128]{2,1,0:T(8,128)(2,1)}, bf16[2,384,128]{2,1,0:T(8,128)(2,1)S(1)}, u32[]{:S(2)}, u32[]{:S(2)}) collective-permute-start(bf16[2,384,128]{2,1,0:T(8,128)(2,1)} %copy-done.17), channel_id=1, source_target_pairs={{12,0},{0,4},{4,8},{8,12},{28,16},{16,20},{20,24},{24,28},{44,32},... | collective-permute-start | bytes 589832 | tf_op jit(solution)/shard_map/ppermute | solution.py:326
  122.2 0.9 copy-start.13
  123.1 0.9 copy-start.15

commit v5 on v4

--- a/solution.py
+++ b/solution.py
@@ -24,6 +24,8 @@
 PIECE = 2 * TOK + COMP_PAD
 PARTS = 8
 CHUNKS = ((1, 0, 8), (0, 0, 6), (0, 6, 2))
+EARLY = tuple((k, h) for k in (0, 1, 2, 3, 5, 6, 7) for h in range(2))
+LATE = ((4, 0), (4, 1))
 KEYS = TOPN * BLOCK
 ROWS = HPG * BLOCK
 COMP_ROWS = SHARDS * COMP_PAD
@@ -123,21 +125,33 @@
         copy.wait()
 
 
-def attend(half, begin, count, place, picks, owns, *refs):
-    pieces, refs = refs[: 2 * CHIPS], refs[2 * CHIPS :]
+def copies_of(place, pieces, names, pool, sems):
+    copies = []
+    for i, (k, h) in enumerate(names):
+        slot = 2 * ((place[2] + k) % CHIPS) + (place[1] + h) % 2
+        rows = pl.ds(pl.multiple_of(slot * PIECE, COMP_PAD), PIECE)
+        copies.append(pltpu.make_async_copy(pieces[i], pool.at[rows, :], sems.at[i]))
+    for copy in copies:
+        copy.start()
+    return copies
+
+
+def stage(place, *refs):
+    *pieces, pool, sems = refs
+    for copy in copies_of(place, pieces, EARLY, pool, sems):
+        copy.wait()
+
+
+def attend(half, begin, count, fresh, place, picks, owns, given, *refs):
+    pieces, refs = (refs[: len(LATE)], refs[len(LATE) :]) if fresh else ((), refs)
     queries, refs = refs[:COLS], refs[COLS:]
     outs, refs = refs[:COLS], refs[COLS:]
-    pooled, pool, comp, mask, *rest, sems = refs
+    pooled, *refs = refs
+    pool, refs = (refs[0], refs[1:]) if fresh else (given, refs)
+    comp, mask, *rest, sems = refs
     turned, scores, logits, tops = rest[0:2], rest[2:4], rest[4:6], rest[6:8]
     core, chip = place[1], place[2]
-    copies = []
-    for k in range(CHIPS):
-        for h in range(2):
-            slot = 2 * ((chip + k) % CHIPS) + (core + h) % 2
-            rows = pl.ds(pl.multiple_of(slot * PIECE, COMP_PAD), PIECE)
-            copies.append(pltpu.make_async_copy(pieces[2 * k + h], pool.at[rows, :], sems.at[2 * k + h]))
-    for copy in copies:
-        copy.start()
+    copies = copies_of(place, pieces, LATE, pool, sems) if fresh else []
     shape = (2 * BLOCK, DH)
     row = iota(shape, 0)
     hidden = (row >= BLOCK) & (row - BLOCK > iota(shape, 1))
@@ -273,14 +287,30 @@
     )(place, queries)
 
 
-def call_attend(half, begin, count, place, picks, owns, pieces, queries):
+def call_stage(place, pieces):
     return pl.pallas_call(
-        functools.partial(attend, half, begin, count),
-        in_specs=[SMEM] * 3 + [ANY] * (2 * CHIPS) + [VMEM] * COLS,
-        out_specs=[VMEM] * (COLS + 1),
-        out_shape=[bf16(2, count * BLOCK, DH)] * COLS + [jax.ShapeDtypeStruct((count, NBLK), jnp.float32)],
+        stage,
+        in_specs=[SMEM] + [ANY] * len(EARLY),
+        out_specs=VMEM,
+        out_shape=bf16(SHARDS * PIECE, DH),
+        scratch_shapes=[pltpu.SemaphoreType.DMA((len(EARLY),))],
+        compiler_params=grant(12),
+        name="stage",
+    )(place, *[pieces[2 * k + h] for k, h in EARLY])
+
+
+def call_attend(chunk, place, picks, owns, pool, late, queries):
+    half, begin, count = chunk
+    fresh = bool(late)
+    return pl.pallas_call(
+        functools.partial(attend, half, begin, count, fresh),
+        in_specs=[SMEM] * 3 + [VMEM] + [ANY] * len(late) + [VMEM] * COLS,
+        out_specs=[VMEM] * (COLS + 1 + fresh),
+        out_shape=[bf16(2, count * BLOCK, DH)] * COLS
+        + [jax.ShapeDtypeStruct((count, NBLK), jnp.float32)]
+        + [bf16(SHARDS * PIECE, DH)] * fresh,
+        input_output_aliases={3: COLS + 1} if fresh else {},
         scratch_shapes=[
-            pltpu.VMEM((SHARDS * PIECE, DH), jnp.bfloat16),
             pltpu.VMEM((NBLK, DH), jnp.bfloat16),
             pltpu.VMEM((2 * BLOCK, DH), jnp.bfloat16),
         ]
@@ -288,10 +318,10 @@
         + [pltpu.VMEM((KEYS, ROWS), jnp.float32)] * 2
         + [pltpu.VMEM((NBLK, ROWS), jnp.float32)] * 2
         + [pltpu.VMEM((8, ROWS), jnp.float32)] * 2
-        + [pltpu.SemaphoreType.DMA((2 * CHIPS,))],
+        + [pltpu.SemaphoreType.DMA((len(LATE),))],
         compiler_params=grant(28),
         name="attend",
-    )(place, picks, owns, *pieces, *[queries[2 * dx + half] for dx in range(COLS)])
+    )(place, picks, owns, pool, *late, *[queries[2 * dx + half] for dx in range(COLS)])
 
 
 def call_join_outputs(place, parts):
@@ -360,9 +390,14 @@
     number = shard[:, None] * TILES + jnp.arange(TILES, dtype=jnp.int32)
     picks = (blocks // TILES * PIECE + blocks % TILES * BLOCK).reshape(-1)
     owns = jnp.where(blocks == number[..., None], BLOCK, 0).reshape(-1)
+    pool = call_stage(place, pieces)
     joined, sums = [], []
-    for half, begin, count in CHUNKS:
-        *outs, rows = call_attend(half, begin, count, place, picks, owns, pieces, moved)
+    late = [pieces[2 * k + h] for k, h in LATE]
+    for chunk in CHUNKS:
+        half = chunk[0]
+        *outs, rows = call_attend(chunk, place, picks, owns, pool, late, moved)
+        if late:
+            late, rows, pool = [], outs.pop(), rows
         back = [None] * COLS
         for dx in (2, 1, 3, 0):
             back[dx] = by_part(outs[dx], dx, half, True)

time: 127 us -> 122 us (0.961)
  local copies, waits for them, and re-layouts: 11.5 us -> 5.45 us
  starting transfers between devices: 47.6 us -> 53 us
  Pallas kernels: 30.8 us -> 27.6 us
  waiting for transfers between devices: 35.2 us -> 33.8 us
    unnamed x37 -> x23, local copies, waits for them, and re-layouts: 10.4 us -> 4.37 us
    ppermute x17, starting transfers between devices: 25.3 us -> 28.3 us  [by_part(): return lax.ppermute(value, ('seq', 'head'), pairs)]
    pallas_call x3 -> x4, Pallas kernels: 20.9 us -> 18 us  [the longest x3 16 us: call_attend(): pl.pallas_call(functools.partial(attend, half, begin, count, fresh), in_s...]
    ppermute x17, starting transfers between devices: 22.3 us -> 24.6 us  [by_seq(): lax.ppermute(value, 'seq', [(s, move(s // 2, s % 2)) for s in range(SHARD...]
  transfers between devices with their start and end apart: 34 -> 34, of which waited for: 9 -> 7; matrix products, arithmetic and copies ran while one was open for 1% -> 1% of each run, Pallas kernels for 20% -> 13%
where the time goes in v5:
time: 122 us
  starting transfers between devices  53 us (43%)
  waiting for transfers between devices  33.8 us (28%)
  Pallas kernels  27.6 us (23%)
  local copies, waits for them, and re-layouts  5.45 us (4%)
    ppermute x17, starting transfers between devices, by_part(): return lax.ppermute(value, ('seq', 'head'), pairs)  28.3 us
    ppermute x17, starting transfers between devices, by_seq(): lax.ppermute(value, 'seq', [(s, move(s // 2, s % 2)) for s in range(SHARD...  24.6 us
    ppermute x17, waiting for transfers between devices, by_part(): return lax.ppermute(value, ('seq', 'head'), pairs)  23.5 us
    pallas_call x3, Pallas kernels, call_attend(): pl.pallas_call(functools.partial(attend, half, begin, count, fresh), in_s...  16 us
    ppermute x17, waiting for transfers between devices, by_seq(): lax.ppermute(value, 'seq', [(s, move(s // 2, s % 2)) for s in range(SHARD...  10.2 us
    pallas_call x1, Pallas kernels, call_split_queries(): pl.pallas_call(functools.partial(split_queries, tokens), grid=(steps,), i...  4.6 us
    unnamed x23, local copies, waits for them, and re-layouts  4.37 us
    pallas_call x1, Pallas kernels, call_split_pools(): pl.pallas_call(split_pools, in_specs=[SMEM, VMEM, VMEM, VMEM], out_specs=...  2.84 us
  transfers between devices with their start and end apart: 34, of which 7 were waited for; matrix products, arithmetic and copies ran while one was open for 1% of the time, Pallas kernels for 13%

profile of v5, /device:TPU:1, one launch (start us, length us, event | category | flops | bytes accessed | tf_op | source)
XLA Modules:
  0.0 121.5 jit_solution(5914600647051567668)
XLA Ops:
  0.6 0.6 pad_add_fusion.1.place
  1.2 4.6 %split_queries.1 = (bf16[2,512,128]{2,1,0:T(8,128)(2,1)}, bf16[2,512,128]{2,1,0:T(8,128)(2,1)}, bf16[2,512,128]{2,1,0:T(8,128)(2,1)}, bf16[2,512,128]{2,1,0:T(8,...) custom-call(s32[3]{0:T(128)} %pad_add_fusion.1.place, ...), custom_call_target="tpu_custom_call" | custom-call | tf_op jit(solution)/shard_map/split_queries/pallas_call | solution.py:280
  5.8 3.3 %collective-permute-start.16 = (bf16[2,512,128]{2,1,0:T(8,128)(2,1)}, bf16[2,512,128]{2,1,0:T(8,128)(2,1)S(1)}, u32[]{:S(2)}, u32[]{:S(2)}) collective-permute-start(bf16[2,512,128]{2,1,0:T(8,128)(2,1)} %get-tuple-element.30), channel_id=1, source_target_pairs={{0,16},{4,20},{8,24},{12,28},{16,0},{20,4},{24,8},{28,12},{32,48},... | collective-permute-start | bytes 786440 | tf_op jit(solution)/shard_map/ppermute | solution.py:356
  9.1 0.0 collective-permute-start.17
  9.1 0.8 constant_dynamic-slice_fusion.1
  9.9 0.2 collective-permute-start
  10.1 2.8 %split_pools.1 = (bf16[1040,128]{1,0:T(8,128)(2,1)}, bf16[1040,128]{1,0:T(8,128)(2,1)}) custom-call(s32[3]{0:T(128)} %pad_add_fusion.1.place, bf16[4096,128]{1,0:T(8,128)(2,1)} %bitcast.20, bf16[4096,128]{1,0:T(8,128)(2,1)} %bitcast.21, bf16[64,128]{1,0:T(8,128)(2,1)} %bitcast.22), custom_call_target="tpu_custom_call" | custom-call | tf_op jit(solution)/shard_map/split_pools/pallas_call | solution.py:268
  13.0 1.4 %collective-permute-start.8 = (bf16[1040,128]{1,0:T(8,128)(2,1)}, bf16[1040,128]{1,0:T(8,128)(2,1)S(1)}, u32[]{:S(2)}, u32[]{:S(2)}) collective-permute-start(bf16[1040,128]{1,0:T(8,128)(2,1)} %get-tuple-element.28.refs_0_), channel_id=1, source_target_pairs={{0,32},{16,48},{32,64},{48,80},{64,96},{80,112},{96,128},{112,144}... | collective-permute-start | bytes 798728 | tf_op jit(solution)/shard_map/ppermute | solution.py:340
  14.4 3.9 %collective-permute-start.2 = (bf16[1040,128]{1,0:T(8,128)(2,1)}, bf16[1040,128]{1,0:T(8,128)(2,1)S(1)}, u32[]{:S(2)}, u32[]{:S(2)}) collective-permute-start(bf16[1040,128]{1,0:T(8,128)(2,1)} %get-tuple-element.28.refs_0_), channel_id=1, source_target_pairs={{0,224},{16,240},{32,0},{48,16},{64,32},{80,48},{96,64},{112,80},{... | collective-permute-start | bytes 798728 | tf_op jit(solution)/shard_map/ppermute | solution.py:340
  18.4 0.7 copy-done.2
  19.1 3.0 %collective-permute-start.3 = (bf16[1040,128]{1,0:T(8,128)(2,1)}, bf16[1040,128]{1,0:T(8,128)(2,1)S(1)}, u32[]{:S(2)}, u32[]{:S(2)}) collective-permute-start(bf16[1040,128]{1,0:T(8,128)(2,1)} %get-tuple-element.29), channel_id=1, source_target_pairs={{0,240},{16,224},{32,16},{48,0},{64,48},{80,32},{96,80},{112,64},{... | collective-permute-start | bytes 798728 | tf_op jit(solution)/shard_map/ppermute | solution.py:340
  22.0 0.0 collective-permute-done.17.refs_3_
  22.0 0.7 copy-done.4
  22.7 2.7 %collective-permute-start.18 = (bf16[2,512,128]{2,1,0:T(8,128)(2,1)}, bf16[2,512,128]{2,1,0:T(8,128)(2,1)S(1)}, u32[]{:S(2)}, u32[]{:S(2)}) collective-permute-start(bf16[2,512,128]{2,1,0:T(8,128)(2,1)} %get-tuple-element.32), channel_id=1, source_target_pairs={{0,24},{4,28},{8,16},{12,20},{16,8},{20,12},{24,0},{28,4},{32,56},... | collective-permute-start | bytes 786440 | tf_op jit(solution)/shard_map/ppermute | solution.py:356
  25.4 0.0 collective-permute-done.8.refs_12_
  25.4 0.0 collective-permute-start.9
  25.4 0.0 collective-permute-done.2.refs_2_
  25.4 2.7 %collective-permute-start.4 = (bf16[1040,128]{1,0:T(8,128)(2,1)S(1)}, bf16[1040,128]{1,0:T(8,128)(2,1)S(1)}, u32[]{:S(2)}, u32[]{:S(2)}) collective-permute-start(bf16[1040,128]{1,0:T(8,128)(2,1)S(1)} %collective-permute-done.2.refs_2_), channel_id=1, source_target_pairs={{0,224},{16,240},{32,0},{48,16},{64,32},{80,48},{96,64},{112,80},{... | collective-permute-start | bytes 798728 | tf_op jit(solution)/shard_map/ppermute | solution.py:340
  28.1 3.4 %collective-permute-done.11.refs_13_ = bf16[1040,128]{1,0:T(8,128)(2,1)S(1)} collective-permute-done((bf16[1040,128]{1,0:T(8,128)(2,1)}, bf16[1040,128]{1,0:T(8,128)(2,1)S(1)}, u32[]{:S(2)}, u32[]{:S(2)}) %collective-permute-start.11) | collective-permute-done | bytes 266272 | tf_op jit(solution)/shard_map/ppermute | solution.py:340
  31.5 0.0 collective-permute-start.12
  31.5 0.0 collective-permute-done.3.refs_3_
  31.5 2.7 %collective-permute-start.5 = (bf16[1040,128]{1,0:T(8,128)(2,1)S(1)}, bf16[1040,128]{1,0:T(8,128)(2,1)S(1)}, u32[]{:S(2)}, u32[]{:S(2)}) collective-permute-start(bf16[1040,128]{1,0:T(8,128)(2,1)S(1)} %collective-permute-done.3.refs_3_), channel_id=1, source_target_pairs={{0,224},{16,240},{32,0},{48,16},{64,32},{80,48},{96,64},{112,80},{... | collective-permute-start | bytes 798728 | tf_op jit(solution)/shard_map/ppermute | solution.py:340
  34.1 0.0 collective-permute-done.18.refs_4_
  34.2 0.7 copy-done.6
  34.8 1.8 %collective-permute-start.19 = (bf16[2,512,128]{2,1,0:T(8,128)(2,1)}, bf16[2,512,128]{2,1,0:T(8,128)(2,1)S(1)}, u32[]{:S(2)}, u32[]{:S(2)}) collective-permute-start(bf16[2,512,128]{2,1,0:T(8,128)(2,1)} %get-tuple-element.33), channel_id=1, source_target_pairs={{0,28},{4,16},{8,20},{12,24},{16,12},{20,0},{24,4},{28,8},{32,60},... | collective-permute-start | bytes 786440 | tf_op jit(solution)/shard_map/ppermute | solution.py:356
  36.6 6.8 %collective-permute-done.19.refs_5_ = bf16[2,512,128]{2,1,0:T(8,128)(2,1)S(1)} collective-permute-done((bf16[2,512,128]{2,1,0:T(8,128)(2,1)}, bf16[2,512,128]{2,1,0:T(8,128)(2,1)S(1)}, u32[]{:S(2)}, u32[]{:S(2)}) %collective-permute-start.19) | collective-permute-done | bytes 262176 | tf_op jit(solution)/shard_map/ppermute | solution.py:356
  43.4 0.7 copy-done.8
  44.1 0.4 collective-permute-start.1
  44.5 0.0 collective-permute-done.9.refs_10_
  44.5 2.7 %collective-permute-start.6 = (bf16[1040,128]{1,0:T(8,128)(2,1)S(1)}, bf16[1040,128]{1,0:T(8,128)(2,1)}, u32[]{:S(2)}, u32[]{:S(2)}) collective-permute-start(bf16[1040,128]{1,0:T(8,128)(2,1)S(1)} %collective-permute-done.4.refs_4_), channel_id=1, source_target_pairs={{0,224},{16,240},{32,0},{48,16},{64,32},{80,48},{96,64},{112,80},{... | collective-permute-start | bytes 798728 | tf_op jit(solution)/shard_map/ppermute | solution.py:340
  47.2 0.0 collective-permute-done.12.refs_11_
  47.2 0.0 collective-permute-start.13
  47.2 2.7 %collective-permute-start.7 = (bf16[1040,128]{1,0:T(8,128)(2,1)S(1)}, bf16[1040,128]{1,0:T(8,128)(2,1)}, u32[]{:S(2)}, u32[]{:S(2)}) collective-permute-start(bf16[1040,128]{1,0:T(8,128)(2,1)S(1)} %collective-permute-done.5.refs_5_), channel_id=1, source_target_pairs={{0,224},{16,240},{32,0},{48,16},{64,32},{80,48},{96,64},{112,80},{... | collective-permute-start | bytes 798728 | tf_op jit(solution)/shard_map/ppermute | solution.py:340
  49.9 0.1 iota_add_fusion
  49.9 0.1 eq.21
  50.0 0.1 eq.22
  50.1 1.3 %collective-permute-start.20 = (bf16[2,512,128]{2,1,0:T(8,128)(2,1)}, bf16[2,512,128]{2,1,0:T(8,128)(2,1)S(1)}, u32[]{:S(2)}, u32[]{:S(2)}) collective-permute-start(bf16[2,512,128]{2,1,0:T(8,128)(2,1)} %get-tuple-element.36), channel_id=1, source_target_pairs={{0,4},{4,8},{8,12},{12,0},{16,20},{20,24},{24,28},{28,16},{32,36},... | collective-permute-start | bytes 786440 | tf_op jit(solution)/shard_map/ppermute | solution.py:356
  51.4 2.1 %collective-permute-done.10.refs_8_ = bf16[1040,128]{1,0:T(8,128)(2,1)S(1)} collective-permute-done((bf16[1040,128]{1,0:T(8,128)(2,1)S(1)}, bf16[1040,128]{1,0:T(8,128)(2,1)S(1)}, u32[]{:S(2)}, u32[]{:S(2)}) %collective-permute-start.10) | collective-permute-done | bytes 266272 | tf_op jit(solution)/shard_map/ppermute | solution.py:340
  53.5 2.5 %collective-permute-start.21 = (bf16[2,512,128]{2,1,0:T(8,128)(2,1)}, bf16[2,512,128]{2,1,0:T(8,128)(2,1)S(1)}, u32[]{:S(2)}, u32[]{:S(2)}) collective-permute-start(bf16[2,512,128]{2,1,0:T(8,128)(2,1)} %get-tuple-element.37), channel_id=1, source_target_pairs={{0,8},{4,12},{8,0},{12,4},{16,24},{20,28},{24,16},{28,20},{32,40},... | collective-permute-start | bytes 786440 | tf_op jit(solution)/shard_map/ppermute | solution.py:356
  56.0 1.2 collective-permute-start.22
  57.2 2.2 %collective-permute-done.13.refs_9_ = bf16[1040,128]{1,0:T(8,128)(2,1)} collective-permute-done((bf16[1040,128]{1,0:T(8,128)(2,1)S(1)}, bf16[1040,128]{1,0:T(8,128)(2,1)}, u32[]{:S(2)}, u32[]{:S(2)}) %collective-permute-start.13) | collective-permute-done | bytes 266272 | tf_op jit(solution)/shard_map/ppermute | solution.py:340
  59.4 2.7 %collective-permute-start.15 = (bf16[1040,128]{1,0:T(8,128)(2,1)}, bf16[1040,128]{1,0:T(8,128)(2,1)}, u32[]{:S(2)}, u32[]{:S(2)}) collective-permute-start(bf16[1040,128]{1,0:T(8,128)(2,1)} %collective-permute-done.7.refs_7_), channel_id=1, source_target_pairs={{0,224},{16,240},{32,0},{48,16},{64,32},{80,48},{96,64},{112,80},{... | collective-permute-start | bytes 798728 | tf_op jit(solution)/shard_map/ppermute | solution.py:340
  62.0 0.1 stack.41
  62.1 0.0 copy-start.1
  62.2 0.9 copy-done.1
  63.1 2.0 %stage.1.given = bf16[16640,128]{1,0:T(8,128)(2,1)S(1)} custom-call(s32[3]{0:T(128)S(1)} %copy-done.10, bf16[1040,128]{1,0:T(8,128)(2,1)S(1)} %copy-done.1, bf16[1040,128]{1,0:T(8,128)(2,1)S(1)} %collective-permute-done.1.refs_1_, bf16[1040,128]{1,0:T(8,128)(2,1)S(1)} %collective-permute-done.2.refs_2_, ...), custom_call_target="tpu_custom_call" | custom-call | tf_op jit(solution)/shard_map/stage/pallas_call | solution.py:291
  65.1 2.5 %collective-permute-done.14.refs_0_ = bf16[1040,128]{1,0:T(8,128)(2,1)} collective-permute-done((bf16[1040,128]{1,0:T(8,128)(2,1)S(1)}, bf16[1040,128]{1,0:T(8,128)(2,1)}, u32[]{:S(2)}, u32[]{:S(2)}) %collective-permute-start.14) | collective-permute-done | bytes 266272 | tf_op jit(solution)/shard_map/ppermute | solution.py:340
  67.7 7.9 %attend.3 = (bf16[2,512,128]{2,1,0:T(8,128)(2,1)S(1)}, bf16[2,512,128]{2,1,0:T(8,128)(2,1)S(1)}, bf16[2,512,128]{2,1,0:T(8,128)(2,1)S(1)}, bf16[2,512,128]{2,1,0...) custom-call(s32[3]{0:T(128)S(1)} %copy-done.10, ...), custom_call_target="tpu_custom_call", output_to_operand_aliasing={{5}: (3, {})} | custom-call | tf_op jit(solution)/shard_map/attend/pallas_call | solution.py:305
  75.7 5.4 %attend.4 = (bf16[2,384,128]{2,1,0:T(8,128)(2,1)S(1)}, bf16[2,384,128]{2,1,0:T(8,128)(2,1)S(1)}, bf16[2,384,128]{2,1,0:T(8,128)(2,1)S(1)}, bf16[2,384,128]{2,1,0:T(8,128)(2,1)S(1)}, f32[6,128]{1,0:T(8,128)S(1)}) custom-call(s32[3]{0:T(128)S(1)} %copy-done.10, s32[256]{0:T(256)S(1)} %get-tuple-element.59.picks, s32[256]{0:T(256)S(1)} %get-tuple-element.58.owns, ...), custom_call_target="tpu_custom_call" | custom-call | tf_op jit(solution)/shard_map/attend/pallas_call | solution.py:305
  81.0 3.0 %collective-permute-start.28 = (bf16[2,384,128]{2,1,0:T(8,128)(2,1)S(1)}, bf16[2,384,128]{2,1,0:T(8,128)(2,1)S(1)}, u32[]{:S(2)}, u32[]{:S(2)}) collective-permute-start(bf16[2,384,128]{2,1,0:T(8,128)(2,1)S(1)} %get-tuple-element.47), channel_id=1, source_target_pairs={{4,0},{8,4},{12,8},{0,12},{20,16},{24,20},{28,24},{16,28},{36,32},... | collective-permute-start | bytes 589832 | tf_op jit(solution)/shard_map/ppermute | solution.py:356
  84.0 0.3 collective-permute-start.29
  84.4 2.3 %collective-permute-start.23 = (f32[8,128]{1,0:T(8,128)S(1)}, f32[8,128]{1,0:T(8,128)S(1)}, u32[]{:S(2)}, u32[]{:S(2)}) collective-permute-start(f32[8,128]{1,0:T(8,128)S(1)} %get-tuple-element.41), channel_id=1, source_target_pairs={{0,16},{16,0},{32,48},{48,32},{64,80},{80,64},{96,112},{112,96},{1... | collective-permute-start | bytes 12296 | tf_op jit(solution)/shard_map/ppermute | solution.py:340
  86.7 2.7 %attend.5 = (bf16[2,128,128]{2,1,0:T(8,128)(2,1)S(1)}, bf16[2,128,128]{2,1,0:T(8,128)(2,1)S(1)}, bf16[2,128,128]{2,1,0:T(8,128)(2,1)S(1)}, bf16[2,128,128]{2,1,0:T(8,128)(2,1)S(1)}, f32[2,128]{1,0:T(2,128)S(1)}) custom-call(s32[3]{0:T(128)S(1)} %copy-done.10, s32[256]{0:T(256)S(1)} %get-tuple-element.59.picks, s32[256]{0:T(256)S(1)} %get-tuple-element.58.owns, ...), custom_call_target="tpu_custom_call" | custom-call | tf_op jit(solution)/shard_map/attend/pallas_call | solution.py:305
  89.4 0.9 collective-permute-start.31
  90.4 1.9 %collective-permute-start.32 = (bf16[2,128,128]{2,1,0:T(8,128)(2,1)S(1)}, bf16[2,128,128]{2,1,0:T(8,128)(2,1)S(1)}, u32[]{:S(2)}, u32[]{:S(2)}) collective-permute-start(bf16[2,128,128]{2,1,0:T(8,128)(2,1)S(1)} %get-tuple-element.52), channel_id=1, source_target_pairs={{8,0},{12,4},{0,8},{4,12},{24,16},{28,20},{16,24},{20,28},{40,32},... | collective-permute-start | bytes 196616 | tf_op jit(solution)/shard_map/ppermute | solution.py:356
  92.2 0.8 collective-permute-start.33
  93.0 0.6 collective-permute-done.31.refs_9_
  93.6 2.6 %collective-permute-start.24 = (bf16[2,512,128]{2,1,0:T(8,128)(2,1)S(1)}, bf16[2,512,128]{2,1,0:T(8,128)(2,1)S(1)}, u32[]{:S(2)}, u32[]{:S(2)}) collective-permute-start(bf16[2,512,128]{2,1,0:T(8,128)(2,1)S(1)} %get-tuple-element.42), channel_id=1, source_target_pairs={{16,0},{20,4},{24,8},{28,12},{0,16},{4,20},{8,24},{12,28},{48,32},... | collective-permute-start | bytes 786440 | tf_op jit(solution)/shard_map/ppermute | solution.py:356
  96.2 3.3 %collective-permute-start.25 = (bf16[2,512,128]{2,1,0:T(8,128)(2,1)S(1)}, bf16[2,512,128]{2,1,0:T(8,128)(2,1)S(1)}, u32[]{:S(2)}, u32[]{:S(2)}) collective-permute-start(bf16[2,512,128]{2,1,0:T(8,128)(2,1)S(1)} %get-tuple-element.43), channel_id=1, source_target_pairs={{20,0},{24,4},{28,8},{16,12},{4,16},{8,20},{12,24},{0,28},{52,32},... | collective-permute-start | bytes 786440 | tf_op jit(solution)/shard_map/ppermute | solution.py:356
  99.5 1.1 collective-permute-start.27
  100.5 1.9 %collective-permute-start.30 = (bf16[2,384,128]{2,1,0:T(8,128)(2,1)S(1)}, bf16[2,384,128]{2,1,0:T(8,128)(2,1)S(1)}, u32[]{:S(2)}, u32[]{:S(2)}) collective-permute-start(bf16[2,384,128]{2,1,0:T(8,128)(2,1)S(1)} %get-tuple-element.49), channel_id=1, source_target_pairs={{12,0},{0,4},{4,8},{8,12},{28,16},{16,20},{20,24},{24,28},{44,32},... | collective-permute-start | bytes 589832 | tf_op jit(solution)/shard_map/ppermute | solution.py:356
  102.4 0.6 copy.10
  103.0 16.1 %collective-permute-done.30.refs_7_ = bf16[2,384,128]{2,1,0:T(8,128)(2,1)S(1)} collective-permute-done((bf16[2,384,128]{2,1,0:T(8,128)(2,1)S(1)}, bf16[2,384,128]{2,1,0:T(8,128)(2,1)S(1)}, u32[]{:S(2)}, u32[]{:S(2)}) %collective-permute-start.30) | collective-permute-done | bytes 196640 | tf_op jit(solution)/shard_map/ppermute | solution.py:356
  119.1 2.2 %join_outputs.1 = bf16[8192,128]{1,0:T(8,128)(2,1)} custom-call(s32[3]{0:T(128)S(1)} %copy-done.10, bf16[2,512,128]{2,1,0:T(8,128)(2,1)S(1)} %collective-permute-done.24.refs_0_, bf16[2,512,128]{2,1,0:T(8,128)(2,1)S(1)} %collective-permute-done.25.refs_1_, bf16[2,512,128]{2,1,0:T(8,128)(2,1)S(1)} %collective-permute-done.26.refs_2_, ...), custom_call_target="tpu_custom_call" | custom-call | tf_op jit(solution)/shard_map/join_outputs/pallas_call | solution.py:328
  (45 shorter events, 0.1 us)
Async XLA Ops:
  1.2 60.9 %copy-start.10 = (s32[3]{0:T(128)S(1)}, s32[3]{0:T(128)}, u32[]{:S(2)}) copy-start(s32[3]{0:T(128)} %pad_add_fusion.1.place) | copy-start | bytes 40
  5.8 12.5 %collective-permute-start.16 = (bf16[2,512,128]{2,1,0:T(8,128)(2,1)}, bf16[2,512,128]{2,1,0:T(8,128)(2,1)S(1)}, u32[]{:S(2)}, u32[]{:S(2)}) collective-permute-start(bf16[2,512,128]{2,1,0:T(8,128)(2,1)} %get-tuple-element.30), channel_id=1, source_target_pairs={{0,16},{4,20},{8,24},{12,28},{16,0},{20,4},{24,8},{28,12},{32,48},... | collective-permute-start | bytes 786440 | tf_op jit(solution)/shard_map/ppermute | solution.py:356
  9.1 12.9 %collective-permute-start.17 = (bf16[2,512,128]{2,1,0:T(8,128)(2,1)}, bf16[2,512,128]{2,1,0:T(8,128)(2,1)S(1)}, u32[]{:S(2)}, u32[]{:S(2)}) collective-permute-start(bf16[2,512,128]{2,1,0:T(8,128)(2,1)} %get-tuple-element.31), channel_id=1, source_target_pairs={{0,20},{4,24},{8,28},{12,16},{16,4},{20,8},{24,12},{28,0},{32,52},... | collective-permute-start | bytes 786440 | tf_op jit(solution)/shard_map/ppermute | solution.py:356
  9.9 8.4 %collective-permute-start = (s32[8,16]{1,0:T(8,128)S(1)}, s32[8,16]{1,0:T(8,128)S(1)}, u32[]{:S(2)}, u32[]{:S(2)}) collective-permute-start(s32[8,16]{1,0:T(8,128)S(1)} %bitcast.24), channel_id=1, source_target_pairs={{0,16},{16,0},{32,48},{48,32},{64,80},{80,64},{96,112},{112,96},{1... | collective-permute-start | bytes 1544 | tf_op jit(solution)/shard_map/ppermute | solution.py:340
  13.0 12.4 %collective-permute-start.8 = (bf16[1040,128]{1,0:T(8,128)(2,1)}, bf16[1040,128]{1,0:T(8,128)(2,1)S(1)}, u32[]{:S(2)}, u32[]{:S(2)}) collective-permute-start(bf16[1040,128]{1,0:T(8,128)(2,1)} %get-tuple-element.28.refs_0_), channel_id=1, source_target_pairs={{0,32},{16,48},{32,64},{48,80},{64,96},{80,112},{96,128},{112,144}... | collective-permute-start | bytes 798728 | tf_op jit(solution)/shard_map/ppermute | solution.py:340
  14.4 11.0 %collective-permute-start.2 = (bf16[1040,128]{1,0:T(8,128)(2,1)}, bf16[1040,128]{1,0:T(8,128)(2,1)S(1)}, u32[]{:S(2)}, u32[]{:S(2)}) collective-permute-start(bf16[1040,128]{1,0:T(8,128)(2,1)} %get-tuple-element.28.refs_0_), channel_id=1, source_target_pairs={{0,224},{16,240},{32,0},{48,16},{64,32},{80,48},{96,64},{112,80},{... | collective-permute-start | bytes 798728 | tf_op jit(solution)/shard_map/ppermute | solution.py:340
  18.3 13.1 %collective-permute-start.11 = (bf16[1040,128]{1,0:T(8,128)(2,1)}, bf16[1040,128]{1,0:T(8,128)(2,1)S(1)}, u32[]{:S(2)}, u32[]{:S(2)}) collective-permute-start(bf16[1040,128]{1,0:T(8,128)(2,1)} %get-tuple-element.29), channel_id=1, source_target_pairs={{0,48},{16,32},{32,80},{48,64},{64,112},{80,96},{96,144},{112,128}... | collective-permute-start | bytes 798728 | tf_op jit(solution)/shard_map/ppermute | solution.py:340
  18.3 0.7 copy-start.2
  19.1 12.4 %collective-permute-start.3 = (bf16[1040,128]{1,0:T(8,128)(2,1)}, bf16[1040,128]{1,0:T(8,128)(2,1)S(1)}, u32[]{:S(2)}, u32[]{:S(2)}) collective-permute-start(bf16[1040,128]{1,0:T(8,128)(2,1)} %get-tuple-element.29), channel_id=1, source_target_pairs={{0,240},{16,224},{32,16},{48,0},{64,48},{80,32},{96,80},{112,64},{... | collective-permute-start | bytes 798728 | tf_op jit(solution)/shard_map/ppermute | solution.py:340
  22.0 0.7 copy-start.4
  22.7 11.4 %collective-permute-start.18 = (bf16[2,512,128]{2,1,0:T(8,128)(2,1)}, bf16[2,512,128]{2,1,0:T(8,128)(2,1)S(1)}, u32[]{:S(2)}, u32[]{:S(2)}) collective-permute-start(bf16[2,512,128]{2,1,0:T(8,128)(2,1)} %get-tuple-element.32), channel_id=1, source_target_pairs={{0,24},{4,28},{8,16},{12,20},{16,8},{20,12},{24,0},{28,4},{32,56},... | collective-permute-start | bytes 786440 | tf_op jit(solution)/shard_map/ppermute | solution.py:356
  25.4 19.1 %collective-permute-start.9 = (bf16[1040,128]{1,0:T(8,128)(2,1)S(1)}, bf16[1040,128]{1,0:T(8,128)(2,1)S(1)}, u32[]{:S(2)}, u32[]{:S(2)}) collective-permute-start(bf16[1040,128]{1,0:T(8,128)(2,1)S(1)} %collective-permute-done.8.refs_12_), channel_id=1, source_target_pairs={{0,32},{16,48},{32,64},{48,80},{64,96},{80,112},{96,128},{112,144}... | collective-permute-start | bytes 798728 | tf_op jit(solution)/shard_map/ppermute | solution.py:340
  25.4 19.1 %collective-permute-start.4 = (bf16[1040,128]{1,0:T(8,128)(2,1)S(1)}, bf16[1040,128]{1,0:T(8,128)(2,1)S(1)}, u32[]{:S(2)}, u32[]{:S(2)}) collective-permute-start(bf16[1040,128]{1,0:T(8,128)(2,1)S(1)} %collective-permute-done.2.refs_2_), channel_id=1, source_target_pairs={{0,224},{16,240},{32,0},{48,16},{64,32},{80,48},{96,64},{112,80},{... | collective-permute-start | bytes 798728 | tf_op jit(solution)/shard_map/ppermute | solution.py:340
  31.5 15.7 %collective-permute-start.12 = (bf16[1040,128]{1,0:T(8,128)(2,1)S(1)}, bf16[1040,128]{1,0:T(8,128)(2,1)S(1)}, u32[]{:S(2)}, u32[]{:S(2)}) collective-permute-start(bf16[1040,128]{1,0:T(8,128)(2,1)S(1)} %collective-permute-done.11.refs_13_), channel_id=1, source_target_pairs={{0,32},{16,48},{32,64},{48,80},{64,96},{80,112},{96,128},{112,144}... | collective-permute-start | bytes 798728 | tf_op jit(solution)/shard_map/ppermute | solution.py:340
  31.5 15.7 %collective-permute-start.5 = (bf16[1040,128]{1,0:T(8,128)(2,1)S(1)}, bf16[1040,128]{1,0:T(8,128)(2,1)S(1)}, u32[]{:S(2)}, u32[]{:S(2)}) collective-permute-start(bf16[1040,128]{1,0:T(8,128)(2,1)S(1)} %collective-permute-done.3.refs_3_), channel_id=1, source_target_pairs={{0,224},{16,240},{32,0},{48,16},{64,32},{80,48},{96,64},{112,80},{... | collective-permute-start | bytes 798728 | tf_op jit(solution)/shard_map/ppermute | solution.py:340
  34.2 0.7 copy-start.6
  34.8 8.6 %collective-permute-start.19 = (bf16[2,512,128]{2,1,0:T(8,128)(2,1)}, bf16[2,512,128]{2,1,0:T(8,128)(2,1)S(1)}, u32[]{:S(2)}, u32[]{:S(2)}) collective-permute-start(bf16[2,512,128]{2,1,0:T(8,128)(2,1)} %get-tuple-element.33), channel_id=1, source_target_pairs={{0,28},{4,16},{8,20},{12,24},{16,12},{20,0},{24,4},{28,8},{32,60},... | collective-permute-start | bytes 786440 | tf_op jit(solution)/shard_map/ppermute | solution.py:356
  43.4 0.7 copy-start.8
  44.1 6.0 %collective-permute-start.1 = (bf16[1040,128]{1,0:T(8,128)(2,1)}, bf16[1040,128]{1,0:T(8,128)(2,1)S(1)}, u32[]{:S(2)}, u32[]{:S(2)}) collective-permute-start(bf16[1040,128]{1,0:T(8,128)(2,1)} %get-tuple-element.29), channel_id=1, source_target_pairs={{0,16},{16,0},{32,48},{48,32},{64,80},{80,64},{96,112},{112,96},{1... | collective-permute-start | bytes 798728 | tf_op jit(solution)/shard_map/ppermute | solution.py:340
  44.5 9.0 %collective-permute-start.10 = (bf16[1040,128]{1,0:T(8,128)(2,1)S(1)}, bf16[1040,128]{1,0:T(8,128)(2,1)S(1)}, u32[]{:S(2)}, u32[]{:S(2)}) collective-permute-start(bf16[1040,128]{1,0:T(8,128)(2,1)S(1)} %collective-permute-done.9.refs_10_), channel_id=1, source_target_pairs={{0,32},{16,48},{32,64},{48,80},{64,96},{80,112},{96,128},{112,144}... | collective-permute-start | bytes 798728 | tf_op jit(solution)/shard_map/ppermute | solution.py:340
  44.5 11.5 %collective-permute-start.6 = (bf16[1040,128]{1,0:T(8,128)(2,1)S(1)}, bf16[1040,128]{1,0:T(8,128)(2,1)}, u32[]{:S(2)}, u32[]{:S(2)}) collective-permute-start(bf16[1040,128]{1,0:T(8,128)(2,1)S(1)} %collective-permute-done.4.refs_4_), channel_id=1, source_target_pairs={{0,224},{16,240},{32,0},{48,16},{64,32},{80,48},{96,64},{112,80},{... | collective-permute-start | bytes 798728 | tf_op jit(solution)/shard_map/ppermute | solution.py:340
  47.2 12.2 %collective-permute-start.13 = (bf16[1040,128]{1,0:T(8,128)(2,1)S(1)}, bf16[1040,128]{1,0:T(8,128)(2,1)}, u32[]{:S(2)}, u32[]{:S(2)}) collective-permute-start(bf16[1040,128]{1,0:T(8,128)(2,1)S(1)} %collective-permute-done.12.refs_11_), channel_id=1, source_target_pairs={{0,32},{16,48},{32,64},{48,80},{64,96},{80,112},{96,128},{112,144}... | collective-permute-start | bytes 798728 | tf_op jit(solution)/shard_map/ppermute | solution.py:340
  47.2 12.2 %collective-permute-start.7 = (bf16[1040,128]{1,0:T(8,128)(2,1)S(1)}, bf16[1040,128]{1,0:T(8,128)(2,1)}, u32[]{:S(2)}, u32[]{:S(2)}) collective-permute-start(bf16[1040,128]{1,0:T(8,128)(2,1)S(1)} %collective-permute-done.5.refs_5_), channel_id=1, source_target_pairs={{0,224},{16,240},{32,0},{48,16},{64,32},{80,48},{96,64},{112,80},{... | collective-permute-start | bytes 798728 | tf_op jit(solution)/shard_map/ppermute | solution.py:340
  50.1 25.5 %collective-permute-start.20 = (bf16[2,512,128]{2,1,0:T(8,128)(2,1)}, bf16[2,512,128]{2,1,0:T(8,128)(2,1)S(1)}, u32[]{:S(2)}, u32[]{:S(2)}) collective-permute-start(bf16[2,512,128]{2,1,0:T(8,128)(2,1)} %get-tuple-element.36), channel_id=1, source_target_pairs={{0,4},{4,8},{8,12},{12,0},{16,20},{20,24},{24,28},{28,16},{32,36},... | collective-permute-start | bytes 786440 | tf_op jit(solution)/shard_map/ppermute | solution.py:356
  53.5 22.1 %collective-permute-start.21 = (bf16[2,512,128]{2,1,0:T(8,128)(2,1)}, bf16[2,512,128]{2,1,0:T(8,128)(2,1)S(1)}, u32[]{:S(2)}, u32[]{:S(2)}) collective-permute-start(bf16[2,512,128]{2,1,0:T(8,128)(2,1)} %get-tuple-element.37), channel_id=1, source_target_pairs={{0,8},{4,12},{8,0},{12,4},{16,24},{20,28},{24,16},{28,20},{32,40},... | collective-permute-start | bytes 786440 | tf_op jit(solution)/shard_map/ppermute | solution.py:356
  56.0 19.6 %collective-permute-start.22 = (bf16[2,512,128]{2,1,0:T(8,128)(2,1)}, bf16[2,512,128]{2,1,0:T(8,128)(2,1)S(1)}, u32[]{:S(2)}, u32[]{:S(2)}) collective-permute-start(bf16[2,512,128]{2,1,0:T(8,128)(2,1)} %get-tuple-element.38), channel_id=1, source_target_pairs={{0,12},{4,0},{8,4},{12,8},{16,28},{20,16},{24,20},{28,24},{32,44},... | collective-permute-start | bytes 786440 | tf_op jit(solution)/shard_map/ppermute | solution.py:356
  59.4 8.3 %collective-permute-start.14 = (bf16[1040,128]{1,0:T(8,128)(2,1)S(1)}, bf16[1040,128]{1,0:T(8,128)(2,1)}, u32[]{:S(2)}, u32[]{:S(2)}) collective-permute-start(bf16[1040,128]{1,0:T(8,128)(2,1)S(1)} %collective-permute-done.10.refs_8_), channel_id=1, source_target_pairs={{0,32},{16,48},{32,64},{48,80},{64,96},{80,112},{96,128},{112,144}... | collective-permute-start | bytes 798728 | tf_op jit(solution)/shard_map/ppermute | solution.py:340
  59.4 8.3 %collective-permute-start.15 = (bf16[1040,128]{1,0:T(8,128)(2,1)}, bf16[1040,128]{1,0:T(8,128)(2,1)}, u32[]{:S(2)}, u32[]{:S(2)}) collective-permute-start(bf16[1040,128]{1,0:T(8,128)(2,1)} %collective-permute-done.7.refs_7_), channel_id=1, source_target_pairs={{0,224},{16,240},{32,0},{48,16},{64,32},{80,48},{96,64},{112,80},{... | collective-permute-start | bytes 798728 | tf_op jit(solution)/shard_map/ppermute | solution.py:340
  62.1 1.0 copy-start.1
  63.1 4.6 %copy-start.3 = (bf16[2,512,128]{2,1,0:T(8,128)(2,1)S(1)}, bf16[2,512,128]{2,1,0:T(8,128)(2,1)}, u32[]{:S(2)}) copy-start(bf16[2,512,128]{2,1,0:T(8,128)(2,1)} %copy-done.2) | copy-start | bytes 786436
  63.1 4.6 %copy-start.5 = (bf16[2,512,128]{2,1,0:T(8,128)(2,1)S(1)}, bf16[2,512,128]{2,1,0:T(8,128)(2,1)}, u32[]{:S(2)}) copy-start(bf16[2,512,128]{2,1,0:T(8,128)(2,1)} %copy-done.4) | copy-start | bytes 786436
  63.1 4.6 %copy-start.7 = (bf16[2,512,128]{2,1,0:T(8,128)(2,1)S(1)}, bf16[2,512,128]{2,1,0:T(8,128)(2,1)}, u32[]{:S(2)}) copy-start(bf16[2,512,128]{2,1,0:T(8,128)(2,1)} %copy-done.6) | copy-start | bytes 786436
  63.1 4.6 %copy-start.9 = (bf16[2,512,128]{2,1,0:T(8,128)(2,1)S(1)}, bf16[2,512,128]{2,1,0:T(8,128)(2,1)}, u32[]{:S(2)}) copy-start(bf16[2,512,128]{2,1,0:T(8,128)(2,1)} %copy-done.8) | copy-start | bytes 786436
  65.1 10.5 %copy-start = (bf16[2,512,128]{2,1,0:T(8,128)(2,1)S(1)}, bf16[2,512,128]{2,1,0:T(8,128)(2,1)}, u32[]{:S(2)}) copy-start(bf16[2,512,128]{2,1,0:T(8,128)(2,1)} %get-tuple-element.35.refs_0_) | copy-start | bytes 786436
  81.0 18.4 %collective-permute-start.28 = (bf16[2,384,128]{2,1,0:T(8,128)(2,1)S(1)}, bf16[2,384,128]{2,1,0:T(8,128)(2,1)S(1)}, u32[]{:S(2)}, u32[]{:S(2)}) collective-permute-start(bf16[2,384,128]{2,1,0:T(8,128)(2,1)S(1)} %get-tuple-element.47), channel_id=1, source_target_pairs={{4,0},{8,4},{12,8},{0,12},{20,16},{24,20},{28,24},{16,28},{36,32},... | collective-permute-start | bytes 589832 | tf_op jit(solution)/shard_map/ppermute | solution.py:356
  84.0 16.5 %collective-permute-start.29 = (bf16[2,384,128]{2,1,0:T(8,128)(2,1)S(1)}, bf16[2,384,128]{2,1,0:T(8,128)(2,1)S(1)}, u32[]{:S(2)}, u32[]{:S(2)}) collective-permute-start(bf16[2,384,128]{2,1,0:T(8,128)(2,1)S(1)} %get-tuple-element.48), channel_id=1, source_target_pairs={{8,0},{12,4},{0,8},{4,12},{24,16},{28,20},{16,24},{20,28},{40,32},... | collective-permute-start | bytes 589832 | tf_op jit(solution)/shard_map/ppermute | solution.py:356
  84.4 7.9 %collective-permute-start.23 = (f32[8,128]{1,0:T(8,128)S(1)}, f32[8,128]{1,0:T(8,128)S(1)}, u32[]{:S(2)}, u32[]{:S(2)}) collective-permute-start(f32[8,128]{1,0:T(8,128)S(1)} %get-tuple-element.41), channel_id=1, source_target_pairs={{0,16},{16,0},{32,48},{48,32},{64,80},{80,64},{96,112},{112,96},{1... | collective-permute-start | bytes 12296 | tf_op jit(solution)/shard_map/ppermute | solution.py:340
  89.4 4.2 %collective-permute-start.31 = (bf16[2,128,128]{2,1,0:T(8,128)(2,1)S(1)}, bf16[2,128,128]{2,1,0:T(8,128)(2,1)S(1)}, u32[]{:S(2)}, u32[]{:S(2)}) collective-permute-start(bf16[2,128,128]{2,1,0:T(8,128)(2,1)S(1)} %get-tuple-element.51), channel_id=1, source_target_pairs={{4,0},{8,4},{12,8},{0,12},{20,16},{24,20},{28,24},{16,28},{36,32},... | collective-permute-start | bytes 196616 | tf_op jit(solution)/shard_map/ppermute | solution.py:356
  90.4 5.8 %collective-permute-start.32 = (bf16[2,128,128]{2,1,0:T(8,128)(2,1)S(1)}, bf16[2,128,128]{2,1,0:T(8,128)(2,1)S(1)}, u32[]{:S(2)}, u32[]{:S(2)}) collective-permute-start(bf16[2,128,128]{2,1,0:T(8,128)(2,1)S(1)} %get-tuple-element.52), channel_id=1, source_target_pairs={{8,0},{12,4},{0,8},{4,12},{24,16},{28,20},{16,24},{20,28},{40,32},... | collective-permute-start | bytes 196616 | tf_op jit(solution)/shard_map/ppermute | solution.py:356
  92.2 7.2 %collective-permute-start.33 = (bf16[2,128,128]{2,1,0:T(8,128)(2,1)S(1)}, bf16[2,128,128]{2,1,0:T(8,128)(2,1)S(1)}, u32[]{:S(2)}, u32[]{:S(2)}) collective-permute-start(bf16[2,128,128]{2,1,0:T(8,128)(2,1)S(1)} %get-tuple-element.53), channel_id=1, source_target_pairs={{12,0},{0,4},{4,8},{8,12},{28,16},{16,20},{20,24},{24,28},{44,32},... | collective-permute-start | bytes 196616 | tf_op jit(solution)/shard_map/ppermute | solution.py:356
  93.6 25.5 %collective-permute-start.24 = (bf16[2,512,128]{2,1,0:T(8,128)(2,1)S(1)}, bf16[2,512,128]{2,1,0:T(8,128)(2,1)S(1)}, u32[]{:S(2)}, u32[]{:S(2)}) collective-permute-start(bf16[2,512,128]{2,1,0:T(8,128)(2,1)S(1)} %get-tuple-element.42), channel_id=1, source_target_pairs={{16,0},{20,4},{24,8},{28,12},{0,16},{4,20},{8,24},{12,28},{48,32},... | collective-permute-start | bytes 786440 | tf_op jit(solution)/shard_map/ppermute | solution.py:356
  96.2 22.9 %collective-permute-start.25 = (bf16[2,512,128]{2,1,0:T(8,128)(2,1)S(1)}, bf16[2,512,128]{2,1,0:T(8,128)(2,1)S(1)}, u32[]{:S(2)}, u32[]{:S(2)}) collective-permute-start(bf16[2,512,128]{2,1,0:T(8,128)(2,1)S(1)} %get-tuple-element.43), channel_id=1, source_target_pairs={{20,0},{24,4},{28,8},{16,12},{4,16},{8,20},{12,24},{0,28},{52,32},... | collective-permute-start | bytes 786440 | tf_op jit(solution)/shard_map/ppermute | solution.py:356
  99.5 19.7 %collective-permute-start.26 = (bf16[2,512,128]{2,1,0:T(8,128)(2,1)S(1)}, bf16[2,512,128]{2,1,0:T(8,128)(2,1)S(1)}, u32[]{:S(2)}, u32[]{:S(2)}) collective-permute-start(bf16[2,512,128]{2,1,0:T(8,128)(2,1)S(1)} %get-tuple-element.44), channel_id=1, source_target_pairs={{24,0},{28,4},{16,8},{20,12},{8,16},{12,20},{0,24},{4,28},{56,32},... | collective-permute-start | bytes 786440 | tf_op jit(solution)/shard_map/ppermute | solution.py:356
  99.5 19.7 %collective-permute-start.27 = (bf16[2,512,128]{2,1,0:T(8,128)(2,1)S(1)}, bf16[2,512,128]{2,1,0:T(8,128)(2,1)S(1)}, u32[]{:S(2)}, u32[]{:S(2)}) collective-permute-start(bf16[2,512,128]{2,1,0:T(8,128)(2,1)S(1)} %get-tuple-element.45), channel_id=1, source_target_pairs={{28,0},{16,4},{20,8},{24,12},{12,16},{0,20},{4,24},{8,28},{60,32},... | collective-permute-start | bytes 786440 | tf_op jit(solution)/shard_map/ppermute | solution.py:356
  100.5 18.6 %collective-permute-start.30 = (bf16[2,384,128]{2,1,0:T(8,128)(2,1)S(1)}, bf16[2,384,128]{2,1,0:T(8,128)(2,1)S(1)}, u32[]{:S(2)}, u32[]{:S(2)}) collective-permute-start(bf16[2,384,128]{2,1,0:T(8,128)(2,1)S(1)} %get-tuple-element.49), channel_id=1, source_target_pairs={{12,0},{0,4},{4,8},{8,12},{28,16},{16,20},{20,24},{24,28},{44,32},... | collective-permute-start | bytes 589832 | tf_op jit(solution)/shard_map/ppermute | solution.py:356
